TPU v7x, 256 devices: a whole 4x4x8 slice. The times are simulated.
256 devices in a mesh: row: 16 (over z, x_lo), col: 8 (over y, x_hi), depth: 2 (over core).
Axes of the slice: x: 4 (x_hi: 2, x_lo: 2; x = x_hi * 2 + x_lo), y: 4, z: 8, core: 2. Of those that a mesh axis runs over, the one named last changes fastest.
Arguments:
- tokens: bfloat16 [2048, 5376], P('row', 'depth'), may hold values from -6 to 6
- gate_weight: bfloat16 [9216, 5376], P(('col', 'row'), 'depth'), may hold values from -0.078125 to 0.078125
- up_weight: bfloat16 [9216, 5376], P(('col', 'row'), 'depth'), may hold values from -0.078125 to 0.078125
- down_weight: bfloat16 [9216, 5376], P(('col', 'depth'), 'row'), may hold values from -0.09375 to 0.09375
Outputs:
- output: bfloat16 [2048, 5376], P('row', ('col', 'depth'))
All inputs are finite; a program needn't handle non-finite values.
Results may differ from a plain program's by a relative error of at most 0.0049.
Values may be sent and summed in bfloat16 or wider, within the bound.
No kernel may reach another device: no remote copies, remote signals or barrier semaphores. Data moves between devices by JAX's collectives and lax.ppermute only.
A program may use at most 64 MiB of HBM per device.

v0:
```python
import jax
import jax.numpy as jnp


def reference(tokens, gate_weight, up_weight, down_weight):
    gate_part = jnp.dot(tokens, gate_weight.T, preferred_element_type=jnp.float32)
    up_part = jnp.dot(tokens, up_weight.T, preferred_element_type=jnp.float32)
    hidden = (jax.nn.silu(gate_part) * up_part).astype(jnp.bfloat16)
    return jnp.dot(hidden, down_weight, preferred_element_type=jnp.float32).astype(jnp.bfloat16)


def solution(mesh):
    return reference
```

profile of v0, /device:TPU:40, one launch (start us, length us, event | category | flops | bytes accessed | tf_op | source)
XLA Modules:
  0.0 484.3 jit_solution(230915049926508180)
XLA Ops:
  6.5 0.0 copy-start
  6.5 0.0 copy-start.2
  6.5 0.0 all-gather.6.cloned.1.call-start
  6.5 0.7 all-gather.6.cloned.1.call-update
  7.3 0.0 all-reduce.6.cloned.1.call-start
  7.3 240.0 %all-gather.6.cloned.1.call-done = bf16[2048,2688]{1,0:T(8,128)(2,1)} async-done(((bf16[128,2688]{1,0:T(8,128)(2,1)}), bf16[2048,2688]{1,0:T(8,128)(2,1)}) %all-gather.6.cloned.1.call-update) | async-done | bytes 11010064 | tf_op args[0]
  247.3 0.0 copy-start.1
  247.3 8.7 %fusion.1 = f32[2048,72]{0,1:T(8,128)} fusion(bf16[2048,2688]{1,0:T(8,128)(2,1)} %all-gather.6.cloned.1.call-done, bf16[72,2688]{1,0:T(8,128)(2,1)} %param.2), kind=kOutput, calls=%fused_computation.2 | convolution fusion | flops 792723456 | bytes 11986944 | tf_op jit(solution)/dot_general | solution.py:7
  256.0 0.0 copy-done.2
  256.0 0.0 copy-done.1
  256.0 4.4 fusion
  260.5 0.0 all-reduce.6.cloned.1.call-update
  260.5 0.0 all-gather.8.cloned.1.call-start
  260.5 31.0 %all-reduce.6.cloned.1.call-done = (f32[2048,72]{0,1:T(8,128)}, f32[2048,72]{0,1:T(8,128)}) async-done(((f32[2048,72]{0,1:T(8,128)}, f32[2048,72]{0,1:T(8,128)}), (f32[2048,72]{0,1:T(8,128)}, f32[2048,72]{0,1:T(8,128)})) %all-reduce.6.cloned.1.call-update) | async-done | bytes 1179664 | tf_op jit(solution)/dot_general | solution.py:7
  291.5 1.4 multiply_convert_fusion
  292.9 0.7 collective-permute-start
  293.6 0.0 collective-permute-done
  293.6 0.0 copy-start.3
  293.6 0.7 copy-done.3
  294.3 0.0 all-gather.8.cloned.1.call-update
  294.3 0.0 reduce-scatter.4.cloned.1.call-start
  294.4 72.7 %all-gather.8.cloned.1.call-done = bf16[2048,576]{0,1:T(8,128)(2,1)} async-done(((bf16[2048,72]{0,1:T(8,128)(2,1)}), bf16[2048,576]{0,1:T(8,128)(2,1)}) %all-gather.8.cloned.1.call-update) | async-done | bytes 2359312 | tf_op jit(solution)/convert_element_type | solution.py:8
  367.1 0.0 copy-done
  367.1 4.4 fusion.2
  371.5 0.0 reduce-scatter.4.cloned.1.call-update
  371.5 80.8 %reduce-scatter.4.cloned.1.call-done = f32[128,336]{0,1:T(8,128)} async-done(((f32[2048,336]{0,1:T(8,128)}), f32[128,336]{0,1:T(8,128)}) %reduce-scatter.4.cloned.1.call-update) | async-done | bytes 172048
  452.4 5.2 %collective-permute-start.1 = (f32[128,336]{0,1:T(8,128)}, f32[128,336]{0,1:T(8,128)S(1)}, u32[]{:S(2)}, u32[]{:S(2)}) collective-permute-start(f32[128,336]{0,1:T(8,128)} %reduce-scatter.4.cloned.1.call-done), channel_id=8, source_target_pairs={{0,0},{16,1},{32,2},{48,3},{64,4},{80,5},{96,6},{112,7},{128,8},{1... | collective-permute-start | bytes 516104 | tf_op jit(solution)/dot_general | solution.py:9
  457.5 19.5 %collective-permute-done.1 = f32[128,336]{0,1:T(8,128)S(1)} collective-permute-done((f32[128,336]{0,1:T(8,128)}, f32[128,336]{0,1:T(8,128)S(1)}, u32[]{:S(2)}, u32[]{:S(2)}) %collective-permute-start.1) | collective-permute-done | bytes 172064 | tf_op jit(solution)/dot_general | solution.py:9
  477.1 0.6 convert_element_type.9
Async XLA Ops:
  6.5 360.5 %copy-start = (bf16[576,336]{0,1:T(8,128)(2,1)S(1)}, bf16[576,336]{0,1:T(8,128)(2,1)}, u32[]{:S(2)}) copy-start(bf16[576,336]{0,1:T(8,128)(2,1)} %param.3) | copy-start | bytes 1161220
  6.5 249.5 %copy-start.2 = (bf16[72,2688]{1,0:T(8,128)(2,1)S(1)}, bf16[72,2688]{1,0:T(8,128)(2,1)}, u32[]{:S(2)}) copy-start(bf16[72,2688]{1,0:T(8,128)(2,1)} %param.1) | copy-start | bytes 1161220
  6.5 240.8 %all-gather.6.cloned.1.call-start = ((), (), s32[]{:S(2)}) async-start(), calls=%async_computation.1 | async-start | bytes 11698176 | tf_op args[0]
  7.3 284.2 %all-reduce.6.cloned.1.call-start = ((), (), s32[]{:S(2)}) async-start(), calls=%async_computation.4 | async-start | bytes 2359296 | tf_op jit(solution)/dot_general | solution.py:7
  247.3 8.7 %copy-start.1 = (bf16[2048,2688]{1,0:T(8,128)(2,1)S(1)}, bf16[2048,2688]{1,0:T(8,128)(2,1)}, u32[]{:S(2)}) copy-start(bf16[2048,2688]{1,0:T(8,128)(2,1)} %all-gather.6.cloned.1.call-done) | copy-start | bytes 33030148
  260.5 106.6 %all-gather.8.cloned.1.call-start = ((), (), s32[]{:S(2)}) async-start(), calls=%async_computation.2 | async-start | bytes 2654208 | tf_op jit(solution)/convert_element_type | solution.py:8
  292.9 0.7 collective-permute-start
  293.6 0.7 copy-start.3
  294.3 158.0 %reduce-scatter.4.cloned.1.call-start = ((), (), s32[]{:S(2)}) async-start(), calls=%async_computation.3 | async-start | bytes 2924544
  452.4 24.7 %collective-permute-start.1 = (f32[128,336]{0,1:T(8,128)}, f32[128,336]{0,1:T(8,128)S(1)}, u32[]{:S(2)}, u32[]{:S(2)}) collective-permute-start(f32[128,336]{0,1:T(8,128)} %reduce-scatter.4.cloned.1.call-done), channel_id=8, source_target_pairs={{0,0},{16,1},{32,2},{48,3},{64,4},{80,5},{96,6},{112,7},{128,8},{1... | collective-permute-start | bytes 516104 | tf_op jit(solution)/dot_general | solution.py:9
Sparse Core Ops, SparseCore 0:
  9.1 238.1 all-gather.5
  260.6 30.8 all-reduce.5
  294.4 72.5 all-gather.7
  371.7 80.6 reduce-scatter.3
where the time goes:
time: 484 us
  waiting for transfers between devices  445 us (92%)
  matrix products  17.6 us (4%)
  between operations  13.2 us (3%)
  starting transfers between devices  5.97 us (1%)
    unnamed x6, waiting for transfers between devices  322 us
    convert_element_type x2, waiting for transfers between devices, reference(): hidden = (jax.nn.silu(gate_part) * up_part).astype(jnp.bfloat16)  72.7 us
    dot_general x1, waiting for transfers between devices, reference(): up_part = jnp.dot(tokens, up_weight.T, preferred_element_type=jnp.float32)  31 us
    dot_general x1, waiting for transfers between devices, reference(): jnp.dot(hidden, down_weight, preferred_element_type=jnp.float32)  19.5 us
  transfers between devices with their start and end apart: 6, of which 5 were waited for; matrix products, arithmetic and copies ran while one was open for 0% of the time, Pallas kernels for 0%

commit v1 on v0

v1 whole, which is shorter than its diff:
```python
import jax
import jax.numpy as jnp
from jax import lax
from jax.experimental import pallas as pl
from jax.experimental.pallas import tpu as pltpu
from jax.sharding import Mesh, PartitionSpec as P


Z, XL, Y, XH, C = 8, 2, 4, 2, 2
PAD = 384
OFFSETS = (0, -1, -2, -3, 1, 2, 3)


def ring(n, k):
    return [(i, (i + k) % n) for i in range(n)]


def x_ring(k):
    at = [(x % 2) * 2 + x // 2 for x in range(4)]
    return [(at[a], at[b]) for a, b in ring(4, k)]


def px(v, k):
    return lax.ppermute(v, ("xl", "xh"), x_ring(k))


def py(v, k):
    return lax.ppermute(v, "y", ring(Y, k))


def pz(v, k):
    return lax.ppermute(v, "z", ring(Z, k))


def core_swap(v):
    return lax.ppermute(v, "c", ring(C, 1))


def z_ring(block):
    half = block.shape[0] // 2
    ups, downs = [block], [block]
    for _ in range(3):
        ups.append(pz(ups[-1], 1))
        downs.append(pz(downs[-1], -1))
    return ups + downs[1:] + [pz(ups[-1][:half], 1), pz(downs[-1][half:], -1)]


def down_kernel(down_t, out):
    rows = down_t[...].T
    out[...] = jnp.concatenate([rows, jnp.zeros((rows.shape[0], PAD - rows.shape[1]), rows.dtype)], 1)


def place(z, c, off):
    src = lax.rem(z + off + Z, Z)
    return src // 4 ^ c, lax.rem(src, 4)


def first_kernel(*refs):
    blocks, (u4, d4), weights = refs[:7], refs[7:9], refs[9:14]
    keep, send, tok, wts = refs[14:]
    z, xl, c, xh = (lax.axis_index(a) for a in ("z", "xl", "c", "xh"))
    n, units = blocks[0].shape[0], weights[3].shape[1]
    for block, off in zip(blocks, OFFSETS):
        half, at = place(z, c, off)
        tok[pl.ds(pl.multiple_of((half * 4 + at) * n, n), n), :] = block[...]
    half, at = place(z, c, 4)
    for i, part in enumerate((u4, d4)):
        tok[pl.ds(pl.multiple_of((half * 4 + at) * n + i * n // 2, n // 2), n // 2), :] = part[...]
    w, w_m1, w_p1, g2, u2 = weights
    for (gate, up), off in zip(((w.at[0], w.at[1]), (w_m1.at[0], w_m1.at[1]), (w_p1.at[0], w_p1.at[1]), (g2.at[0], u2.at[0])),
                               (0, -1, 1, 2)):
        src = lax.rem(xh * 2 + xl + off + 4, 4)
        dst = (src // 2 ^ xh) * 2 + lax.rem(src, 2)
        wts[dst, :units, :] = gate[...]
        wts[dst, units:, :] = up[...]
    flat = wts[...].reshape(8 * units, wts.shape[2])
    for out, lo in ((send, 4 * n), (keep, 0)):
        out[...] = lax.dot_general(flat, tok[lo:lo + 4 * n, :], (((1,), (1,)), ((), ())),
                                   preferred_element_type=jnp.float32)


def second_kernel(*refs):
    blocks, (u4, d4), near, far = refs[:7], refs[7:9], refs[9], refs[10]
    outs, hid, val = refs[11:15], refs[15], refs[16]
    z, xl, c, y = (lax.axis_index(a) for a in ("z", "xl", "c", "y"))
    n = u4.shape[0]
    rows = 4 * n

    def put(off, part, value):
        half, at = place(z, c, off)
        hid[pl.ds(pl.multiple_of((half * 2 + part) * rows + at * n, 16), n), :] = value

    for block, off in zip(blocks, OFFSETS):
        put(off, 0, block[:n, :])
        put(off, 1, block[n:, :])
    put(4, 0, u4[...])
    put(4, 1, d4[...])
    t = outs[0].shape[0]
    for d in range(2):
        total = None
        for half, down in enumerate((near, far)):
            for h in range(2):
                slot = jnp.where(xl == d, h, 2 + (1 - xl ^ h))
                lo = (half * 2 + h) * rows
                term = lax.dot_general(hid[lo:lo + rows, :], down[slot], (((0,), (0,)), ((), ())),
                                       preferred_element_type=jnp.float32)
                total = term if total is None else total + term
        val[...] = total
        for k, out in enumerate(outs):
            at = lax.rem(y + k, 4) * t
            out[:, d * PAD:(d + 1) * PAD] = val[pl.ds(pl.multiple_of(at, t), t), :].astype(out.dtype)


VMEM = pl.BlockSpec(memory_space=pltpu.VMEM)


def solution(mesh):
    grid = Mesh(mesh.devices.reshape(Z, XL, Y, XH, C), ("z", "xl", "y", "xh", "c"))
    final_axes = ("z", "y", "xh", "c")
    final_perms = ([], [])
    for z in range(Z):
        for y in range(Y):
            for xh in range(XH):
                for c in range(C):
                    src = ((z * Y + y) * XH + xh) * C + c
                    dst = (((4 * c + y) * Y + z // 2) * XH + z % 2) * C
                    final_perms[0].append((src, dst + xh))
                    final_perms[1].append((src, dst + 1 - xh))

    def body(tokens, gate, up, down):
        xh, c = lax.axis_index("xh"), lax.axis_index("c")
        units, k, n = gate.shape[0], tokens.shape[1], tokens.shape[0] // 2
        bf16 = jnp.bfloat16

        toks = z_ring(lax.dynamic_slice_in_dim(tokens, xh * n, n, 0))

        w = jnp.stack([gate, up])
        w_m1, w_p1 = px(w, 1), px(w, -1)
        weights = w, w_m1, w_p1, px(w_m1[:1], 1), px(w_p1[1:], -1)

        dblk = pl.pallas_call(
            down_kernel,
            out_shape=jax.ShapeDtypeStruct((down.shape[0], PAD), bf16),
            in_specs=[VMEM],
            out_specs=VMEM,
            compiler_params=pltpu.CompilerParams(vmem_limit_bytes=4 << 20),
            cost_estimate=pl.CostEstimate(flops=10**8, bytes_accessed=1 << 20, transcendentals=0),
            name="down",
        )(down.T)
        near = jnp.stack([dblk, px(dblk, 2), px(dblk, 1), px(dblk, -1)])
        far = core_swap(near)

        m, t = 8 * units, Z * n
        half = jax.ShapeDtypeStruct((m, t // 2), jnp.float32)
        keep, send = pl.pallas_call(
            first_kernel,
            out_shape=(half, half),
            in_specs=[VMEM] * 14,
            out_specs=(VMEM, VMEM),
            scratch_shapes=[pltpu.VMEM((t, k), bf16), pltpu.VMEM((4, 2 * units, k), bf16)],
            compiler_params=pltpu.CompilerParams(vmem_limit_bytes=12 << 20),
            cost_estimate=pl.CostEstimate(flops=2 * m * t * k, bytes_accessed=2 * k * (m + t), transcendentals=0),
            name="first",
        )(*toks, *weights)
        whole = (keep + core_swap(send)).reshape(4, 2, units, t // 2)
        g, u = whole[:, 0], whole[:, 1]
        hidden = (jax.nn.silu(g) * u).astype(bf16).reshape(4 * units, t // 2)

        hids = z_ring(hidden)
        piece = jax.ShapeDtypeStruct((n, 2 * PAD), bf16)
        shares = pl.pallas_call(
            second_kernel,
            out_shape=(piece,) * 4,
            in_specs=[VMEM] * 11,
            out_specs=(VMEM,) * 4,
            scratch_shapes=[pltpu.VMEM((Z * 4 * units, t // 2), bf16), pltpu.VMEM((t // 2, PAD), jnp.float32)],
            compiler_params=pltpu.CompilerParams(vmem_limit_bytes=10 << 20),
            cost_estimate=pl.CostEstimate(flops=2 * Z * 4 * units * t * PAD, bytes_accessed=6 << 20, transcendentals=0),
            name="second",
        )(*hids, near, far)

        parts = shares[0], py(shares[1], 1), py(shares[2], 2), py(shares[3], -1)
        total = sum(p.astype(jnp.float32) for p in parts).astype(bf16)
        mine, other = (lax.dynamic_slice_in_dim(total, d * PAD, PAD, 1) for d in (xh, 1 - xh))
        got_a, got_b = lax.ppermute(mine, final_axes, final_perms[0]), lax.ppermute(other, final_axes, final_perms[1])
        rows = jnp.where(c == 0, jnp.concatenate([got_a, got_b], 0), jnp.concatenate([got_b, got_a], 0))
        return rows[:, :down.shape[1]]

    row, col = ("z", "xl"), ("y", "xh")
    return jax.shard_map(
        body,
        mesh=grid,
        in_specs=(P(row, "c"), P(col + row, "c"), P(col + row, "c"), P(col + ("c",), row)),
        out_specs=P(row, col + ("c",)),
        check_vma=False,
    )
```

time: 484 us -> 119 us (0.25)
  the two profiles are of different devices: /device:TPU:40 before, /device:TPU:56 now
where the time goes in v1:
time: 119 us
  waiting for transfers between devices  60.2 us (51%)
  starting transfers between devices  50.1 us (42%)
  Pallas kernels  4.38 us (4%)
  local copies, waits for them, and re-layouts  2.03 us (2%)
  other arithmetic  1.71 us (1%)
    ppermute x16, waiting for transfers between devices, pz(): return lax.ppermute(v, 'z', ring(Z, k))  24.8 us
    ppermute x16, starting transfers between devices, pz(): return lax.ppermute(v, 'z', ring(Z, k))  24.3 us
    ppermute x7, waiting for transfers between devices, px(): return lax.ppermute(v, ('xl', 'xh'), x_ring(k))  15.7 us
    ppermute x7, starting transfers between devices, px(): return lax.ppermute(v, ('xl', 'xh'), x_ring(k))  13 us
    ppermute x1, waiting for transfers between devices, body(): lax.ppermute(other, final_axes, final_perms[1])  10.1 us
    ppermute x1, starting transfers between devices, body(): lax.ppermute(mine, final_axes, final_perms[0])  9.49 us
    ppermute x3, waiting for transfers between devices, py(): return lax.ppermute(v, 'y', ring(Y, k))  5.82 us
    ppermute x3, starting transfers between devices, py(): return lax.ppermute(v, 'y', ring(Y, k))  2.89 us
  transfers between devices with their start and end apart: 30, of which 21 were waited for; matrix products, arithmetic and copies ran while one was open for 1% of the time, Pallas kernels for 2%

profile of v1, /device:TPU:56, one launch (start us, length us, event | category | flops | bytes accessed | tf_op | source)
XLA Modules:
  0.0 118.5 jit_solution(12467603403400117071)
XLA Ops:
  0.0 1.1 copy-done
  1.1 2.0 %collective-permute-start = (bf16[64,2688]{1,0:T(8,128)(2,1)S(1)}, bf16[64,2688]{1,0:T(8,128)(2,1)S(1)}, u32[]{:S(2)}, u32[]{:S(2)}) collective-permute-start(bf16[64,2688]{1,0:T(8,128)(2,1)S(1)} %constant_dynamic-slice_fusion.2.refs_0_), channel_id=1, source_target_pairs={{0,32},{32,64},{64,96},{96,128},{128,160},{160,192},{192,224},{224... | collective-permute-start | bytes 1032200 | tf_op jit(solution)/shard_map/ppermute | solution.py:32
  3.2 1.2 %pad_maximum_fusion.1.refs_9_ = bf16[2,72,2688]{2,1,0:T(8,128)(2,1)S(1)} fusion(bf16[1,72,2688]{2,1,0:T(8,128)(2,1)} %bitcast.35, bf16[1,72,2688]{2,1,0:T(8,128)(2,1)} %bitcast.36), kind=kLoop, calls=%fused_computation.1 | loop fusion | flops 387072 | bytes 1548288 | tf_op jit(solution)/shard_map/stack | solution.py:137
  4.4 1.6 %collective-permute-start.8 = (bf16[2,72,2688]{2,1,0:T(8,128)(2,1)S(1)}, bf16[2,72,2688]{2,1,0:T(8,128)(2,1)S(1)}, u32[]{:S(2)}, u32[]{:S(2)}) collective-permute-start(bf16[2,72,2688]{2,1,0:T(8,128)(2,1)S(1)} %pad_maximum_fusion.1.refs_9_), channel_id=1, source_target_pairs={{0,16},{16,2},{2,18},{18,0},{1,17},{17,3},{3,19},{19,1},{4,20},{20... | collective-permute-start | bytes 2322440 | tf_op jit(solution)/shard_map/ppermute | solution.py:24
  6.0 1.7 %collective-permute-start.9 = (bf16[2,72,2688]{2,1,0:T(8,128)(2,1)S(1)}, bf16[2,72,2688]{2,1,0:T(8,128)(2,1)S(1)}, u32[]{:S(2)}, u32[]{:S(2)}) collective-permute-start(bf16[2,72,2688]{2,1,0:T(8,128)(2,1)S(1)} %pad_maximum_fusion.1.refs_9_), channel_id=1, source_target_pairs={{0,18},{16,0},{2,16},{18,2},{1,19},{17,1},{3,17},{19,3},{4,22},{20... | collective-permute-start | bytes 2322440 | tf_op jit(solution)/shard_map/ppermute | solution.py:24
  7.7 3.3 %collective-permute-done.refs_1_ = bf16[64,2688]{1,0:T(8,128)(2,1)S(1)} collective-permute-done((bf16[64,2688]{1,0:T(8,128)(2,1)S(1)}, bf16[64,2688]{1,0:T(8,128)(2,1)S(1)}, u32[]{:S(2)}, u32[]{:S(2)}) %collective-permute-start) | collective-permute-done | bytes 344096 | tf_op jit(solution)/shard_map/ppermute | solution.py:32
  11.0 1.9 %collective-permute-start.1 = (bf16[64,2688]{1,0:T(8,128)(2,1)S(1)}, bf16[64,2688]{1,0:T(8,128)(2,1)S(1)}, u32[]{:S(2)}, u32[]{:S(2)}) collective-permute-start(bf16[64,2688]{1,0:T(8,128)(2,1)S(1)} %collective-permute-done.refs_1_), channel_id=1, source_target_pairs={{0,32},{32,64},{64,96},{96,128},{128,160},{160,192},{192,224},{224... | collective-permute-start | bytes 1032200 | tf_op jit(solution)/shard_map/ppermute | solution.py:32
  12.9 2.3 %collective-permute-start.4 = (bf16[64,2688]{1,0:T(8,128)(2,1)S(1)}, bf16[64,2688]{1,0:T(8,128)(2,1)S(1)}, u32[]{:S(2)}, u32[]{:S(2)}) collective-permute-start(bf16[64,2688]{1,0:T(8,128)(2,1)S(1)} %collective-permute-done.3.refs_4_), channel_id=1, source_target_pairs={{0,224},{32,0},{64,32},{96,64},{128,96},{160,128},{192,160},{224,1... | collective-permute-start | bytes 1032200 | tf_op jit(solution)/shard_map/ppermute | solution.py:32
  15.2 7.5 %collective-permute-done.1.refs_2_ = bf16[64,2688]{1,0:T(8,128)(2,1)S(1)} collective-permute-done((bf16[64,2688]{1,0:T(8,128)(2,1)S(1)}, bf16[64,2688]{1,0:T(8,128)(2,1)S(1)}, u32[]{:S(2)}, u32[]{:S(2)}) %collective-permute-start.1) | collective-permute-done | bytes 344096 | tf_op jit(solution)/shard_map/ppermute | solution.py:32
  22.7 0.4 collective-permute-done.4.refs_5_
  23.2 2.5 %collective-permute-start.5 = (bf16[64,2688]{1,0:T(8,128)(2,1)S(1)}, bf16[64,2688]{1,0:T(8,128)(2,1)S(1)}, u32[]{:S(2)}, u32[]{:S(2)}) collective-permute-start(bf16[64,2688]{1,0:T(8,128)(2,1)S(1)} %collective-permute-done.4.refs_5_), channel_id=1, source_target_pairs={{0,224},{32,0},{64,32},{96,64},{128,96},{160,128},{192,160},{224,1... | collective-permute-start | bytes 1032200 | tf_op jit(solution)/shard_map/ppermute | solution.py:32
  25.7 0.2 down.1
  25.9 3.1 %collective-permute-start.21 = (bf16[576,384]{1,0:T(8,128)(2,1)S(1)}, bf16[576,384]{1,0:T(8,128)(2,1)S(1)}, u32[]{:S(2)}, u32[]{:S(2)}) collective-permute-start(bf16[576,384]{1,0:T(8,128)(2,1)S(1)} %down.1), channel_id=1, source_target_pairs={{0,2},{16,18},{2,0},{18,16},{1,3},{17,19},{3,1},{19,17},{4,6},{20,... | collective-permute-start | bytes 1327112 | tf_op jit(solution)/shard_map/ppermute | solution.py:24
  29.0 0.6 collective-permute-start.22
  29.6 2.6 %collective-permute-start.23 = (bf16[576,384]{1,0:T(8,128)(2,1)S(1)}, bf16[576,384]{1,0:T(8,128)(2,1)S(1)}, u32[]{:S(2)}, u32[]{:S(2)}) collective-permute-start(bf16[576,384]{1,0:T(8,128)(2,1)S(1)} %down.1), channel_id=1, source_target_pairs={{0,18},{16,0},{2,16},{18,2},{1,19},{17,1},{3,17},{19,3},{4,22},{20... | collective-permute-start | bytes 1327112 | tf_op jit(solution)/shard_map/ppermute | solution.py:24
  32.3 1.5 %collective-permute-start.10 = (bf16[1,72,2688]{2,1,0:T(8,128)(2,1)S(1)}, bf16[1,72,2688]{2,1,0:T(8,128)(2,1)S(1)}, u32[]{:S(2)}, u32[]{:S(2)}) collective-permute-start(bf16[1,72,2688]{2,1,0:T(8,128)(2,1)S(1)} %slice.38), channel_id=1, source_target_pairs={{0,16},{16,2},{2,18},{18,0},{1,17},{17,3},{3,19},{19,1},{4,20},{20... | collective-permute-start | bytes 1161224 | tf_op jit(solution)/shard_map/ppermute | solution.py:24
  33.8 1.8 %collective-permute-start.11 = (bf16[1,72,2688]{2,1,0:T(8,128)(2,1)S(1)}, bf16[1,72,2688]{2,1,0:T(8,128)(2,1)S(1)}, u32[]{:S(2)}, u32[]{:S(2)}) collective-permute-start(bf16[1,72,2688]{2,1,0:T(8,128)(2,1)S(1)} %slice.39), channel_id=1, source_target_pairs={{0,18},{16,0},{2,16},{18,2},{1,19},{17,1},{3,17},{19,3},{4,22},{20... | collective-permute-start | bytes 1161224 | tf_op jit(solution)/shard_map/ppermute | solution.py:24
  35.7 4.9 %collective-permute-done.21 = bf16[576,384]{1,0:T(8,128)(2,1)S(1)} collective-permute-done((bf16[576,384]{1,0:T(8,128)(2,1)S(1)}, bf16[576,384]{1,0:T(8,128)(2,1)S(1)}, u32[]{:S(2)}, u32[]{:S(2)}) %collective-permute-start.21) | collective-permute-done | bytes 442400 | tf_op jit(solution)/shard_map/ppermute | solution.py:24
  40.5 0.4 collective-permute-start.6
  41.0 8.0 %collective-permute-done.22 = bf16[576,384]{1,0:T(8,128)(2,1)S(1)} collective-permute-done((bf16[576,384]{1,0:T(8,128)(2,1)S(1)}, bf16[576,384]{1,0:T(8,128)(2,1)S(1)}, u32[]{:S(2)}, u32[]{:S(2)}) %collective-permute-start.22) | collective-permute-done | bytes 442400 | tf_op jit(solution)/shard_map/ppermute | solution.py:24
  49.0 3.2 %collective-permute-start.7 = (bf16[32,2688]{1,0:T(8,128)(2,1)S(1)}, bf16[32,2688]{1,0:T(8,128)(2,1)S(1)}, u32[]{:S(2)}, u32[]{:S(2)}) collective-permute-start(bf16[32,2688]{1,0:T(8,128)(2,1)S(1)} %slice.37), channel_id=1, source_target_pairs={{0,224},{32,0},{64,32},{96,64},{128,96},{160,128},{192,160},{224,1... | collective-permute-start | bytes 516104 | tf_op jit(solution)/shard_map/ppermute | solution.py:32
  52.3 0.3 pad_maximum_fusion.refs_9_
  52.5 0.3 collective-permute-start.24
  52.8 2.6 %collective-permute-done.10.refs_12_ = bf16[1,72,2688]{2,1,0:T(8,128)(2,1)S(1)} collective-permute-done((bf16[1,72,2688]{2,1,0:T(8,128)(2,1)S(1)}, bf16[1,72,2688]{2,1,0:T(8,128)(2,1)S(1)}, u32[]{:S(2)}, u32[]{:S(2)}) %collective-permute-start.10) | collective-permute-done | bytes 387104 | tf_op jit(solution)/shard_map/ppermute | solution.py:24
  55.6 2.2 %first.1 = (f32[576,256]{1,0:T(8,128)S(1)}, f32[576,256]{1,0:T(8,128)S(1)}) custom-call(bf16[64,2688]{1,0:T(8,128)(2,1)S(1)} %constant_dynamic-slice_fusion.2.refs_0_, bf16[64,2688]{1,0:T(8,128)(2,1)S(1)} %collective-permute-done.refs_1_, bf16[64,2688]{1,0:T(8,128)(2,1)S(1)} %collective-permute-done.1.refs_2_, ...), custom_call_target="tpu_custom_call" | custom-call | flops 1585446912 | bytes 5849088 | tf_op jit(solution)/shard_map/first/pallas_call | solution.py:155
  57.9 2.0 %collective-permute-done.12 = f32[576,256]{1,0:T(8,128)S(1)} collective-permute-done((f32[576,256]{1,0:T(8,128)S(1)}, f32[576,256]{1,0:T(8,128)S(1)}, u32[]{:S(2)}, u32[]{:S(2)}) %collective-permute-start.12) | collective-permute-done | bytes 589856 | tf_op jit(solution)/shard_map/ppermute | solution.py:36
  60.1 0.6 collective-permute-start.13
  60.7 2.5 %collective-permute-start.16 = (bf16[288,256]{1,0:T(8,128)(2,1)S(1)}, bf16[288,256]{1,0:T(8,128)(2,1)S(1)}, u32[]{:S(2)}, u32[]{:S(2)}) collective-permute-start(bf16[288,256]{1,0:T(8,128)(2,1)S(1)} %fusion.refs_0_), channel_id=1, source_target_pairs={{0,224},{32,0},{64,32},{96,64},{128,96},{160,128},{192,160},{224,1... | collective-permute-start | bytes 442376 | tf_op jit(solution)/shard_map/ppermute | solution.py:32
  63.3 4.1 %collective-permute-done.13.refs_1_ = bf16[288,256]{1,0:T(8,128)(2,1)S(1)} collective-permute-done((bf16[288,256]{1,0:T(8,128)(2,1)S(1)}, bf16[288,256]{1,0:T(8,128)(2,1)S(1)}, u32[]{:S(2)}, u32[]{:S(2)}) %collective-permute-start.13) | collective-permute-done | bytes 147488 | tf_op jit(solution)/shard_map/ppermute | solution.py:32
  67.4 0.5 collective-permute-done.16.refs_4_
  67.8 2.5 %collective-permute-start.17 = (bf16[288,256]{1,0:T(8,128)(2,1)S(1)}, bf16[288,256]{1,0:T(8,128)(2,1)S(1)}, u32[]{:S(2)}, u32[]{:S(2)}) collective-permute-start(bf16[288,256]{1,0:T(8,128)(2,1)S(1)} %collective-permute-done.16.refs_4_), channel_id=1, source_target_pairs={{0,224},{32,0},{64,32},{96,64},{128,96},{160,128},{192,160},{224,1... | collective-permute-start | bytes 442376 | tf_op jit(solution)/shard_map/ppermute | solution.py:32
  70.3 3.3 %collective-permute-done.14.refs_2_ = bf16[288,256]{1,0:T(8,128)(2,1)S(1)} collective-permute-done((bf16[288,256]{1,0:T(8,128)(2,1)S(1)}, bf16[288,256]{1,0:T(8,128)(2,1)S(1)}, u32[]{:S(2)}, u32[]{:S(2)}) %collective-permute-start.14) | collective-permute-done | bytes 147488 | tf_op jit(solution)/shard_map/ppermute | solution.py:32
  73.6 0.2 collective-permute-done.17.refs_5_
  73.7 2.9 %collective-permute-start.18 = (bf16[288,256]{1,0:T(8,128)(2,1)S(1)}, bf16[288,256]{1,0:T(8,128)(2,1)S(1)}, u32[]{:S(2)}, u32[]{:S(2)}) collective-permute-start(bf16[288,256]{1,0:T(8,128)(2,1)S(1)} %collective-permute-done.17.refs_5_), channel_id=1, source_target_pairs={{0,224},{32,0},{64,32},{96,64},{128,96},{160,128},{192,160},{224,1... | collective-permute-start | bytes 442376 | tf_op jit(solution)/shard_map/ppermute | solution.py:32
  76.6 3.1 %collective-permute-done.15.refs_3_ = bf16[288,256]{1,0:T(8,128)(2,1)S(1)} collective-permute-done((bf16[288,256]{1,0:T(8,128)(2,1)S(1)}, bf16[288,256]{1,0:T(8,128)(2,1)S(1)}, u32[]{:S(2)}, u32[]{:S(2)}) %collective-permute-start.15) | collective-permute-done | bytes 147488 | tf_op jit(solution)/shard_map/ppermute | solution.py:32
  79.9 3.2 %collective-permute-start.20 = (bf16[144,256]{1,0:T(8,128)(2,1)S(1)}, bf16[144,256]{1,0:T(8,128)(2,1)S(1)}, u32[]{:S(2)}, u32[]{:S(2)}) collective-permute-start(bf16[144,256]{1,0:T(8,128)(2,1)S(1)} %slice.43), channel_id=1, source_target_pairs={{0,224},{32,0},{64,32},{96,64},{128,96},{160,128},{192,160},{224,1... | collective-permute-start | bytes 221192 | tf_op jit(solution)/shard_map/ppermute | solution.py:32
  83.1 2.2 %collective-permute-done.19.refs_7_ = bf16[144,256]{1,0:T(8,128)(2,1)S(1)} collective-permute-done((bf16[144,256]{1,0:T(8,128)(2,1)S(1)}, bf16[144,256]{1,0:T(8,128)(2,1)S(1)}, u32[]{:S(2)}, u32[]{:S(2)}) %collective-permute-start.19) | collective-permute-done | bytes 73760 | tf_op jit(solution)/shard_map/ppermute | solution.py:32
  85.3 0.2 collective-permute-done.20.refs_8_
  85.5 2.0 %second.1 = (bf16[64,768]{1,0:T(8,128)(2,1)S(1)}, bf16[64,768]{1,0:T(8,128)(2,1)S(1)}, bf16[64,768]{1,0:T(8,128)(2,1)S(1)}, bf16[64,768]{1,0:T(8,128)(2,1)S(1)}) custom-call(bf16[288,256]{1,0:T(8,128)(2,1)S(1)} %fusion.refs_0_, bf16[288,256]{1,0:T(8,128)(2,1)S(1)} %collective-permute-done.13.refs_1_, bf16[288,256]{1,0:T(8,128)(2,1)S(1)} %collective-permute-done.14.refs_2_, ...), custom_call_target="tpu_custom_call" | custom-call | flops 905969664 | bytes 6291456 | tf_op jit(solution)/shard_map/second/pallas_call | solution.py:171
  87.4 0.3 collective-permute-start.25
  87.7 2.6 %collective-permute-start.26 = (bf16[64,768]{1,0:T(8,128)(2,1)S(1)}, bf16[64,768]{1,0:T(8,128)(2,1)S(1)}, u32[]{:S(2)}, u32[]{:S(2)}) collective-permute-start(bf16[64,768]{1,0:T(8,128)(2,1)S(1)} %get-tuple-element.15), channel_id=1, source_target_pairs={{0,8},{4,12},{8,0},{12,4},{1,9},{5,13},{9,1},{13,5},{2,10},{6,14},... | collective-permute-start | bytes 294920 | tf_op jit(solution)/shard_map/ppermute | solution.py:28
  90.3 1.8 %collective-permute-done.25 = bf16[64,768]{1,0:T(8,128)(2,1)S(1)} collective-permute-done((bf16[64,768]{1,0:T(8,128)(2,1)S(1)}, bf16[64,768]{1,0:T(8,128)(2,1)S(1)}, u32[]{:S(2)}, u32[]{:S(2)}) %collective-permute-start.25) | collective-permute-done | bytes 98336 | tf_op jit(solution)/shard_map/ppermute | solution.py:28
  92.1 1.7 %collective-permute-done.26 = bf16[64,768]{1,0:T(8,128)(2,1)S(1)} collective-permute-done((bf16[64,768]{1,0:T(8,128)(2,1)S(1)}, bf16[64,768]{1,0:T(8,128)(2,1)S(1)}, u32[]{:S(2)}, u32[]{:S(2)}) %collective-permute-start.26) | collective-permute-done | bytes 98336 | tf_op jit(solution)/shard_map/ppermute | solution.py:28
  93.9 2.3 %collective-permute-done.27 = bf16[64,768]{1,0:T(8,128)(2,1)S(1)} collective-permute-done((bf16[64,768]{1,0:T(8,128)(2,1)S(1)}, bf16[64,768]{1,0:T(8,128)(2,1)S(1)}, u32[]{:S(2)}, u32[]{:S(2)}) %collective-permute-start.27) | collective-permute-done | bytes 98336 | tf_op jit(solution)/shard_map/ppermute | solution.py:28
  96.2 9.5 %collective-permute-start.28 = (bf16[64,384]{1,0:T(8,128)(2,1)S(1)}, bf16[64,384]{1,0:T(8,128)(2,1)S(1)}, u32[]{:S(2)}, u32[]{:S(2)}) collective-permute-start(bf16[64,384]{1,0:T(8,128)(2,1)S(1)} %get-tuple-element.19), channel_id=1, source_target_pairs={{0,0},{1,128},{2,1},{3,129},{4,32},{5,160},{6,33},{7,161},{8,64},{... | collective-permute-start | bytes 147464 | tf_op jit(solution)/shard_map/ppermute | solution.py:185
  105.8 1.8 %collective-permute-done.28 = bf16[64,384]{1,0:T(8,128)(2,1)S(1)} collective-permute-done((bf16[64,384]{1,0:T(8,128)(2,1)S(1)}, bf16[64,384]{1,0:T(8,128)(2,1)S(1)}, u32[]{:S(2)}, u32[]{:S(2)}) %collective-permute-start.28) | collective-permute-done | bytes 49184 | tf_op jit(solution)/shard_map/ppermute | solution.py:185
  107.6 10.1 %collective-permute-done.29 = bf16[64,384]{1,0:T(8,128)(2,1)S(1)} collective-permute-done((bf16[64,384]{1,0:T(8,128)(2,1)S(1)}, bf16[64,384]{1,0:T(8,128)(2,1)S(1)}, u32[]{:S(2)}, u32[]{:S(2)}) %collective-permute-start.29) | collective-permute-done | bytes 49184 | tf_op jit(solution)/shard_map/ppermute | solution.py:185
  117.8 0.7 copy.7
  (35 shorter events, 1.1 us)
Async XLA Ops:
  0.0 1.1 copy-start
  0.0 25.7 %copy-start.1 = (bf16[576,336]{0,1:T(8,128)(2,1)S(1)}, bf16[576,336]{0,1:T(8,128)(2,1)}, u32[]{:S(2)}) copy-start(bf16[576,336]{0,1:T(8,128)(2,1)} %param.7) | copy-start | bytes 1161220
  1.1 9.9 %collective-permute-start = (bf16[64,2688]{1,0:T(8,128)(2,1)S(1)}, bf16[64,2688]{1,0:T(8,128)(2,1)S(1)}, u32[]{:S(2)}, u32[]{:S(2)}) collective-permute-start(bf16[64,2688]{1,0:T(8,128)(2,1)S(1)} %constant_dynamic-slice_fusion.2.refs_0_), channel_id=1, source_target_pairs={{0,32},{32,64},{64,96},{96,128},{128,160},{160,192},{192,224},{224... | collective-permute-start | bytes 1032200 | tf_op jit(solution)/shard_map/ppermute | solution.py:32
  3.1 9.8 %collective-permute-start.3 = (bf16[64,2688]{1,0:T(8,128)(2,1)S(1)}, bf16[64,2688]{1,0:T(8,128)(2,1)S(1)}, u32[]{:S(2)}, u32[]{:S(2)}) collective-permute-start(bf16[64,2688]{1,0:T(8,128)(2,1)S(1)} %constant_dynamic-slice_fusion.2.refs_0_), channel_id=1, source_target_pairs={{0,224},{32,0},{64,32},{96,64},{128,96},{160,128},{192,160},{224,1... | collective-permute-start | bytes 1032200 | tf_op jit(solution)/shard_map/ppermute | solution.py:32
  4.4 24.6 %collective-permute-start.8 = (bf16[2,72,2688]{2,1,0:T(8,128)(2,1)S(1)}, bf16[2,72,2688]{2,1,0:T(8,128)(2,1)S(1)}, u32[]{:S(2)}, u32[]{:S(2)}) collective-permute-start(bf16[2,72,2688]{2,1,0:T(8,128)(2,1)S(1)} %pad_maximum_fusion.1.refs_9_), channel_id=1, source_target_pairs={{0,16},{16,2},{2,18},{18,0},{1,17},{17,3},{3,19},{19,1},{4,20},{20... | collective-permute-start | bytes 2322440 | tf_op jit(solution)/shard_map/ppermute | solution.py:24
  6.0 23.6 %collective-permute-start.9 = (bf16[2,72,2688]{2,1,0:T(8,128)(2,1)S(1)}, bf16[2,72,2688]{2,1,0:T(8,128)(2,1)S(1)}, u32[]{:S(2)}, u32[]{:S(2)}) collective-permute-start(bf16[2,72,2688]{2,1,0:T(8,128)(2,1)S(1)} %pad_maximum_fusion.1.refs_9_), channel_id=1, source_target_pairs={{0,18},{16,0},{2,16},{18,2},{1,19},{17,1},{3,17},{19,3},{4,22},{20... | collective-permute-start | bytes 2322440 | tf_op jit(solution)/shard_map/ppermute | solution.py:24
  11.0 11.7 %collective-permute-start.1 = (bf16[64,2688]{1,0:T(8,128)(2,1)S(1)}, bf16[64,2688]{1,0:T(8,128)(2,1)S(1)}, u32[]{:S(2)}, u32[]{:S(2)}) collective-permute-start(bf16[64,2688]{1,0:T(8,128)(2,1)S(1)} %collective-permute-done.refs_1_), channel_id=1, source_target_pairs={{0,32},{32,64},{64,96},{96,128},{128,160},{160,192},{192,224},{224... | collective-permute-start | bytes 1032200 | tf_op jit(solution)/shard_map/ppermute | solution.py:32
  12.9 10.2 %collective-permute-start.4 = (bf16[64,2688]{1,0:T(8,128)(2,1)S(1)}, bf16[64,2688]{1,0:T(8,128)(2,1)S(1)}, u32[]{:S(2)}, u32[]{:S(2)}) collective-permute-start(bf16[64,2688]{1,0:T(8,128)(2,1)S(1)} %collective-permute-done.3.refs_4_), channel_id=1, source_target_pairs={{0,224},{32,0},{64,32},{96,64},{128,96},{160,128},{192,160},{224,1... | collective-permute-start | bytes 1032200 | tf_op jit(solution)/shard_map/ppermute | solution.py:32
  22.7 9.6 %collective-permute-start.2 = (bf16[64,2688]{1,0:T(8,128)(2,1)S(1)}, bf16[64,2688]{1,0:T(8,128)(2,1)S(1)}, u32[]{:S(2)}, u32[]{:S(2)}) collective-permute-start(bf16[64,2688]{1,0:T(8,128)(2,1)S(1)} %collective-permute-done.1.refs_2_), channel_id=1, source_target_pairs={{0,32},{32,64},{64,96},{96,128},{128,160},{160,192},{192,224},{224... | collective-permute-start | bytes 1032200 | tf_op jit(solution)/shard_map/ppermute | solution.py:32
  23.2 10.6 %collective-permute-start.5 = (bf16[64,2688]{1,0:T(8,128)(2,1)S(1)}, bf16[64,2688]{1,0:T(8,128)(2,1)S(1)}, u32[]{:S(2)}, u32[]{:S(2)}) collective-permute-start(bf16[64,2688]{1,0:T(8,128)(2,1)S(1)} %collective-permute-done.4.refs_5_), channel_id=1, source_target_pairs={{0,224},{32,0},{64,32},{96,64},{128,96},{160,128},{192,160},{224,1... | collective-permute-start | bytes 1032200 | tf_op jit(solution)/shard_map/ppermute | solution.py:32
  25.9 14.7 %collective-permute-start.21 = (bf16[576,384]{1,0:T(8,128)(2,1)S(1)}, bf16[576,384]{1,0:T(8,128)(2,1)S(1)}, u32[]{:S(2)}, u32[]{:S(2)}) collective-permute-start(bf16[576,384]{1,0:T(8,128)(2,1)S(1)} %down.1), channel_id=1, source_target_pairs={{0,2},{16,18},{2,0},{18,16},{1,3},{17,19},{3,1},{19,17},{4,6},{20,... | collective-permute-start | bytes 1327112 | tf_op jit(solution)/shard_map/ppermute | solution.py:24
  29.0 20.0 %collective-permute-start.22 = (bf16[576,384]{1,0:T(8,128)(2,1)S(1)}, bf16[576,384]{1,0:T(8,128)(2,1)S(1)}, u32[]{:S(2)}, u32[]{:S(2)}) collective-permute-start(bf16[576,384]{1,0:T(8,128)(2,1)S(1)} %down.1), channel_id=1, source_target_pairs={{0,16},{16,2},{2,18},{18,0},{1,17},{17,3},{3,19},{19,1},{4,20},{20... | collective-permute-start | bytes 1327112 | tf_op jit(solution)/shard_map/ppermute | solution.py:24
  29.6 22.7 %collective-permute-start.23 = (bf16[576,384]{1,0:T(8,128)(2,1)S(1)}, bf16[576,384]{1,0:T(8,128)(2,1)S(1)}, u32[]{:S(2)}, u32[]{:S(2)}) collective-permute-start(bf16[576,384]{1,0:T(8,128)(2,1)S(1)} %down.1), channel_id=1, source_target_pairs={{0,18},{16,0},{2,16},{18,2},{1,19},{17,1},{3,17},{19,3},{4,22},{20... | collective-permute-start | bytes 1327112 | tf_op jit(solution)/shard_map/ppermute | solution.py:24
  32.3 23.1 %collective-permute-start.10 = (bf16[1,72,2688]{2,1,0:T(8,128)(2,1)S(1)}, bf16[1,72,2688]{2,1,0:T(8,128)(2,1)S(1)}, u32[]{:S(2)}, u32[]{:S(2)}) collective-permute-start(bf16[1,72,2688]{2,1,0:T(8,128)(2,1)S(1)} %slice.38), channel_id=1, source_target_pairs={{0,16},{16,2},{2,18},{18,0},{1,17},{17,3},{3,19},{19,1},{4,20},{20... | collective-permute-start | bytes 1161224 | tf_op jit(solution)/shard_map/ppermute | solution.py:24
  33.8 21.8 %collective-permute-start.11 = (bf16[1,72,2688]{2,1,0:T(8,128)(2,1)S(1)}, bf16[1,72,2688]{2,1,0:T(8,128)(2,1)S(1)}, u32[]{:S(2)}, u32[]{:S(2)}) collective-permute-start(bf16[1,72,2688]{2,1,0:T(8,128)(2,1)S(1)} %slice.39), channel_id=1, source_target_pairs={{0,18},{16,0},{2,16},{18,2},{1,19},{17,1},{3,17},{19,3},{4,22},{20... | collective-permute-start | bytes 1161224 | tf_op jit(solution)/shard_map/ppermute | solution.py:24
  40.5 15.0 %collective-permute-start.6 = (bf16[32,2688]{1,0:T(8,128)(2,1)S(1)}, bf16[32,2688]{1,0:T(8,128)(2,1)S(1)}, u32[]{:S(2)}, u32[]{:S(2)}) collective-permute-start(bf16[32,2688]{1,0:T(8,128)(2,1)S(1)} %slice.36), channel_id=1, source_target_pairs={{0,32},{32,64},{64,96},{96,128},{128,160},{160,192},{192,224},{224... | collective-permute-start | bytes 516104 | tf_op jit(solution)/shard_map/ppermute | solution.py:32
  49.0 6.5 %collective-permute-start.7 = (bf16[32,2688]{1,0:T(8,128)(2,1)S(1)}, bf16[32,2688]{1,0:T(8,128)(2,1)S(1)}, u32[]{:S(2)}, u32[]{:S(2)}) collective-permute-start(bf16[32,2688]{1,0:T(8,128)(2,1)S(1)} %slice.37), channel_id=1, source_target_pairs={{0,224},{32,0},{64,32},{96,64},{128,96},{160,128},{192,160},{224,1... | collective-permute-start | bytes 516104 | tf_op jit(solution)/shard_map/ppermute | solution.py:32
  52.5 30.6 %collective-permute-start.24 = (bf16[4,576,384]{2,1,0:T(8,128)(2,1)S(1)}, bf16[4,576,384]{2,1,0:T(8,128)(2,1)S(1)}, u32[]{:S(2)}, u32[]{:S(2)}) collective-permute-start(bf16[4,576,384]{2,1,0:T(8,128)(2,1)S(1)} %pad_maximum_fusion.refs_9_), channel_id=1, source_target_pairs={{0,1},{1,0},{2,3},{3,2},{4,5},{5,4},{6,7},{7,6},{8,9},{9,8},{10,11... | collective-permute-start | bytes 5308424 | tf_op jit(solution)/shard_map/ppermute | solution.py:36
  57.8 2.1 %collective-permute-start.12 = (f32[576,256]{1,0:T(8,128)S(1)}, f32[576,256]{1,0:T(8,128)S(1)}, u32[]{:S(2)}, u32[]{:S(2)}) collective-permute-start(f32[576,256]{1,0:T(8,128)S(1)} %get-tuple-element.12), channel_id=1, source_target_pairs={{0,1},{1,0},{2,3},{3,2},{4,5},{5,4},{6,7},{7,6},{8,9},{9,8},{10,11... | collective-permute-start | bytes 1769480 | tf_op jit(solution)/shard_map/ppermute | solution.py:36
  60.1 7.2 %collective-permute-start.13 = (bf16[288,256]{1,0:T(8,128)(2,1)S(1)}, bf16[288,256]{1,0:T(8,128)(2,1)S(1)}, u32[]{:S(2)}, u32[]{:S(2)}) collective-permute-start(bf16[288,256]{1,0:T(8,128)(2,1)S(1)} %fusion.refs_0_), channel_id=1, source_target_pairs={{0,32},{32,64},{64,96},{96,128},{128,160},{160,192},{192,224},{224... | collective-permute-start | bytes 442376 | tf_op jit(solution)/shard_map/ppermute | solution.py:32
  60.7 7.1 %collective-permute-start.16 = (bf16[288,256]{1,0:T(8,128)(2,1)S(1)}, bf16[288,256]{1,0:T(8,128)(2,1)S(1)}, u32[]{:S(2)}, u32[]{:S(2)}) collective-permute-start(bf16[288,256]{1,0:T(8,128)(2,1)S(1)} %fusion.refs_0_), channel_id=1, source_target_pairs={{0,224},{32,0},{64,32},{96,64},{128,96},{160,128},{192,160},{224,1... | collective-permute-start | bytes 442376 | tf_op jit(solution)/shard_map/ppermute | solution.py:32
  67.3 6.2 %collective-permute-start.14 = (bf16[288,256]{1,0:T(8,128)(2,1)S(1)}, bf16[288,256]{1,0:T(8,128)(2,1)S(1)}, u32[]{:S(2)}, u32[]{:S(2)}) collective-permute-start(bf16[288,256]{1,0:T(8,128)(2,1)S(1)} %collective-permute-done.13.refs_1_), channel_id=1, source_target_pairs={{0,32},{32,64},{64,96},{96,128},{128,160},{160,192},{192,224},{224... | collective-permute-start | bytes 442376 | tf_op jit(solution)/shard_map/ppermute | solution.py:32
  67.8 5.9 %collective-permute-start.17 = (bf16[288,256]{1,0:T(8,128)(2,1)S(1)}, bf16[288,256]{1,0:T(8,128)(2,1)S(1)}, u32[]{:S(2)}, u32[]{:S(2)}) collective-permute-start(bf16[288,256]{1,0:T(8,128)(2,1)S(1)} %collective-permute-done.16.refs_4_), channel_id=1, source_target_pairs={{0,224},{32,0},{64,32},{96,64},{128,96},{160,128},{192,160},{224,1... | collective-permute-start | bytes 442376 | tf_op jit(solution)/shard_map/ppermute | solution.py:32
  73.6 6.2 %collective-permute-start.15 = (bf16[288,256]{1,0:T(8,128)(2,1)S(1)}, bf16[288,256]{1,0:T(8,128)(2,1)S(1)}, u32[]{:S(2)}, u32[]{:S(2)}) collective-permute-start(bf16[288,256]{1,0:T(8,128)(2,1)S(1)} %collective-permute-done.14.refs_2_), channel_id=1, source_target_pairs={{0,32},{32,64},{64,96},{96,128},{128,160},{160,192},{192,224},{224... | collective-permute-start | bytes 442376 | tf_op jit(solution)/shard_map/ppermute | solution.py:32
  73.7 6.2 %collective-permute-start.18 = (bf16[288,256]{1,0:T(8,128)(2,1)S(1)}, bf16[288,256]{1,0:T(8,128)(2,1)S(1)}, u32[]{:S(2)}, u32[]{:S(2)}) collective-permute-start(bf16[288,256]{1,0:T(8,128)(2,1)S(1)} %collective-permute-done.17.refs_5_), channel_id=1, source_target_pairs={{0,224},{32,0},{64,32},{96,64},{128,96},{160,128},{192,160},{224,1... | collective-permute-start | bytes 442376 | tf_op jit(solution)/shard_map/ppermute | solution.py:32
  79.8 5.6 %collective-permute-start.19 = (bf16[144,256]{1,0:T(8,128)(2,1)S(1)}, bf16[144,256]{1,0:T(8,128)(2,1)S(1)}, u32[]{:S(2)}, u32[]{:S(2)}) collective-permute-start(bf16[144,256]{1,0:T(8,128)(2,1)S(1)} %slice.42), channel_id=1, source_target_pairs={{0,32},{32,64},{64,96},{96,128},{128,160},{160,192},{192,224},{224... | collective-permute-start | bytes 221192 | tf_op jit(solution)/shard_map/ppermute | solution.py:32
  79.9 5.6 %collective-permute-start.20 = (bf16[144,256]{1,0:T(8,128)(2,1)S(1)}, bf16[144,256]{1,0:T(8,128)(2,1)S(1)}, u32[]{:S(2)}, u32[]{:S(2)}) collective-permute-start(bf16[144,256]{1,0:T(8,128)(2,1)S(1)} %slice.43), channel_id=1, source_target_pairs={{0,224},{32,0},{64,32},{96,64},{128,96},{160,128},{192,160},{224,1... | collective-permute-start | bytes 221192 | tf_op jit(solution)/shard_map/ppermute | solution.py:32
  87.4 4.7 %collective-permute-start.25 = (bf16[64,768]{1,0:T(8,128)(2,1)S(1)}, bf16[64,768]{1,0:T(8,128)(2,1)S(1)}, u32[]{:S(2)}, u32[]{:S(2)}) collective-permute-start(bf16[64,768]{1,0:T(8,128)(2,1)S(1)} %get-tuple-element.14), channel_id=1, source_target_pairs={{0,4},{4,8},{8,12},{12,0},{1,5},{5,9},{9,13},{13,1},{2,6},{6,10},{... | collective-permute-start | bytes 294920 | tf_op jit(solution)/shard_map/ppermute | solution.py:28
  87.7 6.1 %collective-permute-start.26 = (bf16[64,768]{1,0:T(8,128)(2,1)S(1)}, bf16[64,768]{1,0:T(8,128)(2,1)S(1)}, u32[]{:S(2)}, u32[]{:S(2)}) collective-permute-start(bf16[64,768]{1,0:T(8,128)(2,1)S(1)} %get-tuple-element.15), channel_id=1, source_target_pairs={{0,8},{4,12},{8,0},{12,4},{1,9},{5,13},{9,1},{13,5},{2,10},{6,14},... | collective-permute-start | bytes 294920 | tf_op jit(solution)/shard_map/ppermute | solution.py:28
  90.3 5.8 %collective-permute-start.27 = (bf16[64,768]{1,0:T(8,128)(2,1)S(1)}, bf16[64,768]{1,0:T(8,128)(2,1)S(1)}, u32[]{:S(2)}, u32[]{:S(2)}) collective-permute-start(bf16[64,768]{1,0:T(8,128)(2,1)S(1)} %get-tuple-element.16), channel_id=1, source_target_pairs={{0,12},{4,0},{8,4},{12,8},{1,13},{5,1},{9,5},{13,9},{2,14},{6,2},{... | collective-permute-start | bytes 294920 | tf_op jit(solution)/shard_map/ppermute | solution.py:28
  96.2 11.4 %collective-permute-start.28 = (bf16[64,384]{1,0:T(8,128)(2,1)S(1)}, bf16[64,384]{1,0:T(8,128)(2,1)S(1)}, u32[]{:S(2)}, u32[]{:S(2)}) collective-permute-start(bf16[64,384]{1,0:T(8,128)(2,1)S(1)} %get-tuple-element.19), channel_id=1, source_target_pairs={{0,0},{1,128},{2,1},{3,129},{4,32},{5,160},{6,33},{7,161},{8,64},{... | collective-permute-start | bytes 147464 | tf_op jit(solution)/shard_map/ppermute | solution.py:185
  105.7 12.0 %collective-permute-start.29 = (bf16[64,384]{1,0:T(8,128)(2,1)S(1)}, bf16[64,384]{1,0:T(8,128)(2,1)S(1)}, u32[]{:S(2)}, u32[]{:S(2)}) collective-permute-start(bf16[64,384]{1,0:T(8,128)(2,1)S(1)} %get-tuple-element.20), channel_id=1, source_target_pairs={{0,1},{1,129},{2,0},{3,128},{4,33},{5,161},{6,32},{7,160},{8,65},{... | collective-permute-start | bytes 147464 | tf_op jit(solution)/shard_map/ppermute | solution.py:185

commit v2 on v1

--- a/solution.py
+++ b/solution.py
@@ -43,6 +43,33 @@
         ups.append(pz(ups[-1], 1))
         downs.append(pz(downs[-1], -1))
     return ups + downs[1:] + [pz(ups[-1][:half], 1), pz(downs[-1][half:], -1)]
+
+
+def z_direct(block):
+    half = block.shape[0] // 2
+    up2, dn2 = pz(block, 2), pz(block, -2)
+    up1, dn1 = pz(block, 1), pz(block, -1)
+    up4, dn4 = pz(up2[:half], 2), pz(dn2[half:], -2)
+    up3, dn3 = pz(up2, 1), pz(dn2, -1)
+    return [block, up1, up2, up3, dn1, dn2, dn3, up4, dn4]
+
+
+def kept(z, c, y):
+    def span(a, b, n):
+        return min((a - b) % n, (b - a) % n)
+
+    targets = sorted(range(4), key=lambda j: (-span(z, 4 * c + j, Z), j))
+    owners = sorted(range(Y), key=lambda w: (span(w, z // 2, Y), w))
+    return targets[owners.index(y)]
+
+
+def kept_at(z, c, y):
+    value = jnp.int32(0)
+    for cc in range(C):
+        for w in range(Y):
+            word = sum(kept(zz, cc, w) << (2 * zz) for zz in range(Z))
+            value = jnp.where((c == cc) & (y == w), jnp.int32(word), value)
+    return lax.shift_right_logical(value, (2 * z).astype(jnp.int32)) & 3
 
 
 def down_kernel(down_t, out):
@@ -107,7 +134,7 @@
                 total = term if total is None else total + term
         val[...] = total
         for k, out in enumerate(outs):
-            at = lax.rem(y + k, 4) * t
+            at = kept_at(z, c, lax.rem(y + k, 4)) * t
             out[:, d * PAD:(d + 1) * PAD] = val[pl.ds(pl.multiple_of(at, t), t), :].astype(out.dtype)
 
 
@@ -123,7 +150,7 @@
             for xh in range(XH):
                 for c in range(C):
                     src = ((z * Y + y) * XH + xh) * C + c
-                    dst = (((4 * c + y) * Y + z // 2) * XH + z % 2) * C
+                    dst = (((4 * c + kept(z, c, y)) * Y + z // 2) * XH + z % 2) * C
                     final_perms[0].append((src, dst + xh))
                     final_perms[1].append((src, dst + 1 - xh))
 
@@ -147,7 +174,8 @@
             cost_estimate=pl.CostEstimate(flops=10**8, bytes_accessed=1 << 20, transcendentals=0),
             name="down",
         )(down.T)
-        near = jnp.stack([dblk, px(dblk, 2), px(dblk, 1), px(dblk, -1)])
+        near = [dblk, px(dblk, 2), px(dblk, 1), px(dblk, -1)]
+        near = jnp.stack(near)
         far = core_swap(near)
 
         m, t = 8 * units, Z * n
@@ -166,7 +194,7 @@
         g, u = whole[:, 0], whole[:, 1]
         hidden = (jax.nn.silu(g) * u).astype(bf16).reshape(4 * units, t // 2)
 
-        hids = z_ring(hidden)
+        hids = z_direct(hidden)
         piece = jax.ShapeDtypeStruct((n, 2 * PAD), bf16)
         shares = pl.pallas_call(
             second_kernel,

time: 119 us -> 112 us (0.941)
  waiting for transfers between devices: 60.2 us -> 49.9 us
  starting transfers between devices: 50.1 us -> 53.9 us
    ppermute x16, starting transfers between devices: 24.3 us -> 35.1 us  [pz(): return lax.ppermute(v, 'z', ring(Z, k))]
    ppermute x7, waiting for transfers between devices: 15.7 us -> 7.82 us  [px(): return lax.ppermute(v, ('xl', 'xh'), x_ring(k))]
    ppermute x1, starting transfers between devices: 9.49 us -> 3.09 us  [body(): lax.ppermute(mine, final_axes, final_perms[0])]
    ppermute x1, waiting for transfers between devices: 10.1 us -> 5.41 us  [body(): lax.ppermute(other, final_axes, final_perms[1])]
    ppermute x1, waiting for transfers between devices: 1.79 us -> 6.19 us  [body(): lax.ppermute(mine, final_axes, final_perms[0])]
    ppermute x16, waiting for transfers between devices: 24.8 us -> 22.7 us  [pz(): return lax.ppermute(v, 'z', ring(Z, k))]
  transfers between devices with their start and end apart: 30 -> 30, of which waited for: 21 -> 17; matrix products, arithmetic and copies ran while one was open for 1% -> 2% of each run, Pallas kernels for 2% -> 2%
where the time goes in v2:
time: 112 us
  starting transfers between devices  53.9 us (48%)
  waiting for transfers between devices  49.9 us (45%)
  Pallas kernels  4.39 us (4%)
  local copies, waits for them, and re-layouts  2.03 us (2%)
  other arithmetic  1.71 us (2%)
    ppermute x16, starting transfers between devices, pz(): return lax.ppermute(v, 'z', ring(Z, k))  35.1 us
    ppermute x16, waiting for transfers between devices, pz(): return lax.ppermute(v, 'z', ring(Z, k))  22.7 us
    ppermute x7, starting transfers between devices, px(): return lax.ppermute(v, ('xl', 'xh'), x_ring(k))  12.7 us
    ppermute x7, waiting for transfers between devices, px(): return lax.ppermute(v, ('xl', 'xh'), x_ring(k))  7.82 us
    ppermute x1, waiting for transfers between devices, body(): lax.ppermute(mine, final_axes, final_perms[0])  6.19 us
    ppermute x3, waiting for transfers between devices, py(): return lax.ppermute(v, 'y', ring(Y, k))  5.82 us
    ppermute x1, waiting for transfers between devices, body(): lax.ppermute(other, final_axes, final_perms[1])  5.41 us
    ppermute x1, starting transfers between devices, body(): lax.ppermute(mine, final_axes, final_perms[0])  3.09 us
  transfers between devices with their start and end apart: 30, of which 17 were waited for; matrix products, arithmetic and copies ran while one was open for 2% of the time, Pallas kernels for 2%

profile of v2, /device:TPU:56, one launch (start us, length us, event | category | flops | bytes accessed | tf_op | source)
XLA Modules:
  0.0 112.1 jit_solution(3302290456481204636)
XLA Ops:
  0.0 1.1 copy-done
  1.1 2.0 %collective-permute-start = (bf16[64,2688]{1,0:T(8,128)(2,1)S(1)}, bf16[64,2688]{1,0:T(8,128)(2,1)S(1)}, u32[]{:S(2)}, u32[]{:S(2)}) collective-permute-start(bf16[64,2688]{1,0:T(8,128)(2,1)S(1)} %constant_dynamic-slice_fusion.2.refs_0_), channel_id=1, source_target_pairs={{0,32},{32,64},{64,96},{96,128},{128,160},{160,192},{192,224},{224... | collective-permute-start | bytes 1032200 | tf_op jit(solution)/shard_map/ppermute | solution.py:32
  3.1 0.1 collective-permute-start.3
  3.2 1.2 %pad_maximum_fusion.1.refs_9_ = bf16[2,72,2688]{2,1,0:T(8,128)(2,1)S(1)} fusion(bf16[1,72,2688]{2,1,0:T(8,128)(2,1)} %bitcast.35, bf16[1,72,2688]{2,1,0:T(8,128)(2,1)} %bitcast.36), kind=kLoop, calls=%fused_computation.1 | loop fusion | flops 387072 | bytes 1548288 | tf_op jit(solution)/shard_map/stack | solution.py:164
  4.4 1.6 %collective-permute-start.8 = (bf16[2,72,2688]{2,1,0:T(8,128)(2,1)S(1)}, bf16[2,72,2688]{2,1,0:T(8,128)(2,1)S(1)}, u32[]{:S(2)}, u32[]{:S(2)}) collective-permute-start(bf16[2,72,2688]{2,1,0:T(8,128)(2,1)S(1)} %pad_maximum_fusion.1.refs_9_), channel_id=1, source_target_pairs={{0,16},{16,2},{2,18},{18,0},{1,17},{17,3},{3,19},{19,1},{4,20},{20... | collective-permute-start | bytes 2322440 | tf_op jit(solution)/shard_map/ppermute | solution.py:24
  6.0 1.7 %collective-permute-start.9 = (bf16[2,72,2688]{2,1,0:T(8,128)(2,1)S(1)}, bf16[2,72,2688]{2,1,0:T(8,128)(2,1)S(1)}, u32[]{:S(2)}, u32[]{:S(2)}) collective-permute-start(bf16[2,72,2688]{2,1,0:T(8,128)(2,1)S(1)} %pad_maximum_fusion.1.refs_9_), channel_id=1, source_target_pairs={{0,18},{16,0},{2,16},{18,2},{1,19},{17,1},{3,17},{19,3},{4,22},{20... | collective-permute-start | bytes 2322440 | tf_op jit(solution)/shard_map/ppermute | solution.py:24
  7.7 3.3 %collective-permute-done.refs_1_ = bf16[64,2688]{1,0:T(8,128)(2,1)S(1)} collective-permute-done((bf16[64,2688]{1,0:T(8,128)(2,1)S(1)}, bf16[64,2688]{1,0:T(8,128)(2,1)S(1)}, u32[]{:S(2)}, u32[]{:S(2)}) %collective-permute-start) | collective-permute-done | bytes 344096 | tf_op jit(solution)/shard_map/ppermute | solution.py:32
  11.0 1.9 %collective-permute-start.1 = (bf16[64,2688]{1,0:T(8,128)(2,1)S(1)}, bf16[64,2688]{1,0:T(8,128)(2,1)S(1)}, u32[]{:S(2)}, u32[]{:S(2)}) collective-permute-start(bf16[64,2688]{1,0:T(8,128)(2,1)S(1)} %collective-permute-done.refs_1_), channel_id=1, source_target_pairs={{0,32},{32,64},{64,96},{96,128},{128,160},{160,192},{192,224},{224... | collective-permute-start | bytes 1032200 | tf_op jit(solution)/shard_map/ppermute | solution.py:32
  12.9 2.3 %collective-permute-start.4 = (bf16[64,2688]{1,0:T(8,128)(2,1)S(1)}, bf16[64,2688]{1,0:T(8,128)(2,1)S(1)}, u32[]{:S(2)}, u32[]{:S(2)}) collective-permute-start(bf16[64,2688]{1,0:T(8,128)(2,1)S(1)} %collective-permute-done.3.refs_4_), channel_id=1, source_target_pairs={{0,224},{32,0},{64,32},{96,64},{128,96},{160,128},{192,160},{224,1... | collective-permute-start | bytes 1032200 | tf_op jit(solution)/shard_map/ppermute | solution.py:32
  15.2 0.2 down.1
  15.4 3.1 %collective-permute-start.21 = (bf16[576,384]{1,0:T(8,128)(2,1)S(1)}, bf16[576,384]{1,0:T(8,128)(2,1)S(1)}, u32[]{:S(2)}, u32[]{:S(2)}) collective-permute-start(bf16[576,384]{1,0:T(8,128)(2,1)S(1)} %down.1), channel_id=1, source_target_pairs={{0,2},{16,18},{2,0},{18,16},{1,3},{17,19},{3,1},{19,17},{4,6},{20,... | collective-permute-start | bytes 1327112 | tf_op jit(solution)/shard_map/ppermute | solution.py:24
  18.5 4.2 %collective-permute-done.1.refs_2_ = bf16[64,2688]{1,0:T(8,128)(2,1)S(1)} collective-permute-done((bf16[64,2688]{1,0:T(8,128)(2,1)S(1)}, bf16[64,2688]{1,0:T(8,128)(2,1)S(1)}, u32[]{:S(2)}, u32[]{:S(2)}) %collective-permute-start.1) | collective-permute-done | bytes 344096 | tf_op jit(solution)/shard_map/ppermute | solution.py:32
  22.7 1.5 %collective-permute-start.22 = (bf16[576,384]{1,0:T(8,128)(2,1)S(1)}, bf16[576,384]{1,0:T(8,128)(2,1)S(1)}, u32[]{:S(2)}, u32[]{:S(2)}) collective-permute-start(bf16[576,384]{1,0:T(8,128)(2,1)S(1)} %down.1), channel_id=1, source_target_pairs={{0,16},{16,2},{2,18},{18,0},{1,17},{17,3},{3,19},{19,1},{4,20},{20... | collective-permute-start | bytes 1327112 | tf_op jit(solution)/shard_map/ppermute | solution.py:24
  24.2 1.7 %collective-permute-start.23 = (bf16[576,384]{1,0:T(8,128)(2,1)S(1)}, bf16[576,384]{1,0:T(8,128)(2,1)S(1)}, u32[]{:S(2)}, u32[]{:S(2)}) collective-permute-start(bf16[576,384]{1,0:T(8,128)(2,1)S(1)} %down.1), channel_id=1, source_target_pairs={{0,18},{16,0},{2,16},{18,2},{1,19},{17,1},{3,17},{19,3},{4,22},{20... | collective-permute-start | bytes 1327112 | tf_op jit(solution)/shard_map/ppermute | solution.py:24
  26.0 10.3 %collective-permute-start.2 = (bf16[64,2688]{1,0:T(8,128)(2,1)S(1)}, bf16[64,2688]{1,0:T(8,128)(2,1)S(1)}, u32[]{:S(2)}, u32[]{:S(2)}) collective-permute-start(bf16[64,2688]{1,0:T(8,128)(2,1)S(1)} %collective-permute-done.1.refs_2_), channel_id=1, source_target_pairs={{0,32},{32,64},{64,96},{96,128},{128,160},{160,192},{192,224},{224... | collective-permute-start | bytes 1032200 | tf_op jit(solution)/shard_map/ppermute | solution.py:32
  36.2 1.6 %collective-permute-start.5 = (bf16[64,2688]{1,0:T(8,128)(2,1)S(1)}, bf16[64,2688]{1,0:T(8,128)(2,1)S(1)}, u32[]{:S(2)}, u32[]{:S(2)}) collective-permute-start(bf16[64,2688]{1,0:T(8,128)(2,1)S(1)} %collective-permute-done.4.refs_5_), channel_id=1, source_target_pairs={{0,224},{32,0},{64,32},{96,64},{128,96},{160,128},{192,160},{224,1... | collective-permute-start | bytes 1032200 | tf_op jit(solution)/shard_map/ppermute | solution.py:32
  37.9 1.0 collective-permute-start.10
  38.9 5.5 %collective-permute-done.22 = bf16[576,384]{1,0:T(8,128)(2,1)S(1)} collective-permute-done((bf16[576,384]{1,0:T(8,128)(2,1)S(1)}, bf16[576,384]{1,0:T(8,128)(2,1)S(1)}, u32[]{:S(2)}, u32[]{:S(2)}) %collective-permute-start.22) | collective-permute-done | bytes 442400 | tf_op jit(solution)/shard_map/ppermute | solution.py:24
  44.4 2.0 %collective-permute-start.11 = (bf16[1,72,2688]{2,1,0:T(8,128)(2,1)S(1)}, bf16[1,72,2688]{2,1,0:T(8,128)(2,1)S(1)}, u32[]{:S(2)}, u32[]{:S(2)}) collective-permute-start(bf16[1,72,2688]{2,1,0:T(8,128)(2,1)S(1)} %slice.39), channel_id=1, source_target_pairs={{0,18},{16,0},{2,16},{18,2},{1,19},{17,1},{3,17},{19,3},{4,22},{20... | collective-permute-start | bytes 1161224 | tf_op jit(solution)/shard_map/ppermute | solution.py:24
  46.4 0.3 pad_maximum_fusion.refs_9_
  46.8 2.0 %collective-permute-start.6 = (bf16[32,2688]{1,0:T(8,128)(2,1)S(1)}, bf16[32,2688]{1,0:T(8,128)(2,1)S(1)}, u32[]{:S(2)}, u32[]{:S(2)}) collective-permute-start(bf16[32,2688]{1,0:T(8,128)(2,1)S(1)} %slice.36), channel_id=1, source_target_pairs={{0,32},{32,64},{64,96},{96,128},{128,160},{160,192},{192,224},{224... | collective-permute-start | bytes 516104 | tf_op jit(solution)/shard_map/ppermute | solution.py:32
  48.8 2.4 %collective-permute-start.7 = (bf16[32,2688]{1,0:T(8,128)(2,1)S(1)}, bf16[32,2688]{1,0:T(8,128)(2,1)S(1)}, u32[]{:S(2)}, u32[]{:S(2)}) collective-permute-start(bf16[32,2688]{1,0:T(8,128)(2,1)S(1)} %slice.37), channel_id=1, source_target_pairs={{0,224},{32,0},{64,32},{96,64},{128,96},{160,128},{192,160},{224,1... | collective-permute-start | bytes 516104 | tf_op jit(solution)/shard_map/ppermute | solution.py:32
  51.2 0.5 collective-permute-done.10.refs_12_
  51.8 1.8 %collective-permute-done.11.refs_13_ = bf16[1,72,2688]{2,1,0:T(8,128)(2,1)S(1)} collective-permute-done((bf16[1,72,2688]{2,1,0:T(8,128)(2,1)S(1)}, bf16[1,72,2688]{2,1,0:T(8,128)(2,1)S(1)}, u32[]{:S(2)}, u32[]{:S(2)}) %collective-permute-start.11) | collective-permute-done | bytes 387104 | tf_op jit(solution)/shard_map/ppermute | solution.py:24
  53.5 2.4 %collective-permute-done.6.refs_7_ = bf16[32,2688]{1,0:T(8,128)(2,1)S(1)} collective-permute-done((bf16[32,2688]{1,0:T(8,128)(2,1)S(1)}, bf16[32,2688]{1,0:T(8,128)(2,1)S(1)}, u32[]{:S(2)}, u32[]{:S(2)}) %collective-permute-start.6) | collective-permute-done | bytes 172064 | tf_op jit(solution)/shard_map/ppermute | solution.py:32
  56.0 0.9 collective-permute-done.7.refs_8_
  56.9 2.2 %first.1 = (f32[576,256]{1,0:T(8,128)S(1)}, f32[576,256]{1,0:T(8,128)S(1)}) custom-call(bf16[64,2688]{1,0:T(8,128)(2,1)S(1)} %constant_dynamic-slice_fusion.2.refs_0_, bf16[64,2688]{1,0:T(8,128)(2,1)S(1)} %collective-permute-done.refs_1_, bf16[64,2688]{1,0:T(8,128)(2,1)S(1)} %collective-permute-done.1.refs_2_, ...), custom_call_target="tpu_custom_call" | custom-call | flops 1585446912 | bytes 5849088 | tf_op jit(solution)/shard_map/first/pallas_call | solution.py:183
  59.2 2.0 %collective-permute-done.12 = f32[576,256]{1,0:T(8,128)S(1)} collective-permute-done((f32[576,256]{1,0:T(8,128)S(1)}, f32[576,256]{1,0:T(8,128)S(1)}, u32[]{:S(2)}, u32[]{:S(2)}) %collective-permute-start.12) | collective-permute-done | bytes 589856 | tf_op jit(solution)/shard_map/ppermute | solution.py:36
  61.4 5.7 %collective-permute-start.14 = (bf16[288,256]{1,0:T(8,128)(2,1)S(1)}, bf16[288,256]{1,0:T(8,128)(2,1)S(1)}, u32[]{:S(2)}, u32[]{:S(2)}) collective-permute-start(bf16[288,256]{1,0:T(8,128)(2,1)S(1)} %fusion.refs_0_), channel_id=1, source_target_pairs={{0,64},{32,96},{64,128},{96,160},{128,192},{160,224},{192,0},{224,... | collective-permute-start | bytes 442376 | tf_op jit(solution)/shard_map/ppermute | solution.py:32
  67.1 0.5 collective-permute-start.13
  67.7 1.5 %collective-permute-start.16 = (bf16[288,256]{1,0:T(8,128)(2,1)S(1)}, bf16[288,256]{1,0:T(8,128)(2,1)S(1)}, u32[]{:S(2)}, u32[]{:S(2)}) collective-permute-start(bf16[288,256]{1,0:T(8,128)(2,1)S(1)} %fusion.refs_0_), channel_id=1, source_target_pairs={{0,224},{32,0},{64,32},{96,64},{128,96},{160,128},{192,160},{224,1... | collective-permute-start | bytes 442376 | tf_op jit(solution)/shard_map/ppermute | solution.py:32
  69.2 4.9 %collective-permute-done.14.refs_2_ = bf16[288,256]{1,0:T(8,128)(2,1)S(1)} collective-permute-done((bf16[288,256]{1,0:T(8,128)(2,1)S(1)}, bf16[288,256]{1,0:T(8,128)(2,1)S(1)}, u32[]{:S(2)}, u32[]{:S(2)}) %collective-permute-start.14) | collective-permute-done | bytes 147488 | tf_op jit(solution)/shard_map/ppermute | solution.py:32
  74.1 0.5 collective-permute-start.15
  74.6 2.4 %collective-permute-done.17.refs_5_ = bf16[288,256]{1,0:T(8,128)(2,1)S(1)} collective-permute-done((bf16[288,256]{1,0:T(8,128)(2,1)S(1)}, bf16[288,256]{1,0:T(8,128)(2,1)S(1)}, u32[]{:S(2)}, u32[]{:S(2)}) %collective-permute-start.17) | collective-permute-done | bytes 147488 | tf_op jit(solution)/shard_map/ppermute | solution.py:32
  77.0 3.0 %collective-permute-start.19 = (bf16[144,256]{1,0:T(8,128)(2,1)S(1)}, bf16[144,256]{1,0:T(8,128)(2,1)S(1)}, u32[]{:S(2)}, u32[]{:S(2)}) collective-permute-start(bf16[144,256]{1,0:T(8,128)(2,1)S(1)} %slice.42), channel_id=1, source_target_pairs={{0,64},{32,96},{64,128},{96,160},{128,192},{160,224},{192,0},{224,... | collective-permute-start | bytes 221192 | tf_op jit(solution)/shard_map/ppermute | solution.py:32
  80.0 1.2 %collective-permute-start.20 = (bf16[144,256]{1,0:T(8,128)(2,1)S(1)}, bf16[144,256]{1,0:T(8,128)(2,1)S(1)}, u32[]{:S(2)}, u32[]{:S(2)}) collective-permute-start(bf16[144,256]{1,0:T(8,128)(2,1)S(1)} %slice.43), channel_id=1, source_target_pairs={{0,192},{32,224},{64,0},{96,32},{128,64},{160,96},{192,128},{224,1... | collective-permute-start | bytes 221192 | tf_op jit(solution)/shard_map/ppermute | solution.py:32
  81.3 2.7 %collective-permute-done.19.refs_7_ = bf16[144,256]{1,0:T(8,128)(2,1)S(1)} collective-permute-done((bf16[144,256]{1,0:T(8,128)(2,1)S(1)}, bf16[144,256]{1,0:T(8,128)(2,1)S(1)}, u32[]{:S(2)}, u32[]{:S(2)}) %collective-permute-start.19) | collective-permute-done | bytes 73760 | tf_op jit(solution)/shard_map/ppermute | solution.py:32
  83.9 1.9 %collective-permute-done.20.refs_8_ = bf16[144,256]{1,0:T(8,128)(2,1)S(1)} collective-permute-done((bf16[144,256]{1,0:T(8,128)(2,1)S(1)}, bf16[144,256]{1,0:T(8,128)(2,1)S(1)}, u32[]{:S(2)}, u32[]{:S(2)}) %collective-permute-start.20) | collective-permute-done | bytes 73760 | tf_op jit(solution)/shard_map/ppermute | solution.py:32
  85.9 2.0 %second.1 = (bf16[64,768]{1,0:T(8,128)(2,1)S(1)}, bf16[64,768]{1,0:T(8,128)(2,1)S(1)}, bf16[64,768]{1,0:T(8,128)(2,1)S(1)}, bf16[64,768]{1,0:T(8,128)(2,1)S(1)}) custom-call(bf16[288,256]{1,0:T(8,128)(2,1)S(1)} %fusion.refs_0_, bf16[288,256]{1,0:T(8,128)(2,1)S(1)} %collective-permute-done.13.refs_1_, bf16[288,256]{1,0:T(8,128)(2,1)S(1)} %collective-permute-done.14.refs_2_, ...), custom_call_target="tpu_custom_call" | custom-call | flops 905969664 | bytes 6291456 | tf_op jit(solution)/shard_map/second/pallas_call | solution.py:199
  87.8 0.3 collective-permute-start.25
  88.1 2.6 %collective-permute-start.26 = (bf16[64,768]{1,0:T(8,128)(2,1)S(1)}, bf16[64,768]{1,0:T(8,128)(2,1)S(1)}, u32[]{:S(2)}, u32[]{:S(2)}) collective-permute-start(bf16[64,768]{1,0:T(8,128)(2,1)S(1)} %get-tuple-element.15), channel_id=1, source_target_pairs={{0,8},{4,12},{8,0},{12,4},{1,9},{5,13},{9,1},{13,5},{2,10},{6,14},... | collective-permute-start | bytes 294920 | tf_op jit(solution)/shard_map/ppermute | solution.py:28
  90.7 1.8 %collective-permute-done.25 = bf16[64,768]{1,0:T(8,128)(2,1)S(1)} collective-permute-done((bf16[64,768]{1,0:T(8,128)(2,1)S(1)}, bf16[64,768]{1,0:T(8,128)(2,1)S(1)}, u32[]{:S(2)}, u32[]{:S(2)}) %collective-permute-start.25) | collective-permute-done | bytes 98336 | tf_op jit(solution)/shard_map/ppermute | solution.py:28
  92.5 1.7 %collective-permute-done.26 = bf16[64,768]{1,0:T(8,128)(2,1)S(1)} collective-permute-done((bf16[64,768]{1,0:T(8,128)(2,1)S(1)}, bf16[64,768]{1,0:T(8,128)(2,1)S(1)}, u32[]{:S(2)}, u32[]{:S(2)}) %collective-permute-start.26) | collective-permute-done | bytes 98336 | tf_op jit(solution)/shard_map/ppermute | solution.py:28
  94.3 2.3 %collective-permute-done.27 = bf16[64,768]{1,0:T(8,128)(2,1)S(1)} collective-permute-done((bf16[64,768]{1,0:T(8,128)(2,1)S(1)}, bf16[64,768]{1,0:T(8,128)(2,1)S(1)}, u32[]{:S(2)}, u32[]{:S(2)}) %collective-permute-start.27) | collective-permute-done | bytes 98336 | tf_op jit(solution)/shard_map/ppermute | solution.py:28
  96.6 3.1 %collective-permute-start.28 = (bf16[64,384]{1,0:T(8,128)(2,1)S(1)}, bf16[64,384]{1,0:T(8,128)(2,1)S(1)}, u32[]{:S(2)}, u32[]{:S(2)}) collective-permute-start(bf16[64,384]{1,0:T(8,128)(2,1)S(1)} %get-tuple-element.19), channel_id=1, source_target_pairs={{0,96},{1,128},{2,97},{3,129},{4,64},{5,160},{6,65},{7,161},{8,0},... | collective-permute-start | bytes 147464 | tf_op jit(solution)/shard_map/ppermute | solution.py:213
  99.7 6.2 %collective-permute-done.28 = bf16[64,384]{1,0:T(8,128)(2,1)S(1)} collective-permute-done((bf16[64,384]{1,0:T(8,128)(2,1)S(1)}, bf16[64,384]{1,0:T(8,128)(2,1)S(1)}, u32[]{:S(2)}, u32[]{:S(2)}) %collective-permute-start.28) | collective-permute-done | bytes 49184 | tf_op jit(solution)/shard_map/ppermute | solution.py:213
  105.9 5.4 %collective-permute-done.29 = bf16[64,384]{1,0:T(8,128)(2,1)S(1)} collective-permute-done((bf16[64,384]{1,0:T(8,128)(2,1)S(1)}, bf16[64,384]{1,0:T(8,128)(2,1)S(1)}, u32[]{:S(2)}, u32[]{:S(2)}) %collective-permute-start.29) | collective-permute-done | bytes 49184 | tf_op jit(solution)/shard_map/ppermute | solution.py:213
  111.4 0.7 copy.7
  (35 shorter events, 0.7 us)
Async XLA Ops:
  0.0 1.1 copy-start
  0.0 15.2 %copy-start.1 = (bf16[576,336]{0,1:T(8,128)(2,1)S(1)}, bf16[576,336]{0,1:T(8,128)(2,1)}, u32[]{:S(2)}) copy-start(bf16[576,336]{0,1:T(8,128)(2,1)} %param.7) | copy-start | bytes 1161220
  1.1 9.9 %collective-permute-start = (bf16[64,2688]{1,0:T(8,128)(2,1)S(1)}, bf16[64,2688]{1,0:T(8,128)(2,1)S(1)}, u32[]{:S(2)}, u32[]{:S(2)}) collective-permute-start(bf16[64,2688]{1,0:T(8,128)(2,1)S(1)} %constant_dynamic-slice_fusion.2.refs_0_), channel_id=1, source_target_pairs={{0,32},{32,64},{64,96},{96,128},{128,160},{160,192},{192,224},{224... | collective-permute-start | bytes 1032200 | tf_op jit(solution)/shard_map/ppermute | solution.py:32
  3.1 9.8 %collective-permute-start.3 = (bf16[64,2688]{1,0:T(8,128)(2,1)S(1)}, bf16[64,2688]{1,0:T(8,128)(2,1)S(1)}, u32[]{:S(2)}, u32[]{:S(2)}) collective-permute-start(bf16[64,2688]{1,0:T(8,128)(2,1)S(1)} %constant_dynamic-slice_fusion.2.refs_0_), channel_id=1, source_target_pairs={{0,224},{32,0},{64,32},{96,64},{128,96},{160,128},{192,160},{224,1... | collective-permute-start | bytes 1032200 | tf_op jit(solution)/shard_map/ppermute | solution.py:32
  4.4 21.5 %collective-permute-start.8 = (bf16[2,72,2688]{2,1,0:T(8,128)(2,1)S(1)}, bf16[2,72,2688]{2,1,0:T(8,128)(2,1)S(1)}, u32[]{:S(2)}, u32[]{:S(2)}) collective-permute-start(bf16[2,72,2688]{2,1,0:T(8,128)(2,1)S(1)} %pad_maximum_fusion.1.refs_9_), channel_id=1, source_target_pairs={{0,16},{16,2},{2,18},{18,0},{1,17},{17,3},{3,19},{19,1},{4,20},{20... | collective-permute-start | bytes 2322440 | tf_op jit(solution)/shard_map/ppermute | solution.py:24
  6.0 30.2 %collective-permute-start.9 = (bf16[2,72,2688]{2,1,0:T(8,128)(2,1)S(1)}, bf16[2,72,2688]{2,1,0:T(8,128)(2,1)S(1)}, u32[]{:S(2)}, u32[]{:S(2)}) collective-permute-start(bf16[2,72,2688]{2,1,0:T(8,128)(2,1)S(1)} %pad_maximum_fusion.1.refs_9_), channel_id=1, source_target_pairs={{0,18},{16,0},{2,16},{18,2},{1,19},{17,1},{3,17},{19,3},{4,22},{20... | collective-permute-start | bytes 2322440 | tf_op jit(solution)/shard_map/ppermute | solution.py:24
  11.0 11.7 %collective-permute-start.1 = (bf16[64,2688]{1,0:T(8,128)(2,1)S(1)}, bf16[64,2688]{1,0:T(8,128)(2,1)S(1)}, u32[]{:S(2)}, u32[]{:S(2)}) collective-permute-start(bf16[64,2688]{1,0:T(8,128)(2,1)S(1)} %collective-permute-done.refs_1_), channel_id=1, source_target_pairs={{0,32},{32,64},{64,96},{96,128},{128,160},{160,192},{192,224},{224... | collective-permute-start | bytes 1032200 | tf_op jit(solution)/shard_map/ppermute | solution.py:32
  12.9 11.3 %collective-permute-start.4 = (bf16[64,2688]{1,0:T(8,128)(2,1)S(1)}, bf16[64,2688]{1,0:T(8,128)(2,1)S(1)}, u32[]{:S(2)}, u32[]{:S(2)}) collective-permute-start(bf16[64,2688]{1,0:T(8,128)(2,1)S(1)} %collective-permute-done.3.refs_4_), channel_id=1, source_target_pairs={{0,224},{32,0},{64,32},{96,64},{128,96},{160,128},{192,160},{224,1... | collective-permute-start | bytes 1032200 | tf_op jit(solution)/shard_map/ppermute | solution.py:32
  15.4 22.5 %collective-permute-start.21 = (bf16[576,384]{1,0:T(8,128)(2,1)S(1)}, bf16[576,384]{1,0:T(8,128)(2,1)S(1)}, u32[]{:S(2)}, u32[]{:S(2)}) collective-permute-start(bf16[576,384]{1,0:T(8,128)(2,1)S(1)} %down.1), channel_id=1, source_target_pairs={{0,2},{16,18},{2,0},{18,16},{1,3},{17,19},{3,1},{19,17},{4,6},{20,... | collective-permute-start | bytes 1327112 | tf_op jit(solution)/shard_map/ppermute | solution.py:24
  22.7 21.7 %collective-permute-start.22 = (bf16[576,384]{1,0:T(8,128)(2,1)S(1)}, bf16[576,384]{1,0:T(8,128)(2,1)S(1)}, u32[]{:S(2)}, u32[]{:S(2)}) collective-permute-start(bf16[576,384]{1,0:T(8,128)(2,1)S(1)} %down.1), channel_id=1, source_target_pairs={{0,16},{16,2},{2,18},{18,0},{1,17},{17,3},{3,19},{19,1},{4,20},{20... | collective-permute-start | bytes 1327112 | tf_op jit(solution)/shard_map/ppermute | solution.py:24
  24.2 22.2 %collective-permute-start.23 = (bf16[576,384]{1,0:T(8,128)(2,1)S(1)}, bf16[576,384]{1,0:T(8,128)(2,1)S(1)}, u32[]{:S(2)}, u32[]{:S(2)}) collective-permute-start(bf16[576,384]{1,0:T(8,128)(2,1)S(1)} %down.1), channel_id=1, source_target_pairs={{0,18},{16,0},{2,16},{18,2},{1,19},{17,1},{3,17},{19,3},{4,22},{20... | collective-permute-start | bytes 1327112 | tf_op jit(solution)/shard_map/ppermute | solution.py:24
  26.0 20.8 %collective-permute-start.2 = (bf16[64,2688]{1,0:T(8,128)(2,1)S(1)}, bf16[64,2688]{1,0:T(8,128)(2,1)S(1)}, u32[]{:S(2)}, u32[]{:S(2)}) collective-permute-start(bf16[64,2688]{1,0:T(8,128)(2,1)S(1)} %collective-permute-done.1.refs_2_), channel_id=1, source_target_pairs={{0,32},{32,64},{64,96},{96,128},{128,160},{160,192},{192,224},{224... | collective-permute-start | bytes 1032200 | tf_op jit(solution)/shard_map/ppermute | solution.py:32
  36.2 12.6 %collective-permute-start.5 = (bf16[64,2688]{1,0:T(8,128)(2,1)S(1)}, bf16[64,2688]{1,0:T(8,128)(2,1)S(1)}, u32[]{:S(2)}, u32[]{:S(2)}) collective-permute-start(bf16[64,2688]{1,0:T(8,128)(2,1)S(1)} %collective-permute-done.4.refs_5_), channel_id=1, source_target_pairs={{0,224},{32,0},{64,32},{96,64},{128,96},{160,128},{192,160},{224,1... | collective-permute-start | bytes 1032200 | tf_op jit(solution)/shard_map/ppermute | solution.py:32
  37.9 13.8 %collective-permute-start.10 = (bf16[1,72,2688]{2,1,0:T(8,128)(2,1)S(1)}, bf16[1,72,2688]{2,1,0:T(8,128)(2,1)S(1)}, u32[]{:S(2)}, u32[]{:S(2)}) collective-permute-start(bf16[1,72,2688]{2,1,0:T(8,128)(2,1)S(1)} %slice.38), channel_id=1, source_target_pairs={{0,16},{16,2},{2,18},{18,0},{1,17},{17,3},{3,19},{19,1},{4,20},{20... | collective-permute-start | bytes 1161224 | tf_op jit(solution)/shard_map/ppermute | solution.py:24
  44.4 9.2 %collective-permute-start.11 = (bf16[1,72,2688]{2,1,0:T(8,128)(2,1)S(1)}, bf16[1,72,2688]{2,1,0:T(8,128)(2,1)S(1)}, u32[]{:S(2)}, u32[]{:S(2)}) collective-permute-start(bf16[1,72,2688]{2,1,0:T(8,128)(2,1)S(1)} %slice.39), channel_id=1, source_target_pairs={{0,18},{16,0},{2,16},{18,2},{1,19},{17,1},{3,17},{19,3},{4,22},{20... | collective-permute-start | bytes 1161224 | tf_op jit(solution)/shard_map/ppermute | solution.py:24
  46.7 39.2 %collective-permute-start.24 = (bf16[4,576,384]{2,1,0:T(8,128)(2,1)S(1)}, bf16[4,576,384]{2,1,0:T(8,128)(2,1)S(1)}, u32[]{:S(2)}, u32[]{:S(2)}) collective-permute-start(bf16[4,576,384]{2,1,0:T(8,128)(2,1)S(1)} %pad_maximum_fusion.refs_9_), channel_id=1, source_target_pairs={{0,1},{1,0},{2,3},{3,2},{4,5},{5,4},{6,7},{7,6},{8,9},{9,8},{10,11... | collective-permute-start | bytes 5308424 | tf_op jit(solution)/shard_map/ppermute | solution.py:36
  46.8 9.1 %collective-permute-start.6 = (bf16[32,2688]{1,0:T(8,128)(2,1)S(1)}, bf16[32,2688]{1,0:T(8,128)(2,1)S(1)}, u32[]{:S(2)}, u32[]{:S(2)}) collective-permute-start(bf16[32,2688]{1,0:T(8,128)(2,1)S(1)} %slice.36), channel_id=1, source_target_pairs={{0,32},{32,64},{64,96},{96,128},{128,160},{160,192},{192,224},{224... | collective-permute-start | bytes 516104 | tf_op jit(solution)/shard_map/ppermute | solution.py:32
  48.8 8.0 %collective-permute-start.7 = (bf16[32,2688]{1,0:T(8,128)(2,1)S(1)}, bf16[32,2688]{1,0:T(8,128)(2,1)S(1)}, u32[]{:S(2)}, u32[]{:S(2)}) collective-permute-start(bf16[32,2688]{1,0:T(8,128)(2,1)S(1)} %slice.37), channel_id=1, source_target_pairs={{0,224},{32,0},{64,32},{96,64},{128,96},{160,128},{192,160},{224,1... | collective-permute-start | bytes 516104 | tf_op jit(solution)/shard_map/ppermute | solution.py:32
  59.1 2.1 %collective-permute-start.12 = (f32[576,256]{1,0:T(8,128)S(1)}, f32[576,256]{1,0:T(8,128)S(1)}, u32[]{:S(2)}, u32[]{:S(2)}) collective-permute-start(f32[576,256]{1,0:T(8,128)S(1)} %get-tuple-element.12), channel_id=1, source_target_pairs={{0,1},{1,0},{2,3},{3,2},{4,5},{5,4},{6,7},{7,6},{8,9},{9,8},{10,11... | collective-permute-start | bytes 1769480 | tf_op jit(solution)/shard_map/ppermute | solution.py:36
  61.4 12.7 %collective-permute-start.14 = (bf16[288,256]{1,0:T(8,128)(2,1)S(1)}, bf16[288,256]{1,0:T(8,128)(2,1)S(1)}, u32[]{:S(2)}, u32[]{:S(2)}) collective-permute-start(bf16[288,256]{1,0:T(8,128)(2,1)S(1)} %fusion.refs_0_), channel_id=1, source_target_pairs={{0,64},{32,96},{64,128},{96,160},{128,192},{160,224},{192,0},{224,... | collective-permute-start | bytes 442376 | tf_op jit(solution)/shard_map/ppermute | solution.py:32
  67.1 9.9 %collective-permute-start.17 = (bf16[288,256]{1,0:T(8,128)(2,1)S(1)}, bf16[288,256]{1,0:T(8,128)(2,1)S(1)}, u32[]{:S(2)}, u32[]{:S(2)}) collective-permute-start(bf16[288,256]{1,0:T(8,128)(2,1)S(1)} %fusion.refs_0_), channel_id=1, source_target_pairs={{0,192},{32,224},{64,0},{96,32},{128,64},{160,96},{192,128},{224,1... | collective-permute-start | bytes 442376 | tf_op jit(solution)/shard_map/ppermute | solution.py:32
  67.1 9.9 %collective-permute-start.13 = (bf16[288,256]{1,0:T(8,128)(2,1)S(1)}, bf16[288,256]{1,0:T(8,128)(2,1)S(1)}, u32[]{:S(2)}, u32[]{:S(2)}) collective-permute-start(bf16[288,256]{1,0:T(8,128)(2,1)S(1)} %fusion.refs_0_), channel_id=1, source_target_pairs={{0,32},{32,64},{64,96},{96,128},{128,160},{160,192},{192,224},{224... | collective-permute-start | bytes 442376 | tf_op jit(solution)/shard_map/ppermute | solution.py:32
  67.7 12.4 %collective-permute-start.16 = (bf16[288,256]{1,0:T(8,128)(2,1)S(1)}, bf16[288,256]{1,0:T(8,128)(2,1)S(1)}, u32[]{:S(2)}, u32[]{:S(2)}) collective-permute-start(bf16[288,256]{1,0:T(8,128)(2,1)S(1)} %fusion.refs_0_), channel_id=1, source_target_pairs={{0,224},{32,0},{64,32},{96,64},{128,96},{160,128},{192,160},{224,1... | collective-permute-start | bytes 442376 | tf_op jit(solution)/shard_map/ppermute | solution.py:32
  74.1 11.8 %collective-permute-start.15 = (bf16[288,256]{1,0:T(8,128)(2,1)S(1)}, bf16[288,256]{1,0:T(8,128)(2,1)S(1)}, u32[]{:S(2)}, u32[]{:S(2)}) collective-permute-start(bf16[288,256]{1,0:T(8,128)(2,1)S(1)} %collective-permute-done.14.refs_2_), channel_id=1, source_target_pairs={{0,32},{32,64},{64,96},{96,128},{128,160},{160,192},{192,224},{224... | collective-permute-start | bytes 442376 | tf_op jit(solution)/shard_map/ppermute | solution.py:32
  77.0 8.8 %collective-permute-start.18 = (bf16[288,256]{1,0:T(8,128)(2,1)S(1)}, bf16[288,256]{1,0:T(8,128)(2,1)S(1)}, u32[]{:S(2)}, u32[]{:S(2)}) collective-permute-start(bf16[288,256]{1,0:T(8,128)(2,1)S(1)} %collective-permute-done.17.refs_5_), channel_id=1, source_target_pairs={{0,224},{32,0},{64,32},{96,64},{128,96},{160,128},{192,160},{224,1... | collective-permute-start | bytes 442376 | tf_op jit(solution)/shard_map/ppermute | solution.py:32
  77.0 6.9 %collective-permute-start.19 = (bf16[144,256]{1,0:T(8,128)(2,1)S(1)}, bf16[144,256]{1,0:T(8,128)(2,1)S(1)}, u32[]{:S(2)}, u32[]{:S(2)}) collective-permute-start(bf16[144,256]{1,0:T(8,128)(2,1)S(1)} %slice.42), channel_id=1, source_target_pairs={{0,64},{32,96},{64,128},{96,160},{128,192},{160,224},{192,0},{224,... | collective-permute-start | bytes 221192 | tf_op jit(solution)/shard_map/ppermute | solution.py:32
  80.0 5.8 %collective-permute-start.20 = (bf16[144,256]{1,0:T(8,128)(2,1)S(1)}, bf16[144,256]{1,0:T(8,128)(2,1)S(1)}, u32[]{:S(2)}, u32[]{:S(2)}) collective-permute-start(bf16[144,256]{1,0:T(8,128)(2,1)S(1)} %slice.43), channel_id=1, source_target_pairs={{0,192},{32,224},{64,0},{96,32},{128,64},{160,96},{192,128},{224,1... | collective-permute-start | bytes 221192 | tf_op jit(solution)/shard_map/ppermute | solution.py:32
  87.8 4.7 %collective-permute-start.25 = (bf16[64,768]{1,0:T(8,128)(2,1)S(1)}, bf16[64,768]{1,0:T(8,128)(2,1)S(1)}, u32[]{:S(2)}, u32[]{:S(2)}) collective-permute-start(bf16[64,768]{1,0:T(8,128)(2,1)S(1)} %get-tuple-element.14), channel_id=1, source_target_pairs={{0,4},{4,8},{8,12},{12,0},{1,5},{5,9},{9,13},{13,1},{2,6},{6,10},{... | collective-permute-start | bytes 294920 | tf_op jit(solution)/shard_map/ppermute | solution.py:28
  88.1 6.1 %collective-permute-start.26 = (bf16[64,768]{1,0:T(8,128)(2,1)S(1)}, bf16[64,768]{1,0:T(8,128)(2,1)S(1)}, u32[]{:S(2)}, u32[]{:S(2)}) collective-permute-start(bf16[64,768]{1,0:T(8,128)(2,1)S(1)} %get-tuple-element.15), channel_id=1, source_target_pairs={{0,8},{4,12},{8,0},{12,4},{1,9},{5,13},{9,1},{13,5},{2,10},{6,14},... | collective-permute-start | bytes 294920 | tf_op jit(solution)/shard_map/ppermute | solution.py:28
  90.7 5.8 %collective-permute-start.27 = (bf16[64,768]{1,0:T(8,128)(2,1)S(1)}, bf16[64,768]{1,0:T(8,128)(2,1)S(1)}, u32[]{:S(2)}, u32[]{:S(2)}) collective-permute-start(bf16[64,768]{1,0:T(8,128)(2,1)S(1)} %get-tuple-element.16), channel_id=1, source_target_pairs={{0,12},{4,0},{8,4},{12,8},{1,13},{5,1},{9,5},{13,9},{2,14},{6,2},{... | collective-permute-start | bytes 294920 | tf_op jit(solution)/shard_map/ppermute | solution.py:28
  96.6 9.3 %collective-permute-start.28 = (bf16[64,384]{1,0:T(8,128)(2,1)S(1)}, bf16[64,384]{1,0:T(8,128)(2,1)S(1)}, u32[]{:S(2)}, u32[]{:S(2)}) collective-permute-start(bf16[64,384]{1,0:T(8,128)(2,1)S(1)} %get-tuple-element.19), channel_id=1, source_target_pairs={{0,96},{1,128},{2,97},{3,129},{4,64},{5,160},{6,65},{7,161},{8,0},... | collective-permute-start | bytes 147464 | tf_op jit(solution)/shard_map/ppermute | solution.py:213
  99.7 11.6 %collective-permute-start.29 = (bf16[64,384]{1,0:T(8,128)(2,1)S(1)}, bf16[64,384]{1,0:T(8,128)(2,1)S(1)}, u32[]{:S(2)}, u32[]{:S(2)}) collective-permute-start(bf16[64,384]{1,0:T(8,128)(2,1)S(1)} %get-tuple-element.20), channel_id=1, source_target_pairs={{0,97},{1,129},{2,96},{3,128},{4,65},{5,161},{6,64},{7,160},{8,1},... | collective-permute-start | bytes 147464 | tf_op jit(solution)/shard_map/ppermute | solution.py:213

commit v3 on v2

--- a/solution.py
+++ b/solution.py
@@ -84,15 +84,26 @@
 
 def first_kernel(*refs):
     blocks, (u4, d4), weights = refs[:7], refs[7:9], refs[9:14]
-    keep, send, tok, wts = refs[14:]
+    send, tok, wts, far_tok = refs[14:]
     z, xl, c, xh = (lax.axis_index(a) for a in ("z", "xl", "c", "xh"))
     n, units = blocks[0].shape[0], weights[3].shape[1]
+
+    def put(off, lo, rows):
+        half, at = place(z, c, off)
+        at = pl.multiple_of(at * n + lo, n // 2)
+
+        @pl.when(half == 0)
+        def _():
+            tok[pl.ds(at, rows.shape[0]), :] = rows[...]
+
+        @pl.when(half != 0)
+        def _():
+            far_tok[pl.ds(at, rows.shape[0]), :] = rows[...]
+
     for block, off in zip(blocks, OFFSETS):
-        half, at = place(z, c, off)
-        tok[pl.ds(pl.multiple_of((half * 4 + at) * n, n), n), :] = block[...]
-    half, at = place(z, c, 4)
+        put(off, 0, block)
     for i, part in enumerate((u4, d4)):
-        tok[pl.ds(pl.multiple_of((half * 4 + at) * n + i * n // 2, n // 2), n // 2), :] = part[...]
+        put(4, i * n // 2, part)
     w, w_m1, w_p1, g2, u2 = weights
     for (gate, up), off in zip(((w.at[0], w.at[1]), (w_m1.at[0], w_m1.at[1]), (w_p1.at[0], w_p1.at[1]), (g2.at[0], u2.at[0])),
                                (0, -1, 1, 2)):
@@ -100,10 +111,12 @@
         dst = (src // 2 ^ xh) * 2 + lax.rem(src, 2)
         wts[dst, :units, :] = gate[...]
         wts[dst, units:, :] = up[...]
-    flat = wts[...].reshape(8 * units, wts.shape[2])
-    for out, lo in ((send, 4 * n), (keep, 0)):
-        out[...] = lax.dot_general(flat, tok[lo:lo + 4 * n, :], (((1,), (1,)), ((), ())),
-                                   preferred_element_type=jnp.float32)
+    half_product(far_tok, wts, send)
+
+
+def half_product(tok, wts, out):
+    flat = wts[...].reshape(out.shape[0], wts.shape[2])
+    out[...] = lax.dot_general(flat, tok[...], (((1,), (1,)), ((), ())), preferred_element_type=jnp.float32)
 
 
 def second_kernel(*refs):
@@ -180,16 +193,25 @@
 
         m, t = 8 * units, Z * n
         half = jax.ShapeDtypeStruct((m, t // 2), jnp.float32)
-        keep, send = pl.pallas_call(
+        send, tok, wts = pl.pallas_call(
             first_kernel,
-            out_shape=(half, half),
+            out_shape=(half, jax.ShapeDtypeStruct((t // 2, k), bf16), jax.ShapeDtypeStruct((4, 2 * units, k), bf16)),
             in_specs=[VMEM] * 14,
-            out_specs=(VMEM, VMEM),
-            scratch_shapes=[pltpu.VMEM((t, k), bf16), pltpu.VMEM((4, 2 * units, k), bf16)],
+            out_specs=(VMEM,) * 3,
+            scratch_shapes=[pltpu.VMEM((t // 2, k), bf16)],
             compiler_params=pltpu.CompilerParams(vmem_limit_bytes=12 << 20),
-            cost_estimate=pl.CostEstimate(flops=2 * m * t * k, bytes_accessed=2 * k * (m + t), transcendentals=0),
+            cost_estimate=pl.CostEstimate(flops=m * t * k, bytes_accessed=2 * k * (m + t), transcendentals=0),
             name="first",
         )(*toks, *weights)
+        keep = pl.pallas_call(
+            half_product,
+            out_shape=half,
+            in_specs=[VMEM] * 2,
+            out_specs=VMEM,
+            compiler_params=pltpu.CompilerParams(vmem_limit_bytes=8 << 20),
+            cost_estimate=pl.CostEstimate(flops=m * t * k, bytes_accessed=2 * k * (m + t), transcendentals=0),
+            name="keep",
+        )(tok, wts)
         whole = (keep + core_swap(send)).reshape(4, 2, units, t // 2)
         g, u = whole[:, 0], whole[:, 1]
         hidden = (jax.nn.silu(g) * u).astype(bf16).reshape(4 * units, t // 2)

time: 112 us -> 111 us (level)
    pallas_call x1 -> x2, Pallas kernels: 2.25 us -> 2.56 us  [the longest x1 1.52 us: body(): pl.pallas_call(first_kernel, out_shape=(half, jax.ShapeDtypeStruct((t //...]
where the time goes in v3:
time: 111 us
  starting transfers between devices  53.9 us (49%)
  waiting for transfers between devices  48.9 us (44%)
  Pallas kernels  4.69 us (4%)
  local copies, waits for them, and re-layouts  2.03 us (2%)
  other arithmetic  1.71 us (2%)
    ppermute x16, starting transfers between devices, pz(): return lax.ppermute(v, 'z', ring(Z, k))  35.1 us
    ppermute x16, waiting for transfers between devices, pz(): return lax.ppermute(v, 'z', ring(Z, k))  22.7 us
    ppermute x7, starting transfers between devices, px(): return lax.ppermute(v, ('xl', 'xh'), x_ring(k))  12.7 us
    ppermute x7, waiting for transfers between devices, px(): return lax.ppermute(v, ('xl', 'xh'), x_ring(k))  7.82 us
    ppermute x1, waiting for transfers between devices, body(): lax.ppermute(mine, final_axes, final_perms[0])  6.21 us
    ppermute x3, waiting for transfers between devices, py(): return lax.ppermute(v, 'y', ring(Y, k))  5.82 us
    ppermute x1, waiting for transfers between devices, body(): lax.ppermute(other, final_axes, final_perms[1])  5.4 us
    ppermute x1, starting transfers between devices, body(): lax.ppermute(mine, final_axes, final_perms[0])  3.08 us
  transfers between devices with their start and end apart: 30, of which 17 were waited for; matrix products, arithmetic and copies ran while one was open for 2% of the time, Pallas kernels for 2%

profile of v3, /device:TPU:56, one launch (start us, length us, event | category | flops | bytes accessed | tf_op | source)
XLA Modules:
  0.0 111.4 jit_solution(11213925189582206521)
XLA Ops:
  0.0 1.1 copy-done
  1.1 2.0 %collective-permute-start = (bf16[64,2688]{1,0:T(8,128)(2,1)S(1)}, bf16[64,2688]{1,0:T(8,128)(2,1)S(1)}, u32[]{:S(2)}, u32[]{:S(2)}) collective-permute-start(bf16[64,2688]{1,0:T(8,128)(2,1)S(1)} %constant_dynamic-slice_fusion.2.refs_0_), channel_id=1, source_target_pairs={{0,32},{32,64},{64,96},{96,128},{128,160},{160,192},{192,224},{224... | collective-permute-start | bytes 1032200 | tf_op jit(solution)/shard_map/ppermute | solution.py:32
  3.2 1.2 %pad_maximum_fusion.1.refs_9_ = bf16[2,72,2688]{2,1,0:T(8,128)(2,1)S(1)} fusion(bf16[1,72,2688]{2,1,0:T(8,128)(2,1)} %bitcast.35, bf16[1,72,2688]{2,1,0:T(8,128)(2,1)} %bitcast.36), kind=kLoop, calls=%fused_computation.1 | loop fusion | flops 387072 | bytes 1548288 | tf_op jit(solution)/shard_map/stack | solution.py:177
  4.4 1.6 %collective-permute-start.8 = (bf16[2,72,2688]{2,1,0:T(8,128)(2,1)S(1)}, bf16[2,72,2688]{2,1,0:T(8,128)(2,1)S(1)}, u32[]{:S(2)}, u32[]{:S(2)}) collective-permute-start(bf16[2,72,2688]{2,1,0:T(8,128)(2,1)S(1)} %pad_maximum_fusion.1.refs_9_), channel_id=1, source_target_pairs={{0,16},{16,2},{2,18},{18,0},{1,17},{17,3},{3,19},{19,1},{4,20},{20... | collective-permute-start | bytes 2322440 | tf_op jit(solution)/shard_map/ppermute | solution.py:24
  6.0 1.7 %collective-permute-start.9 = (bf16[2,72,2688]{2,1,0:T(8,128)(2,1)S(1)}, bf16[2,72,2688]{2,1,0:T(8,128)(2,1)S(1)}, u32[]{:S(2)}, u32[]{:S(2)}) collective-permute-start(bf16[2,72,2688]{2,1,0:T(8,128)(2,1)S(1)} %pad_maximum_fusion.1.refs_9_), channel_id=1, source_target_pairs={{0,18},{16,0},{2,16},{18,2},{1,19},{17,1},{3,17},{19,3},{4,22},{20... | collective-permute-start | bytes 2322440 | tf_op jit(solution)/shard_map/ppermute | solution.py:24
  7.7 3.3 %collective-permute-done.refs_1_ = bf16[64,2688]{1,0:T(8,128)(2,1)S(1)} collective-permute-done((bf16[64,2688]{1,0:T(8,128)(2,1)S(1)}, bf16[64,2688]{1,0:T(8,128)(2,1)S(1)}, u32[]{:S(2)}, u32[]{:S(2)}) %collective-permute-start) | collective-permute-done | bytes 344096 | tf_op jit(solution)/shard_map/ppermute | solution.py:32
  11.0 1.9 %collective-permute-start.1 = (bf16[64,2688]{1,0:T(8,128)(2,1)S(1)}, bf16[64,2688]{1,0:T(8,128)(2,1)S(1)}, u32[]{:S(2)}, u32[]{:S(2)}) collective-permute-start(bf16[64,2688]{1,0:T(8,128)(2,1)S(1)} %collective-permute-done.refs_1_), channel_id=1, source_target_pairs={{0,32},{32,64},{64,96},{96,128},{128,160},{160,192},{192,224},{224... | collective-permute-start | bytes 1032200 | tf_op jit(solution)/shard_map/ppermute | solution.py:32
  12.9 2.3 %collective-permute-start.4 = (bf16[64,2688]{1,0:T(8,128)(2,1)S(1)}, bf16[64,2688]{1,0:T(8,128)(2,1)S(1)}, u32[]{:S(2)}, u32[]{:S(2)}) collective-permute-start(bf16[64,2688]{1,0:T(8,128)(2,1)S(1)} %collective-permute-done.3.refs_4_), channel_id=1, source_target_pairs={{0,224},{32,0},{64,32},{96,64},{128,96},{160,128},{192,160},{224,1... | collective-permute-start | bytes 1032200 | tf_op jit(solution)/shard_map/ppermute | solution.py:32
  15.2 0.2 down.1
  15.4 3.1 %collective-permute-start.21 = (bf16[576,384]{1,0:T(8,128)(2,1)S(1)}, bf16[576,384]{1,0:T(8,128)(2,1)S(1)}, u32[]{:S(2)}, u32[]{:S(2)}) collective-permute-start(bf16[576,384]{1,0:T(8,128)(2,1)S(1)} %down.1), channel_id=1, source_target_pairs={{0,2},{16,18},{2,0},{18,16},{1,3},{17,19},{3,1},{19,17},{4,6},{20,... | collective-permute-start | bytes 1327112 | tf_op jit(solution)/shard_map/ppermute | solution.py:24
  18.5 4.2 %collective-permute-done.1.refs_2_ = bf16[64,2688]{1,0:T(8,128)(2,1)S(1)} collective-permute-done((bf16[64,2688]{1,0:T(8,128)(2,1)S(1)}, bf16[64,2688]{1,0:T(8,128)(2,1)S(1)}, u32[]{:S(2)}, u32[]{:S(2)}) %collective-permute-start.1) | collective-permute-done | bytes 344096 | tf_op jit(solution)/shard_map/ppermute | solution.py:32
  22.7 1.5 %collective-permute-start.22 = (bf16[576,384]{1,0:T(8,128)(2,1)S(1)}, bf16[576,384]{1,0:T(8,128)(2,1)S(1)}, u32[]{:S(2)}, u32[]{:S(2)}) collective-permute-start(bf16[576,384]{1,0:T(8,128)(2,1)S(1)} %down.1), channel_id=1, source_target_pairs={{0,16},{16,2},{2,18},{18,0},{1,17},{17,3},{3,19},{19,1},{4,20},{20... | collective-permute-start | bytes 1327112 | tf_op jit(solution)/shard_map/ppermute | solution.py:24
  24.2 1.7 %collective-permute-start.23 = (bf16[576,384]{1,0:T(8,128)(2,1)S(1)}, bf16[576,384]{1,0:T(8,128)(2,1)S(1)}, u32[]{:S(2)}, u32[]{:S(2)}) collective-permute-start(bf16[576,384]{1,0:T(8,128)(2,1)S(1)} %down.1), channel_id=1, source_target_pairs={{0,18},{16,0},{2,16},{18,2},{1,19},{17,1},{3,17},{19,3},{4,22},{20... | collective-permute-start | bytes 1327112 | tf_op jit(solution)/shard_map/ppermute | solution.py:24
  26.0 10.3 %collective-permute-start.2 = (bf16[64,2688]{1,0:T(8,128)(2,1)S(1)}, bf16[64,2688]{1,0:T(8,128)(2,1)S(1)}, u32[]{:S(2)}, u32[]{:S(2)}) collective-permute-start(bf16[64,2688]{1,0:T(8,128)(2,1)S(1)} %collective-permute-done.1.refs_2_), channel_id=1, source_target_pairs={{0,32},{32,64},{64,96},{96,128},{128,160},{160,192},{192,224},{224... | collective-permute-start | bytes 1032200 | tf_op jit(solution)/shard_map/ppermute | solution.py:32
  36.2 1.6 %collective-permute-start.5 = (bf16[64,2688]{1,0:T(8,128)(2,1)S(1)}, bf16[64,2688]{1,0:T(8,128)(2,1)S(1)}, u32[]{:S(2)}, u32[]{:S(2)}) collective-permute-start(bf16[64,2688]{1,0:T(8,128)(2,1)S(1)} %collective-permute-done.4.refs_5_), channel_id=1, source_target_pairs={{0,224},{32,0},{64,32},{96,64},{128,96},{160,128},{192,160},{224,1... | collective-permute-start | bytes 1032200 | tf_op jit(solution)/shard_map/ppermute | solution.py:32
  37.9 1.0 collective-permute-start.10
  38.9 5.5 %collective-permute-done.22 = bf16[576,384]{1,0:T(8,128)(2,1)S(1)} collective-permute-done((bf16[576,384]{1,0:T(8,128)(2,1)S(1)}, bf16[576,384]{1,0:T(8,128)(2,1)S(1)}, u32[]{:S(2)}, u32[]{:S(2)}) %collective-permute-start.22) | collective-permute-done | bytes 442400 | tf_op jit(solution)/shard_map/ppermute | solution.py:24
  44.4 2.0 %collective-permute-start.11 = (bf16[1,72,2688]{2,1,0:T(8,128)(2,1)S(1)}, bf16[1,72,2688]{2,1,0:T(8,128)(2,1)S(1)}, u32[]{:S(2)}, u32[]{:S(2)}) collective-permute-start(bf16[1,72,2688]{2,1,0:T(8,128)(2,1)S(1)} %slice.39), channel_id=1, source_target_pairs={{0,18},{16,0},{2,16},{18,2},{1,19},{17,1},{3,17},{19,3},{4,22},{20... | collective-permute-start | bytes 1161224 | tf_op jit(solution)/shard_map/ppermute | solution.py:24
  46.4 0.3 pad_maximum_fusion.refs_9_
  46.8 2.0 %collective-permute-start.6 = (bf16[32,2688]{1,0:T(8,128)(2,1)S(1)}, bf16[32,2688]{1,0:T(8,128)(2,1)S(1)}, u32[]{:S(2)}, u32[]{:S(2)}) collective-permute-start(bf16[32,2688]{1,0:T(8,128)(2,1)S(1)} %slice.36), channel_id=1, source_target_pairs={{0,32},{32,64},{64,96},{96,128},{128,160},{160,192},{192,224},{224... | collective-permute-start | bytes 516104 | tf_op jit(solution)/shard_map/ppermute | solution.py:32
  48.8 2.4 %collective-permute-start.7 = (bf16[32,2688]{1,0:T(8,128)(2,1)S(1)}, bf16[32,2688]{1,0:T(8,128)(2,1)S(1)}, u32[]{:S(2)}, u32[]{:S(2)}) collective-permute-start(bf16[32,2688]{1,0:T(8,128)(2,1)S(1)} %slice.37), channel_id=1, source_target_pairs={{0,224},{32,0},{64,32},{96,64},{128,96},{160,128},{192,160},{224,1... | collective-permute-start | bytes 516104 | tf_op jit(solution)/shard_map/ppermute | solution.py:32
  51.2 0.5 collective-permute-done.10.refs_12_
  51.8 1.8 %collective-permute-done.11.refs_13_ = bf16[1,72,2688]{2,1,0:T(8,128)(2,1)S(1)} collective-permute-done((bf16[1,72,2688]{2,1,0:T(8,128)(2,1)S(1)}, bf16[1,72,2688]{2,1,0:T(8,128)(2,1)S(1)}, u32[]{:S(2)}, u32[]{:S(2)}) %collective-permute-start.11) | collective-permute-done | bytes 387104 | tf_op jit(solution)/shard_map/ppermute | solution.py:24
  53.5 2.4 %collective-permute-done.6.refs_7_ = bf16[32,2688]{1,0:T(8,128)(2,1)S(1)} collective-permute-done((bf16[32,2688]{1,0:T(8,128)(2,1)S(1)}, bf16[32,2688]{1,0:T(8,128)(2,1)S(1)}, u32[]{:S(2)}, u32[]{:S(2)}) %collective-permute-start.6) | collective-permute-done | bytes 172064 | tf_op jit(solution)/shard_map/ppermute | solution.py:32
  56.0 0.9 collective-permute-done.7.refs_8_
  56.9 1.5 %first.1 = (f32[576,256]{1,0:T(8,128)S(1)}, bf16[256,2688]{1,0:T(8,128)(2,1)S(1)}, bf16[4,144,2688]{2,1,0:T(8,128)(2,1)S(1)}) custom-call(bf16[64,2688]{1,0:T(8,128)(2,1)S(1)} %constant_dynamic-slice_fusion.2.refs_0_, bf16[64,2688]{1,0:T(8,128)(2,1)S(1)} %collective-permute-done.refs_1_, bf16[64,2688]{1,0:T(8,128)(2,1)S(1)} %collective-permute-done.1.refs_2_, ...), custom_call_target="tpu_custom_call" | custom-call | flops 792723456 | bytes 5849088 | tf_op jit(solution)/shard_map/first/pallas_call | solution.py:196
  58.5 1.0 keep.1
  59.5 1.0 collective-permute-done.12
  60.7 5.7 %collective-permute-start.14 = (bf16[288,256]{1,0:T(8,128)(2,1)S(1)}, bf16[288,256]{1,0:T(8,128)(2,1)S(1)}, u32[]{:S(2)}, u32[]{:S(2)}) collective-permute-start(bf16[288,256]{1,0:T(8,128)(2,1)S(1)} %fusion.refs_0_), channel_id=1, source_target_pairs={{0,64},{32,96},{64,128},{96,160},{128,192},{160,224},{192,0},{224,... | collective-permute-start | bytes 442376 | tf_op jit(solution)/shard_map/ppermute | solution.py:32
  66.4 0.5 collective-permute-start.13
  67.0 1.5 %collective-permute-start.16 = (bf16[288,256]{1,0:T(8,128)(2,1)S(1)}, bf16[288,256]{1,0:T(8,128)(2,1)S(1)}, u32[]{:S(2)}, u32[]{:S(2)}) collective-permute-start(bf16[288,256]{1,0:T(8,128)(2,1)S(1)} %fusion.refs_0_), channel_id=1, source_target_pairs={{0,224},{32,0},{64,32},{96,64},{128,96},{160,128},{192,160},{224,1... | collective-permute-start | bytes 442376 | tf_op jit(solution)/shard_map/ppermute | solution.py:32
  68.5 4.9 %collective-permute-done.14.refs_2_ = bf16[288,256]{1,0:T(8,128)(2,1)S(1)} collective-permute-done((bf16[288,256]{1,0:T(8,128)(2,1)S(1)}, bf16[288,256]{1,0:T(8,128)(2,1)S(1)}, u32[]{:S(2)}, u32[]{:S(2)}) %collective-permute-start.14) | collective-permute-done | bytes 147488 | tf_op jit(solution)/shard_map/ppermute | solution.py:32
  73.4 0.5 collective-permute-start.15
  73.9 2.4 %collective-permute-done.17.refs_5_ = bf16[288,256]{1,0:T(8,128)(2,1)S(1)} collective-permute-done((bf16[288,256]{1,0:T(8,128)(2,1)S(1)}, bf16[288,256]{1,0:T(8,128)(2,1)S(1)}, u32[]{:S(2)}, u32[]{:S(2)}) %collective-permute-start.17) | collective-permute-done | bytes 147488 | tf_op jit(solution)/shard_map/ppermute | solution.py:32
  76.3 3.0 %collective-permute-start.19 = (bf16[144,256]{1,0:T(8,128)(2,1)S(1)}, bf16[144,256]{1,0:T(8,128)(2,1)S(1)}, u32[]{:S(2)}, u32[]{:S(2)}) collective-permute-start(bf16[144,256]{1,0:T(8,128)(2,1)S(1)} %slice.42), channel_id=1, source_target_pairs={{0,64},{32,96},{64,128},{96,160},{128,192},{160,224},{192,0},{224,... | collective-permute-start | bytes 221192 | tf_op jit(solution)/shard_map/ppermute | solution.py:32
  79.3 1.2 %collective-permute-start.20 = (bf16[144,256]{1,0:T(8,128)(2,1)S(1)}, bf16[144,256]{1,0:T(8,128)(2,1)S(1)}, u32[]{:S(2)}, u32[]{:S(2)}) collective-permute-start(bf16[144,256]{1,0:T(8,128)(2,1)S(1)} %slice.43), channel_id=1, source_target_pairs={{0,192},{32,224},{64,0},{96,32},{128,64},{160,96},{192,128},{224,1... | collective-permute-start | bytes 221192 | tf_op jit(solution)/shard_map/ppermute | solution.py:32
  80.6 2.7 %collective-permute-done.19.refs_7_ = bf16[144,256]{1,0:T(8,128)(2,1)S(1)} collective-permute-done((bf16[144,256]{1,0:T(8,128)(2,1)S(1)}, bf16[144,256]{1,0:T(8,128)(2,1)S(1)}, u32[]{:S(2)}, u32[]{:S(2)}) %collective-permute-start.19) | collective-permute-done | bytes 73760 | tf_op jit(solution)/shard_map/ppermute | solution.py:32
  83.2 1.9 %collective-permute-done.20.refs_8_ = bf16[144,256]{1,0:T(8,128)(2,1)S(1)} collective-permute-done((bf16[144,256]{1,0:T(8,128)(2,1)S(1)}, bf16[144,256]{1,0:T(8,128)(2,1)S(1)}, u32[]{:S(2)}, u32[]{:S(2)}) %collective-permute-start.20) | collective-permute-done | bytes 73760 | tf_op jit(solution)/shard_map/ppermute | solution.py:32
  85.1 2.0 %second.1 = (bf16[64,768]{1,0:T(8,128)(2,1)S(1)}, bf16[64,768]{1,0:T(8,128)(2,1)S(1)}, bf16[64,768]{1,0:T(8,128)(2,1)S(1)}, bf16[64,768]{1,0:T(8,128)(2,1)S(1)}) custom-call(bf16[288,256]{1,0:T(8,128)(2,1)S(1)} %fusion.refs_0_, bf16[288,256]{1,0:T(8,128)(2,1)S(1)} %collective-permute-done.13.refs_1_, bf16[288,256]{1,0:T(8,128)(2,1)S(1)} %collective-permute-done.14.refs_2_, ...), custom_call_target="tpu_custom_call" | custom-call | flops 905969664 | bytes 6291456 | tf_op jit(solution)/shard_map/second/pallas_call | solution.py:221
  87.1 0.3 collective-permute-start.25
  87.4 2.6 %collective-permute-start.26 = (bf16[64,768]{1,0:T(8,128)(2,1)S(1)}, bf16[64,768]{1,0:T(8,128)(2,1)S(1)}, u32[]{:S(2)}, u32[]{:S(2)}) collective-permute-start(bf16[64,768]{1,0:T(8,128)(2,1)S(1)} %get-tuple-element.17), channel_id=1, source_target_pairs={{0,8},{4,12},{8,0},{12,4},{1,9},{5,13},{9,1},{13,5},{2,10},{6,14},... | collective-permute-start | bytes 294920 | tf_op jit(solution)/shard_map/ppermute | solution.py:28
  90.0 1.8 %collective-permute-done.25 = bf16[64,768]{1,0:T(8,128)(2,1)S(1)} collective-permute-done((bf16[64,768]{1,0:T(8,128)(2,1)S(1)}, bf16[64,768]{1,0:T(8,128)(2,1)S(1)}, u32[]{:S(2)}, u32[]{:S(2)}) %collective-permute-start.25) | collective-permute-done | bytes 98336 | tf_op jit(solution)/shard_map/ppermute | solution.py:28
  91.8 1.7 %collective-permute-done.26 = bf16[64,768]{1,0:T(8,128)(2,1)S(1)} collective-permute-done((bf16[64,768]{1,0:T(8,128)(2,1)S(1)}, bf16[64,768]{1,0:T(8,128)(2,1)S(1)}, u32[]{:S(2)}, u32[]{:S(2)}) %collective-permute-start.26) | collective-permute-done | bytes 98336 | tf_op jit(solution)/shard_map/ppermute | solution.py:28
  93.5 2.3 %collective-permute-done.27 = bf16[64,768]{1,0:T(8,128)(2,1)S(1)} collective-permute-done((bf16[64,768]{1,0:T(8,128)(2,1)S(1)}, bf16[64,768]{1,0:T(8,128)(2,1)S(1)}, u32[]{:S(2)}, u32[]{:S(2)}) %collective-permute-start.27) | collective-permute-done | bytes 98336 | tf_op jit(solution)/shard_map/ppermute | solution.py:28
  95.9 3.1 %collective-permute-start.28 = (bf16[64,384]{1,0:T(8,128)(2,1)S(1)}, bf16[64,384]{1,0:T(8,128)(2,1)S(1)}, u32[]{:S(2)}, u32[]{:S(2)}) collective-permute-start(bf16[64,384]{1,0:T(8,128)(2,1)S(1)} %get-tuple-element.21), channel_id=1, source_target_pairs={{0,96},{1,128},{2,97},{3,129},{4,64},{5,160},{6,65},{7,161},{8,0},... | collective-permute-start | bytes 147464 | tf_op jit(solution)/shard_map/ppermute | solution.py:235
  99.0 6.2 %collective-permute-done.28 = bf16[64,384]{1,0:T(8,128)(2,1)S(1)} collective-permute-done((bf16[64,384]{1,0:T(8,128)(2,1)S(1)}, bf16[64,384]{1,0:T(8,128)(2,1)S(1)}, u32[]{:S(2)}, u32[]{:S(2)}) %collective-permute-start.28) | collective-permute-done | bytes 49184 | tf_op jit(solution)/shard_map/ppermute | solution.py:235
  105.2 5.4 %collective-permute-done.29 = bf16[64,384]{1,0:T(8,128)(2,1)S(1)} collective-permute-done((bf16[64,384]{1,0:T(8,128)(2,1)S(1)}, bf16[64,384]{1,0:T(8,128)(2,1)S(1)}, u32[]{:S(2)}, u32[]{:S(2)}) %collective-permute-start.29) | collective-permute-done | bytes 49184 | tf_op jit(solution)/shard_map/ppermute | solution.py:235
  110.6 0.7 copy.7
  (36 shorter events, 0.8 us)
Async XLA Ops:
  0.0 1.1 copy-start
  0.0 15.2 %copy-start.1 = (bf16[576,336]{0,1:T(8,128)(2,1)S(1)}, bf16[576,336]{0,1:T(8,128)(2,1)}, u32[]{:S(2)}) copy-start(bf16[576,336]{0,1:T(8,128)(2,1)} %param.7) | copy-start | bytes 1161220
  1.1 9.9 %collective-permute-start = (bf16[64,2688]{1,0:T(8,128)(2,1)S(1)}, bf16[64,2688]{1,0:T(8,128)(2,1)S(1)}, u32[]{:S(2)}, u32[]{:S(2)}) collective-permute-start(bf16[64,2688]{1,0:T(8,128)(2,1)S(1)} %constant_dynamic-slice_fusion.2.refs_0_), channel_id=1, source_target_pairs={{0,32},{32,64},{64,96},{96,128},{128,160},{160,192},{192,224},{224... | collective-permute-start | bytes 1032200 | tf_op jit(solution)/shard_map/ppermute | solution.py:32
  3.1 9.8 %collective-permute-start.3 = (bf16[64,2688]{1,0:T(8,128)(2,1)S(1)}, bf16[64,2688]{1,0:T(8,128)(2,1)S(1)}, u32[]{:S(2)}, u32[]{:S(2)}) collective-permute-start(bf16[64,2688]{1,0:T(8,128)(2,1)S(1)} %constant_dynamic-slice_fusion.2.refs_0_), channel_id=1, source_target_pairs={{0,224},{32,0},{64,32},{96,64},{128,96},{160,128},{192,160},{224,1... | collective-permute-start | bytes 1032200 | tf_op jit(solution)/shard_map/ppermute | solution.py:32
  4.4 21.5 %collective-permute-start.8 = (bf16[2,72,2688]{2,1,0:T(8,128)(2,1)S(1)}, bf16[2,72,2688]{2,1,0:T(8,128)(2,1)S(1)}, u32[]{:S(2)}, u32[]{:S(2)}) collective-permute-start(bf16[2,72,2688]{2,1,0:T(8,128)(2,1)S(1)} %pad_maximum_fusion.1.refs_9_), channel_id=1, source_target_pairs={{0,16},{16,2},{2,18},{18,0},{1,17},{17,3},{3,19},{19,1},{4,20},{20... | collective-permute-start | bytes 2322440 | tf_op jit(solution)/shard_map/ppermute | solution.py:24
  6.0 30.2 %collective-permute-start.9 = (bf16[2,72,2688]{2,1,0:T(8,128)(2,1)S(1)}, bf16[2,72,2688]{2,1,0:T(8,128)(2,1)S(1)}, u32[]{:S(2)}, u32[]{:S(2)}) collective-permute-start(bf16[2,72,2688]{2,1,0:T(8,128)(2,1)S(1)} %pad_maximum_fusion.1.refs_9_), channel_id=1, source_target_pairs={{0,18},{16,0},{2,16},{18,2},{1,19},{17,1},{3,17},{19,3},{4,22},{20... | collective-permute-start | bytes 2322440 | tf_op jit(solution)/shard_map/ppermute | solution.py:24
  11.0 11.7 %collective-permute-start.1 = (bf16[64,2688]{1,0:T(8,128)(2,1)S(1)}, bf16[64,2688]{1,0:T(8,128)(2,1)S(1)}, u32[]{:S(2)}, u32[]{:S(2)}) collective-permute-start(bf16[64,2688]{1,0:T(8,128)(2,1)S(1)} %collective-permute-done.refs_1_), channel_id=1, source_target_pairs={{0,32},{32,64},{64,96},{96,128},{128,160},{160,192},{192,224},{224... | collective-permute-start | bytes 1032200 | tf_op jit(solution)/shard_map/ppermute | solution.py:32
  12.9 11.3 %collective-permute-start.4 = (bf16[64,2688]{1,0:T(8,128)(2,1)S(1)}, bf16[64,2688]{1,0:T(8,128)(2,1)S(1)}, u32[]{:S(2)}, u32[]{:S(2)}) collective-permute-start(bf16[64,2688]{1,0:T(8,128)(2,1)S(1)} %collective-permute-done.3.refs_4_), channel_id=1, source_target_pairs={{0,224},{32,0},{64,32},{96,64},{128,96},{160,128},{192,160},{224,1... | collective-permute-start | bytes 1032200 | tf_op jit(solution)/shard_map/ppermute | solution.py:32
  15.4 22.5 %collective-permute-start.21 = (bf16[576,384]{1,0:T(8,128)(2,1)S(1)}, bf16[576,384]{1,0:T(8,128)(2,1)S(1)}, u32[]{:S(2)}, u32[]{:S(2)}) collective-permute-start(bf16[576,384]{1,0:T(8,128)(2,1)S(1)} %down.1), channel_id=1, source_target_pairs={{0,2},{16,18},{2,0},{18,16},{1,3},{17,19},{3,1},{19,17},{4,6},{20,... | collective-permute-start | bytes 1327112 | tf_op jit(solution)/shard_map/ppermute | solution.py:24
  22.7 21.7 %collective-permute-start.22 = (bf16[576,384]{1,0:T(8,128)(2,1)S(1)}, bf16[576,384]{1,0:T(8,128)(2,1)S(1)}, u32[]{:S(2)}, u32[]{:S(2)}) collective-permute-start(bf16[576,384]{1,0:T(8,128)(2,1)S(1)} %down.1), channel_id=1, source_target_pairs={{0,16},{16,2},{2,18},{18,0},{1,17},{17,3},{3,19},{19,1},{4,20},{20... | collective-permute-start | bytes 1327112 | tf_op jit(solution)/shard_map/ppermute | solution.py:24
  24.2 22.2 %collective-permute-start.23 = (bf16[576,384]{1,0:T(8,128)(2,1)S(1)}, bf16[576,384]{1,0:T(8,128)(2,1)S(1)}, u32[]{:S(2)}, u32[]{:S(2)}) collective-permute-start(bf16[576,384]{1,0:T(8,128)(2,1)S(1)} %down.1), channel_id=1, source_target_pairs={{0,18},{16,0},{2,16},{18,2},{1,19},{17,1},{3,17},{19,3},{4,22},{20... | collective-permute-start | bytes 1327112 | tf_op jit(solution)/shard_map/ppermute | solution.py:24
  26.0 20.8 %collective-permute-start.2 = (bf16[64,2688]{1,0:T(8,128)(2,1)S(1)}, bf16[64,2688]{1,0:T(8,128)(2,1)S(1)}, u32[]{:S(2)}, u32[]{:S(2)}) collective-permute-start(bf16[64,2688]{1,0:T(8,128)(2,1)S(1)} %collective-permute-done.1.refs_2_), channel_id=1, source_target_pairs={{0,32},{32,64},{64,96},{96,128},{128,160},{160,192},{192,224},{224... | collective-permute-start | bytes 1032200 | tf_op jit(solution)/shard_map/ppermute | solution.py:32
  36.2 12.6 %collective-permute-start.5 = (bf16[64,2688]{1,0:T(8,128)(2,1)S(1)}, bf16[64,2688]{1,0:T(8,128)(2,1)S(1)}, u32[]{:S(2)}, u32[]{:S(2)}) collective-permute-start(bf16[64,2688]{1,0:T(8,128)(2,1)S(1)} %collective-permute-done.4.refs_5_), channel_id=1, source_target_pairs={{0,224},{32,0},{64,32},{96,64},{128,96},{160,128},{192,160},{224,1... | collective-permute-start | bytes 1032200 | tf_op jit(solution)/shard_map/ppermute | solution.py:32
  37.9 13.8 %collective-permute-start.10 = (bf16[1,72,2688]{2,1,0:T(8,128)(2,1)S(1)}, bf16[1,72,2688]{2,1,0:T(8,128)(2,1)S(1)}, u32[]{:S(2)}, u32[]{:S(2)}) collective-permute-start(bf16[1,72,2688]{2,1,0:T(8,128)(2,1)S(1)} %slice.38), channel_id=1, source_target_pairs={{0,16},{16,2},{2,18},{18,0},{1,17},{17,3},{3,19},{19,1},{4,20},{20... | collective-permute-start | bytes 1161224 | tf_op jit(solution)/shard_map/ppermute | solution.py:24
  44.4 9.2 %collective-permute-start.11 = (bf16[1,72,2688]{2,1,0:T(8,128)(2,1)S(1)}, bf16[1,72,2688]{2,1,0:T(8,128)(2,1)S(1)}, u32[]{:S(2)}, u32[]{:S(2)}) collective-permute-start(bf16[1,72,2688]{2,1,0:T(8,128)(2,1)S(1)} %slice.39), channel_id=1, source_target_pairs={{0,18},{16,0},{2,16},{18,2},{1,19},{17,1},{3,17},{19,3},{4,22},{20... | collective-permute-start | bytes 1161224 | tf_op jit(solution)/shard_map/ppermute | solution.py:24
  46.7 38.4 %collective-permute-start.24 = (bf16[4,576,384]{2,1,0:T(8,128)(2,1)S(1)}, bf16[4,576,384]{2,1,0:T(8,128)(2,1)S(1)}, u32[]{:S(2)}, u32[]{:S(2)}) collective-permute-start(bf16[4,576,384]{2,1,0:T(8,128)(2,1)S(1)} %pad_maximum_fusion.refs_9_), channel_id=1, source_target_pairs={{0,1},{1,0},{2,3},{3,2},{4,5},{5,4},{6,7},{7,6},{8,9},{9,8},{10,11... | collective-permute-start | bytes 5308424 | tf_op jit(solution)/shard_map/ppermute | solution.py:36
  46.8 9.1 %collective-permute-start.6 = (bf16[32,2688]{1,0:T(8,128)(2,1)S(1)}, bf16[32,2688]{1,0:T(8,128)(2,1)S(1)}, u32[]{:S(2)}, u32[]{:S(2)}) collective-permute-start(bf16[32,2688]{1,0:T(8,128)(2,1)S(1)} %slice.36), channel_id=1, source_target_pairs={{0,32},{32,64},{64,96},{96,128},{128,160},{160,192},{192,224},{224... | collective-permute-start | bytes 516104 | tf_op jit(solution)/shard_map/ppermute | solution.py:32
  48.8 8.0 %collective-permute-start.7 = (bf16[32,2688]{1,0:T(8,128)(2,1)S(1)}, bf16[32,2688]{1,0:T(8,128)(2,1)S(1)}, u32[]{:S(2)}, u32[]{:S(2)}) collective-permute-start(bf16[32,2688]{1,0:T(8,128)(2,1)S(1)} %slice.37), channel_id=1, source_target_pairs={{0,224},{32,0},{64,32},{96,64},{128,96},{160,128},{192,160},{224,1... | collective-permute-start | bytes 516104 | tf_op jit(solution)/shard_map/ppermute | solution.py:32
  58.4 2.1 %collective-permute-start.12 = (f32[576,256]{1,0:T(8,128)S(1)}, f32[576,256]{1,0:T(8,128)S(1)}, u32[]{:S(2)}, u32[]{:S(2)}) collective-permute-start(f32[576,256]{1,0:T(8,128)S(1)} %get-tuple-element.14), channel_id=1, source_target_pairs={{0,1},{1,0},{2,3},{3,2},{4,5},{5,4},{6,7},{7,6},{8,9},{9,8},{10,11... | collective-permute-start | bytes 1769480 | tf_op jit(solution)/shard_map/ppermute | solution.py:36
  60.7 12.6 %collective-permute-start.14 = (bf16[288,256]{1,0:T(8,128)(2,1)S(1)}, bf16[288,256]{1,0:T(8,128)(2,1)S(1)}, u32[]{:S(2)}, u32[]{:S(2)}) collective-permute-start(bf16[288,256]{1,0:T(8,128)(2,1)S(1)} %fusion.refs_0_), channel_id=1, source_target_pairs={{0,64},{32,96},{64,128},{96,160},{128,192},{160,224},{192,0},{224,... | collective-permute-start | bytes 442376 | tf_op jit(solution)/shard_map/ppermute | solution.py:32
  66.4 9.9 %collective-permute-start.17 = (bf16[288,256]{1,0:T(8,128)(2,1)S(1)}, bf16[288,256]{1,0:T(8,128)(2,1)S(1)}, u32[]{:S(2)}, u32[]{:S(2)}) collective-permute-start(bf16[288,256]{1,0:T(8,128)(2,1)S(1)} %fusion.refs_0_), channel_id=1, source_target_pairs={{0,192},{32,224},{64,0},{96,32},{128,64},{160,96},{192,128},{224,1... | collective-permute-start | bytes 442376 | tf_op jit(solution)/shard_map/ppermute | solution.py:32
  66.4 9.9 %collective-permute-start.13 = (bf16[288,256]{1,0:T(8,128)(2,1)S(1)}, bf16[288,256]{1,0:T(8,128)(2,1)S(1)}, u32[]{:S(2)}, u32[]{:S(2)}) collective-permute-start(bf16[288,256]{1,0:T(8,128)(2,1)S(1)} %fusion.refs_0_), channel_id=1, source_target_pairs={{0,32},{32,64},{64,96},{96,128},{128,160},{160,192},{192,224},{224... | collective-permute-start | bytes 442376 | tf_op jit(solution)/shard_map/ppermute | solution.py:32
  67.0 12.4 %collective-permute-start.16 = (bf16[288,256]{1,0:T(8,128)(2,1)S(1)}, bf16[288,256]{1,0:T(8,128)(2,1)S(1)}, u32[]{:S(2)}, u32[]{:S(2)}) collective-permute-start(bf16[288,256]{1,0:T(8,128)(2,1)S(1)} %fusion.refs_0_), channel_id=1, source_target_pairs={{0,224},{32,0},{64,32},{96,64},{128,96},{160,128},{192,160},{224,1... | collective-permute-start | bytes 442376 | tf_op jit(solution)/shard_map/ppermute | solution.py:32
  73.4 11.8 %collective-permute-start.15 = (bf16[288,256]{1,0:T(8,128)(2,1)S(1)}, bf16[288,256]{1,0:T(8,128)(2,1)S(1)}, u32[]{:S(2)}, u32[]{:S(2)}) collective-permute-start(bf16[288,256]{1,0:T(8,128)(2,1)S(1)} %collective-permute-done.14.refs_2_), channel_id=1, source_target_pairs={{0,32},{32,64},{64,96},{96,128},{128,160},{160,192},{192,224},{224... | collective-permute-start | bytes 442376 | tf_op jit(solution)/shard_map/ppermute | solution.py:32
  76.3 8.8 %collective-permute-start.18 = (bf16[288,256]{1,0:T(8,128)(2,1)S(1)}, bf16[288,256]{1,0:T(8,128)(2,1)S(1)}, u32[]{:S(2)}, u32[]{:S(2)}) collective-permute-start(bf16[288,256]{1,0:T(8,128)(2,1)S(1)} %collective-permute-done.17.refs_5_), channel_id=1, source_target_pairs={{0,224},{32,0},{64,32},{96,64},{128,96},{160,128},{192,160},{224,1... | collective-permute-start | bytes 442376 | tf_op jit(solution)/shard_map/ppermute | solution.py:32
  76.3 6.9 %collective-permute-start.19 = (bf16[144,256]{1,0:T(8,128)(2,1)S(1)}, bf16[144,256]{1,0:T(8,128)(2,1)S(1)}, u32[]{:S(2)}, u32[]{:S(2)}) collective-permute-start(bf16[144,256]{1,0:T(8,128)(2,1)S(1)} %slice.42), channel_id=1, source_target_pairs={{0,64},{32,96},{64,128},{96,160},{128,192},{160,224},{192,0},{224,... | collective-permute-start | bytes 221192 | tf_op jit(solution)/shard_map/ppermute | solution.py:32
  79.3 5.8 %collective-permute-start.20 = (bf16[144,256]{1,0:T(8,128)(2,1)S(1)}, bf16[144,256]{1,0:T(8,128)(2,1)S(1)}, u32[]{:S(2)}, u32[]{:S(2)}) collective-permute-start(bf16[144,256]{1,0:T(8,128)(2,1)S(1)} %slice.43), channel_id=1, source_target_pairs={{0,192},{32,224},{64,0},{96,32},{128,64},{160,96},{192,128},{224,1... | collective-permute-start | bytes 221192 | tf_op jit(solution)/shard_map/ppermute | solution.py:32
  87.1 4.7 %collective-permute-start.25 = (bf16[64,768]{1,0:T(8,128)(2,1)S(1)}, bf16[64,768]{1,0:T(8,128)(2,1)S(1)}, u32[]{:S(2)}, u32[]{:S(2)}) collective-permute-start(bf16[64,768]{1,0:T(8,128)(2,1)S(1)} %get-tuple-element.16), channel_id=1, source_target_pairs={{0,4},{4,8},{8,12},{12,0},{1,5},{5,9},{9,13},{13,1},{2,6},{6,10},{... | collective-permute-start | bytes 294920 | tf_op jit(solution)/shard_map/ppermute | solution.py:28
  87.4 6.1 %collective-permute-start.26 = (bf16[64,768]{1,0:T(8,128)(2,1)S(1)}, bf16[64,768]{1,0:T(8,128)(2,1)S(1)}, u32[]{:S(2)}, u32[]{:S(2)}) collective-permute-start(bf16[64,768]{1,0:T(8,128)(2,1)S(1)} %get-tuple-element.17), channel_id=1, source_target_pairs={{0,8},{4,12},{8,0},{12,4},{1,9},{5,13},{9,1},{13,5},{2,10},{6,14},... | collective-permute-start | bytes 294920 | tf_op jit(solution)/shard_map/ppermute | solution.py:28
  90.0 5.8 %collective-permute-start.27 = (bf16[64,768]{1,0:T(8,128)(2,1)S(1)}, bf16[64,768]{1,0:T(8,128)(2,1)S(1)}, u32[]{:S(2)}, u32[]{:S(2)}) collective-permute-start(bf16[64,768]{1,0:T(8,128)(2,1)S(1)} %get-tuple-element.18), channel_id=1, source_target_pairs={{0,12},{4,0},{8,4},{12,8},{1,13},{5,1},{9,5},{13,9},{2,14},{6,2},{... | collective-permute-start | bytes 294920 | tf_op jit(solution)/shard_map/ppermute | solution.py:28
  95.9 9.3 %collective-permute-start.28 = (bf16[64,384]{1,0:T(8,128)(2,1)S(1)}, bf16[64,384]{1,0:T(8,128)(2,1)S(1)}, u32[]{:S(2)}, u32[]{:S(2)}) collective-permute-start(bf16[64,384]{1,0:T(8,128)(2,1)S(1)} %get-tuple-element.21), channel_id=1, source_target_pairs={{0,96},{1,128},{2,97},{3,129},{4,64},{5,160},{6,65},{7,161},{8,0},... | collective-permute-start | bytes 147464 | tf_op jit(solution)/shard_map/ppermute | solution.py:235
  99.0 11.6 %collective-permute-start.29 = (bf16[64,384]{1,0:T(8,128)(2,1)S(1)}, bf16[64,384]{1,0:T(8,128)(2,1)S(1)}, u32[]{:S(2)}, u32[]{:S(2)}) collective-permute-start(bf16[64,384]{1,0:T(8,128)(2,1)S(1)} %get-tuple-element.22), channel_id=1, source_target_pairs={{0,97},{1,129},{2,96},{3,128},{4,65},{5,161},{6,64},{7,160},{8,1},... | collective-permute-start | bytes 147464 | tf_op jit(solution)/shard_map/ppermute | solution.py:235

commit v4 on v3

--- a/solution.py
+++ b/solution.py
@@ -114,6 +114,12 @@
     half_product(far_tok, wts, send)
 
 
+def out_kernel(a, b, out):
+    c, f = lax.axis_index("c"), out.shape[0]
+    rows = jnp.concatenate([jnp.where(c == 0, a[...], b[...]), jnp.where(c == 0, b[...], a[...])], 0)
+    out[...] = rows.T[:f, :]
+
+
 def half_product(tok, wts, out):
     flat = wts[...].reshape(out.shape[0], wts.shape[2])
     out[...] = lax.dot_general(flat, tok[...], (((1,), (1,)), ((), ())), preferred_element_type=jnp.float32)
@@ -135,20 +141,14 @@
         put(off, 1, block[n:, :])
     put(4, 0, u4[...])
     put(4, 1, d4[...])
-    t = outs[0].shape[0]
-    for d in range(2):
-        total = None
-        for half, down in enumerate((near, far)):
-            for h in range(2):
-                slot = jnp.where(xl == d, h, 2 + (1 - xl ^ h))
-                lo = (half * 2 + h) * rows
-                term = lax.dot_general(hid[lo:lo + rows, :], down[slot], (((0,), (0,)), ((), ())),
-                                       preferred_element_type=jnp.float32)
-                total = term if total is None else total + term
-        val[...] = total
-        for k, out in enumerate(outs):
-            at = kept_at(z, c, lax.rem(y + k, 4)) * t
-            out[:, d * PAD:(d + 1) * PAD] = val[pl.ds(pl.multiple_of(at, t), t), :].astype(out.dtype)
+    t, k = outs[0].shape[0], 2 * rows
+    dims = (((0,), (0,)), ((), ()))
+    val[...] = lax.dot_general(hid[:k, :], near[...], dims, preferred_element_type=jnp.float32)
+    val[...] += lax.dot_general(hid[k:, :], far[...], dims, preferred_element_type=jnp.float32)
+    for i, out in enumerate(outs):
+        at = pl.multiple_of(kept_at(z, c, lax.rem(y + i, 4)) * t, t)
+        for f in range(2):
+            out[:, pl.ds(pl.multiple_of((f ^ xl) * PAD, PAD), PAD)] = val[pl.ds(at, t), f * PAD:(f + 1) * PAD].astype(out.dtype)
 
 
 VMEM = pl.BlockSpec(memory_space=pltpu.VMEM)
@@ -168,7 +168,7 @@
                     final_perms[1].append((src, dst + 1 - xh))
 
     def body(tokens, gate, up, down):
-        xh, c = lax.axis_index("xh"), lax.axis_index("c")
+        xl, xh, _ = (lax.axis_index(a) for a in ("xl", "xh", "c"))
         units, k, n = gate.shape[0], tokens.shape[1], tokens.shape[0] // 2
         bf16 = jnp.bfloat16
 
@@ -187,8 +187,9 @@
             cost_estimate=pl.CostEstimate(flops=10**8, bytes_accessed=1 << 20, transcendentals=0),
             name="down",
         )(down.T)
-        near = [dblk, px(dblk, 2), px(dblk, 1), px(dblk, -1)]
-        near = jnp.stack(near)
+        d_2, d_m1, d_p1 = px(dblk, 2), px(dblk, 1), px(dblk, -1)
+        same, other = jnp.where(xl == 0, d_p1, d_m1), jnp.where(xl == 0, d_m1, d_p1)
+        near = jnp.concatenate([jnp.concatenate([dblk, same], 1), jnp.concatenate([d_2, other], 1)], 0)
         far = core_swap(near)
 
         m, t = 8 * units, Z * n
@@ -223,7 +224,7 @@
             out_shape=(piece,) * 4,
             in_specs=[VMEM] * 11,
             out_specs=(VMEM,) * 4,
-            scratch_shapes=[pltpu.VMEM((Z * 4 * units, t // 2), bf16), pltpu.VMEM((t // 2, PAD), jnp.float32)],
+            scratch_shapes=[pltpu.VMEM((Z * 4 * units, t // 2), bf16), pltpu.VMEM((t // 2, 2 * PAD), jnp.float32)],
             compiler_params=pltpu.CompilerParams(vmem_limit_bytes=10 << 20),
             cost_estimate=pl.CostEstimate(flops=2 * Z * 4 * units * t * PAD, bytes_accessed=6 << 20, transcendentals=0),
             name="second",
@@ -233,8 +234,14 @@
         total = sum(p.astype(jnp.float32) for p in parts).astype(bf16)
         mine, other = (lax.dynamic_slice_in_dim(total, d * PAD, PAD, 1) for d in (xh, 1 - xh))
         got_a, got_b = lax.ppermute(mine, final_axes, final_perms[0]), lax.ppermute(other, final_axes, final_perms[1])
-        rows = jnp.where(c == 0, jnp.concatenate([got_a, got_b], 0), jnp.concatenate([got_b, got_a], 0))
-        return rows[:, :down.shape[1]]
+        return pl.pallas_call(
+            out_kernel,
+            out_shape=jax.ShapeDtypeStruct((down.shape[1], 2 * n), bf16),
+            in_specs=[VMEM] * 2,
+            out_specs=VMEM,
+            compiler_params=pltpu.CompilerParams(vmem_limit_bytes=4 << 20),
+            name="out",
+        )(got_a, got_b).T
 
     row, col = ("z", "xl"), ("y", "xh")
     return jax.shard_map(

time: 111 us -> 116 us (1.045)
  the two profiles are of different devices: /device:TPU:56 before, /device:TPU:58 now
where the time goes in v4:
time: 116 us
  starting transfers between devices  53.1 us (46%)
  waiting for transfers between devices  49.3 us (42%)
  Pallas kernels  6.15 us (5%)
  other arithmetic  3.8 us (3%)
  local copies, waits for them, and re-layouts  3.06 us (3%)
    ppermute x16, starting transfers between devices, pz(): return lax.ppermute(v, 'z', ring(Z, k))  27.2 us
    ppermute x16, waiting for transfers between devices, pz(): return lax.ppermute(v, 'z', ring(Z, k))  24.8 us
    ppermute x7, starting transfers between devices, px(): return lax.ppermute(v, ('xl', 'xh'), x_ring(k))  18.2 us
    ppermute x1, waiting for transfers between devices, body(): lax.ppermute(other, final_axes, final_perms[1])  6.92 us
    ppermute x7, waiting for transfers between devices, px(): return lax.ppermute(v, ('xl', 'xh'), x_ring(k))  6.07 us
    ppermute x3, waiting for transfers between devices, py(): return lax.ppermute(v, 'y', ring(Y, k))  5.82 us
    ppermute x1, waiting for transfers between devices, body(): lax.ppermute(mine, final_axes, final_perms[0])  4.69 us
    ppermute x1, starting transfers between devices, body(): lax.ppermute(mine, final_axes, final_perms[0])  4.61 us
  transfers between devices with their start and end apart: 30, of which 19 were waited for; matrix products, arithmetic and copies ran while one was open for 3% of the time, Pallas kernels for 3%

profile of v4, /device:TPU:58, one launch (start us, length us, event | category | flops | bytes accessed | tf_op | source)
XLA Modules:
  0.0 115.6 jit_solution(16448373213117525631)
XLA Ops:
  0.0 1.1 copy-done
  1.1 2.0 %collective-permute-start = (bf16[64,2688]{1,0:T(8,128)(2,1)S(1)}, bf16[64,2688]{1,0:T(8,128)(2,1)}, u32[]{:S(2)}, u32[]{:S(2)}) collective-permute-start(bf16[64,2688]{1,0:T(8,128)(2,1)S(1)} %constant_dynamic-slice_fusion.2.refs_0_), channel_id=1, source_target_pairs={{0,32},{32,64},{64,96},{96,128},{128,160},{160,192},{192,224},{224... | collective-permute-start | bytes 1032200 | tf_op jit(solution)/shard_map/ppermute | solution.py:32
  3.2 1.0 copy-done.3
  4.4 0.6 collective-permute-start.21
  5.0 1.5 %collective-permute-start.22 = (bf16[576,384]{1,0:T(8,128)(2,1)S(1)}, bf16[576,384]{1,0:T(8,128)(2,1)S(1)}, u32[]{:S(2)}, u32[]{:S(2)}) collective-permute-start(bf16[576,384]{1,0:T(8,128)(2,1)S(1)} %down.1), channel_id=1, source_target_pairs={{0,16},{16,2},{2,18},{18,0},{1,17},{17,3},{3,19},{19,1},{4,20},{20... | collective-permute-start | bytes 1327112 | tf_op jit(solution)/shard_map/ppermute | solution.py:24
  6.5 1.2 %pad_maximum_fusion.refs_9_ = bf16[2,72,2688]{2,1,0:T(8,128)(2,1)S(1)} fusion(bf16[1,72,2688]{2,1,0:T(8,128)(2,1)} %bitcast.28, bf16[1,72,2688]{2,1,0:T(8,128)(2,1)} %bitcast.29), kind=kLoop, calls=%fused_computation.1 | loop fusion | flops 387072 | bytes 1548288 | tf_op jit(solution)/shard_map/stack | solution.py:177
  7.7 1.6 %collective-permute-start.8 = (bf16[2,72,2688]{2,1,0:T(8,128)(2,1)S(1)}, bf16[2,72,2688]{2,1,0:T(8,128)(2,1)S(1)}, u32[]{:S(2)}, u32[]{:S(2)}) collective-permute-start(bf16[2,72,2688]{2,1,0:T(8,128)(2,1)S(1)} %pad_maximum_fusion.refs_9_), channel_id=1, source_target_pairs={{0,16},{16,2},{2,18},{18,0},{1,17},{17,3},{3,19},{19,1},{4,20},{20... | collective-permute-start | bytes 2322440 | tf_op jit(solution)/shard_map/ppermute | solution.py:24
  9.3 1.8 %collective-permute-done.refs_1_ = bf16[64,2688]{1,0:T(8,128)(2,1)} collective-permute-done((bf16[64,2688]{1,0:T(8,128)(2,1)S(1)}, bf16[64,2688]{1,0:T(8,128)(2,1)}, u32[]{:S(2)}, u32[]{:S(2)}) %collective-permute-start) | collective-permute-done | bytes 344096 | tf_op jit(solution)/shard_map/ppermute | solution.py:32
  11.1 0.5 collective-permute-start.9
  11.7 1.3 %collective-permute-done.3.refs_4_ = bf16[64,2688]{1,0:T(8,128)(2,1)} collective-permute-done((bf16[64,2688]{1,0:T(8,128)(2,1)S(1)}, bf16[64,2688]{1,0:T(8,128)(2,1)}, u32[]{:S(2)}, u32[]{:S(2)}) %collective-permute-start.3) | collective-permute-done | bytes 344096 | tf_op jit(solution)/shard_map/ppermute | solution.py:32
  12.9 2.1 %collective-permute-start.23 = (bf16[576,384]{1,0:T(8,128)(2,1)S(1)}, bf16[576,384]{1,0:T(8,128)(2,1)}, u32[]{:S(2)}, u32[]{:S(2)}) collective-permute-start(bf16[576,384]{1,0:T(8,128)(2,1)S(1)} %down.1), channel_id=1, source_target_pairs={{0,2},{16,18},{2,0},{18,16},{1,3},{17,19},{3,1},{19,17},{4,6},{20,... | collective-permute-start | bytes 1327112 | tf_op jit(solution)/shard_map/ppermute | solution.py:24
  15.1 2.5 %collective-permute-done.21 = bf16[576,384]{1,0:T(8,128)(2,1)S(1)} collective-permute-done((bf16[576,384]{1,0:T(8,128)(2,1)S(1)}, bf16[576,384]{1,0:T(8,128)(2,1)S(1)}, u32[]{:S(2)}, u32[]{:S(2)}) %collective-permute-start.21) | collective-permute-done | bytes 442400 | tf_op jit(solution)/shard_map/ppermute | solution.py:24
  17.6 1.9 %collective-permute-start.1 = (bf16[64,2688]{1,0:T(8,128)(2,1)}, bf16[64,2688]{1,0:T(8,128)(2,1)}, u32[]{:S(2)}, u32[]{:S(2)}) collective-permute-start(bf16[64,2688]{1,0:T(8,128)(2,1)} %collective-permute-done.refs_1_), channel_id=1, source_target_pairs={{0,32},{32,64},{64,96},{96,128},{128,160},{160,192},{192,224},{224... | collective-permute-start | bytes 1032200 | tf_op jit(solution)/shard_map/ppermute | solution.py:32
  19.5 0.8 copy-done.5
  20.3 3.4 %collective-permute-start.4 = (bf16[64,2688]{1,0:T(8,128)(2,1)}, bf16[64,2688]{1,0:T(8,128)(2,1)}, u32[]{:S(2)}, u32[]{:S(2)}) collective-permute-start(bf16[64,2688]{1,0:T(8,128)(2,1)} %collective-permute-done.3.refs_4_), channel_id=1, source_target_pairs={{0,224},{32,0},{64,32},{96,64},{128,96},{160,128},{192,160},{224,1... | collective-permute-start | bytes 1032200 | tf_op jit(solution)/shard_map/ppermute | solution.py:32
  23.6 1.2 %broadcast_select_fusion.1 = (bf16[576,384]{1,0:T(8,128)(2,1)S(1)}, bf16[576,384]{1,0:T(8,128)(2,1)S(1)}) fusion(bf16[576,384]{1,0:T(8,128)(2,1)} %copy-done.4, bf16[576,384]{1,0:T(8,128)(2,1)} %copy-done.5, pred[]{:T(512)S(6)} %eq.4), kind=kLoop, calls=%fused_computation.3 | loop fusion | flops 442368 | bytes 1769473 | tf_op jit(solution)/shard_map/jit(_where)/select_n | solution.py:191
  24.9 2.5 %collective-permute-done.1.refs_2_ = bf16[64,2688]{1,0:T(8,128)(2,1)} collective-permute-done((bf16[64,2688]{1,0:T(8,128)(2,1)}, bf16[64,2688]{1,0:T(8,128)(2,1)}, u32[]{:S(2)}, u32[]{:S(2)}) %collective-permute-start.1) | collective-permute-done | bytes 344096 | tf_op jit(solution)/shard_map/ppermute | solution.py:32
  27.4 0.6 collective-permute-start.2
  28.1 1.3 %collective-permute-done.4.refs_5_ = bf16[64,2688]{1,0:T(8,128)(2,1)} collective-permute-done((bf16[64,2688]{1,0:T(8,128)(2,1)}, bf16[64,2688]{1,0:T(8,128)(2,1)}, u32[]{:S(2)}, u32[]{:S(2)}) %collective-permute-start.4) | collective-permute-done | bytes 344096 | tf_op jit(solution)/shard_map/ppermute | solution.py:32
  29.4 2.5 %collective-permute-start.5 = (bf16[64,2688]{1,0:T(8,128)(2,1)}, bf16[64,2688]{1,0:T(8,128)(2,1)S(1)}, u32[]{:S(2)}, u32[]{:S(2)}) collective-permute-start(bf16[64,2688]{1,0:T(8,128)(2,1)} %collective-permute-done.4.refs_5_), channel_id=1, source_target_pairs={{0,224},{32,0},{64,32},{96,64},{128,96},{160,128},{192,160},{224,1... | collective-permute-start | bytes 1032200 | tf_op jit(solution)/shard_map/ppermute | solution.py:32
  31.9 3.6 %collective-permute-done.8.refs_10_ = bf16[2,72,2688]{2,1,0:T(8,128)(2,1)S(1)} collective-permute-done((bf16[2,72,2688]{2,1,0:T(8,128)(2,1)S(1)}, bf16[2,72,2688]{2,1,0:T(8,128)(2,1)S(1)}, u32[]{:S(2)}, u32[]{:S(2)}) %collective-permute-start.8) | collective-permute-done | bytes 774176 | tf_op jit(solution)/shard_map/ppermute | solution.py:24
  35.6 11.8 %collective-permute-start.11 = (bf16[1,72,2688]{2,1,0:T(8,128)(2,1)S(1)}, bf16[1,72,2688]{2,1,0:T(8,128)(2,1)S(1)}, u32[]{:S(2)}, u32[]{:S(2)}) collective-permute-start(bf16[1,72,2688]{2,1,0:T(8,128)(2,1)S(1)} %slice.35), channel_id=1, source_target_pairs={{0,18},{16,0},{2,16},{18,2},{1,19},{17,1},{3,17},{19,3},{4,22},{20... | collective-permute-start | bytes 1161224 | tf_op jit(solution)/shard_map/ppermute | solution.py:24
  47.4 1.2 maximum_maximum_fusion.refs_9_
  48.7 2.0 %collective-permute-start.6 = (bf16[32,2688]{1,0:T(8,128)(2,1)S(1)}, bf16[32,2688]{1,0:T(8,128)(2,1)S(1)}, u32[]{:S(2)}, u32[]{:S(2)}) collective-permute-start(bf16[32,2688]{1,0:T(8,128)(2,1)S(1)} %slice.32), channel_id=1, source_target_pairs={{0,32},{32,64},{64,96},{96,128},{128,160},{160,192},{192,224},{224... | collective-permute-start | bytes 516104 | tf_op jit(solution)/shard_map/ppermute | solution.py:32
  50.7 2.6 %collective-permute-start.7 = (bf16[32,2688]{1,0:T(8,128)(2,1)S(1)}, bf16[32,2688]{1,0:T(8,128)(2,1)S(1)}, u32[]{:S(2)}, u32[]{:S(2)}) collective-permute-start(bf16[32,2688]{1,0:T(8,128)(2,1)S(1)} %slice.33), channel_id=1, source_target_pairs={{0,224},{32,0},{64,32},{96,64},{128,96},{160,128},{192,160},{224,1... | collective-permute-start | bytes 516104 | tf_op jit(solution)/shard_map/ppermute | solution.py:32
  53.2 4.7 %collective-permute-done.6.refs_7_ = bf16[32,2688]{1,0:T(8,128)(2,1)S(1)} collective-permute-done((bf16[32,2688]{1,0:T(8,128)(2,1)S(1)}, bf16[32,2688]{1,0:T(8,128)(2,1)S(1)}, u32[]{:S(2)}, u32[]{:S(2)}) %collective-permute-start.6) | collective-permute-done | bytes 172064 | tf_op jit(solution)/shard_map/ppermute | solution.py:32
  58.0 0.9 collective-permute-done.7.refs_8_
  58.9 2.8 %first.1 = (f32[576,256]{1,0:T(8,128)S(1)}, bf16[256,2688]{1,0:T(8,128)(2,1)S(1)}, bf16[4,144,2688]{2,1,0:T(8,128)(2,1)S(1)}) custom-call(bf16[64,2688]{1,0:T(8,128)(2,1)S(1)} %copy-done.2, bf16[64,2688]{1,0:T(8,128)(2,1)} %collective-permute-done.refs_1_, bf16[64,2688]{1,0:T(8,128)(2,1)} %collective-permute-done.1.refs_2_, ...), custom_call_target="tpu_custom_call" | custom-call | flops 792723456 | bytes 5849088 | tf_op jit(solution)/shard_map/first/pallas_call | solution.py:197
  61.8 1.0 keep.1
  62.8 1.0 collective-permute-done.12
  64.0 5.2 %collective-permute-start.14 = (bf16[288,256]{1,0:T(8,128)(2,1)S(1)}, bf16[288,256]{1,0:T(8,128)(2,1)S(1)}, u32[]{:S(2)}, u32[]{:S(2)}) collective-permute-start(bf16[288,256]{1,0:T(8,128)(2,1)S(1)} %fusion.refs_0_), channel_id=1, source_target_pairs={{0,64},{32,96},{64,128},{96,160},{128,192},{160,224},{192,0},{224,... | collective-permute-start | bytes 442376 | tf_op jit(solution)/shard_map/ppermute | solution.py:32
  69.2 0.5 collective-permute-start.13
  69.7 1.5 %collective-permute-start.16 = (bf16[288,256]{1,0:T(8,128)(2,1)S(1)}, bf16[288,256]{1,0:T(8,128)(2,1)S(1)}, u32[]{:S(2)}, u32[]{:S(2)}) collective-permute-start(bf16[288,256]{1,0:T(8,128)(2,1)S(1)} %fusion.refs_0_), channel_id=1, source_target_pairs={{0,224},{32,0},{64,32},{96,64},{128,96},{160,128},{192,160},{224,1... | collective-permute-start | bytes 442376 | tf_op jit(solution)/shard_map/ppermute | solution.py:32
  71.2 5.3 %collective-permute-done.14.refs_2_ = bf16[288,256]{1,0:T(8,128)(2,1)S(1)} collective-permute-done((bf16[288,256]{1,0:T(8,128)(2,1)S(1)}, bf16[288,256]{1,0:T(8,128)(2,1)S(1)}, u32[]{:S(2)}, u32[]{:S(2)}) %collective-permute-start.14) | collective-permute-done | bytes 147488 | tf_op jit(solution)/shard_map/ppermute | solution.py:32
  76.5 0.8 collective-permute-start.15
  77.3 1.3 %collective-permute-done.17.refs_5_ = bf16[288,256]{1,0:T(8,128)(2,1)S(1)} collective-permute-done((bf16[288,256]{1,0:T(8,128)(2,1)S(1)}, bf16[288,256]{1,0:T(8,128)(2,1)S(1)}, u32[]{:S(2)}, u32[]{:S(2)}) %collective-permute-start.17) | collective-permute-done | bytes 147488 | tf_op jit(solution)/shard_map/ppermute | solution.py:32
  78.9 3.7 %collective-permute-start.19 = (bf16[144,256]{1,0:T(8,128)(2,1)S(1)}, bf16[144,256]{1,0:T(8,128)(2,1)S(1)}, u32[]{:S(2)}, u32[]{:S(2)}) collective-permute-start(bf16[144,256]{1,0:T(8,128)(2,1)S(1)} %slice.38), channel_id=1, source_target_pairs={{0,64},{32,96},{64,128},{96,160},{128,192},{160,224},{192,0},{224,... | collective-permute-start | bytes 221192 | tf_op jit(solution)/shard_map/ppermute | solution.py:32
  83.0 3.1 %collective-permute-done.19.refs_7_ = bf16[144,256]{1,0:T(8,128)(2,1)S(1)} collective-permute-done((bf16[144,256]{1,0:T(8,128)(2,1)S(1)}, bf16[144,256]{1,0:T(8,128)(2,1)S(1)}, u32[]{:S(2)}, u32[]{:S(2)}) %collective-permute-start.19) | collective-permute-done | bytes 73760 | tf_op jit(solution)/shard_map/ppermute | solution.py:32
  86.1 2.3 %collective-permute-done.20.refs_8_ = bf16[144,256]{1,0:T(8,128)(2,1)S(1)} collective-permute-done((bf16[144,256]{1,0:T(8,128)(2,1)S(1)}, bf16[144,256]{1,0:T(8,128)(2,1)S(1)}, u32[]{:S(2)}, u32[]{:S(2)}) %collective-permute-start.20) | collective-permute-done | bytes 73760 | tf_op jit(solution)/shard_map/ppermute | solution.py:32
  88.4 1.4 %second.1 = (bf16[64,768]{1,0:T(8,128)(2,1)S(1)}, bf16[64,768]{1,0:T(8,128)(2,1)S(1)}, bf16[64,768]{1,0:T(8,128)(2,1)S(1)}, bf16[64,768]{1,0:T(8,128)(2,1)S(1)}) custom-call(bf16[288,256]{1,0:T(8,128)(2,1)S(1)} %fusion.refs_0_, bf16[288,256]{1,0:T(8,128)(2,1)S(1)} %collective-permute-done.13.refs_1_, bf16[288,256]{1,0:T(8,128)(2,1)S(1)} %collective-permute-done.14.refs_2_, ...), custom_call_target="tpu_custom_call" | custom-call | flops 905969664 | bytes 6291456 | tf_op jit(solution)/shard_map/second/pallas_call | solution.py:222
  90.2 2.6 %collective-permute-start.26 = (bf16[64,768]{1,0:T(8,128)(2,1)S(1)}, bf16[64,768]{1,0:T(8,128)(2,1)S(1)}, u32[]{:S(2)}, u32[]{:S(2)}) collective-permute-start(bf16[64,768]{1,0:T(8,128)(2,1)S(1)} %get-tuple-element.17), channel_id=1, source_target_pairs={{0,8},{4,12},{8,0},{12,4},{1,9},{5,13},{9,1},{13,5},{2,10},{6,14},... | collective-permute-start | bytes 294920 | tf_op jit(solution)/shard_map/ppermute | solution.py:28
  92.8 1.8 %collective-permute-done.25 = bf16[64,768]{1,0:T(8,128)(2,1)S(1)} collective-permute-done((bf16[64,768]{1,0:T(8,128)(2,1)S(1)}, bf16[64,768]{1,0:T(8,128)(2,1)S(1)}, u32[]{:S(2)}, u32[]{:S(2)}) %collective-permute-start.25) | collective-permute-done | bytes 98336 | tf_op jit(solution)/shard_map/ppermute | solution.py:28
  94.6 1.7 %collective-permute-done.26 = bf16[64,768]{1,0:T(8,128)(2,1)S(1)} collective-permute-done((bf16[64,768]{1,0:T(8,128)(2,1)S(1)}, bf16[64,768]{1,0:T(8,128)(2,1)S(1)}, u32[]{:S(2)}, u32[]{:S(2)}) %collective-permute-start.26) | collective-permute-done | bytes 98336 | tf_op jit(solution)/shard_map/ppermute | solution.py:28
  96.3 2.3 %collective-permute-done.27 = bf16[64,768]{1,0:T(8,128)(2,1)S(1)} collective-permute-done((bf16[64,768]{1,0:T(8,128)(2,1)S(1)}, bf16[64,768]{1,0:T(8,128)(2,1)S(1)}, u32[]{:S(2)}, u32[]{:S(2)}) %collective-permute-start.27) | collective-permute-done | bytes 98336 | tf_op jit(solution)/shard_map/ppermute | solution.py:28
  98.7 4.6 %collective-permute-start.28 = (bf16[64,384]{1,0:T(8,128)(2,1)S(1)}, bf16[64,384]{1,0:T(8,128)(2,1)S(1)}, u32[]{:S(2)}, u32[]{:S(2)}) collective-permute-start(bf16[64,384]{1,0:T(8,128)(2,1)S(1)} %get-tuple-element.24), channel_id=1, source_target_pairs={{0,96},{1,128},{2,97},{3,129},{4,64},{5,160},{6,65},{7,161},{8,0},... | collective-permute-start | bytes 147464 | tf_op jit(solution)/shard_map/ppermute | solution.py:236
  103.3 4.7 %collective-permute-done.28.a = bf16[64,384]{1,0:T(8,128)(2,1)S(1)} collective-permute-done((bf16[64,384]{1,0:T(8,128)(2,1)S(1)}, bf16[64,384]{1,0:T(8,128)(2,1)S(1)}, u32[]{:S(2)}, u32[]{:S(2)}) %collective-permute-start.28) | collective-permute-done | bytes 49184 | tf_op jit(solution)/shard_map/ppermute | solution.py:236
  108.0 6.9 %collective-permute-done.29.b = bf16[64,384]{1,0:T(8,128)(2,1)S(1)} collective-permute-done((bf16[64,384]{1,0:T(8,128)(2,1)S(1)}, bf16[64,384]{1,0:T(8,128)(2,1)S(1)}, u32[]{:S(2)}, u32[]{:S(2)}) %collective-permute-start.29) | collective-permute-done | bytes 49184 | tf_op jit(solution)/shard_map/ppermute | solution.py:236
  114.9 0.7 out.1
  (44 shorter events, 2.1 us)
Async XLA Ops:
  0.0 1.1 copy-start
  1.1 18.4 %copy-start.1 = (bf16[64,2688]{1,0:T(8,128)(2,1)}, bf16[64,2688]{1,0:T(8,128)(2,1)S(1)}, u32[]{:S(2)}) copy-start(bf16[64,2688]{1,0:T(8,128)(2,1)S(1)} %constant_dynamic-slice_fusion.2.refs_0_) | copy-start | bytes 1032196
  1.1 10.0 %collective-permute-start = (bf16[64,2688]{1,0:T(8,128)(2,1)S(1)}, bf16[64,2688]{1,0:T(8,128)(2,1)}, u32[]{:S(2)}, u32[]{:S(2)}) collective-permute-start(bf16[64,2688]{1,0:T(8,128)(2,1)S(1)} %constant_dynamic-slice_fusion.2.refs_0_), channel_id=1, source_target_pairs={{0,32},{32,64},{64,96},{96,128},{128,160},{160,192},{192,224},{224... | collective-permute-start | bytes 1032200 | tf_op jit(solution)/shard_map/ppermute | solution.py:32
  3.1 9.8 %collective-permute-start.3 = (bf16[64,2688]{1,0:T(8,128)(2,1)S(1)}, bf16[64,2688]{1,0:T(8,128)(2,1)}, u32[]{:S(2)}, u32[]{:S(2)}) collective-permute-start(bf16[64,2688]{1,0:T(8,128)(2,1)S(1)} %constant_dynamic-slice_fusion.2.refs_0_), channel_id=1, source_target_pairs={{0,224},{32,0},{64,32},{96,64},{128,96},{160,128},{192,160},{224,1... | collective-permute-start | bytes 1032200 | tf_op jit(solution)/shard_map/ppermute | solution.py:32
  3.2 1.0 copy-start.3
  4.4 13.1 %collective-permute-start.21 = (bf16[576,384]{1,0:T(8,128)(2,1)S(1)}, bf16[576,384]{1,0:T(8,128)(2,1)S(1)}, u32[]{:S(2)}, u32[]{:S(2)}) collective-permute-start(bf16[576,384]{1,0:T(8,128)(2,1)S(1)} %down.1), channel_id=1, source_target_pairs={{0,18},{16,0},{2,16},{18,2},{1,19},{17,1},{3,17},{19,3},{4,22},{20... | collective-permute-start | bytes 1327112 | tf_op jit(solution)/shard_map/ppermute | solution.py:24
  5.0 14.4 %collective-permute-start.22 = (bf16[576,384]{1,0:T(8,128)(2,1)S(1)}, bf16[576,384]{1,0:T(8,128)(2,1)S(1)}, u32[]{:S(2)}, u32[]{:S(2)}) collective-permute-start(bf16[576,384]{1,0:T(8,128)(2,1)S(1)} %down.1), channel_id=1, source_target_pairs={{0,16},{16,2},{2,18},{18,0},{1,17},{17,3},{3,19},{19,1},{4,20},{20... | collective-permute-start | bytes 1327112 | tf_op jit(solution)/shard_map/ppermute | solution.py:24
  7.7 27.7 %collective-permute-start.8 = (bf16[2,72,2688]{2,1,0:T(8,128)(2,1)S(1)}, bf16[2,72,2688]{2,1,0:T(8,128)(2,1)S(1)}, u32[]{:S(2)}, u32[]{:S(2)}) collective-permute-start(bf16[2,72,2688]{2,1,0:T(8,128)(2,1)S(1)} %pad_maximum_fusion.refs_9_), channel_id=1, source_target_pairs={{0,16},{16,2},{2,18},{18,0},{1,17},{17,3},{3,19},{19,1},{4,20},{20... | collective-permute-start | bytes 2322440 | tf_op jit(solution)/shard_map/ppermute | solution.py:24
  11.1 24.4 %collective-permute-start.9 = (bf16[2,72,2688]{2,1,0:T(8,128)(2,1)S(1)}, bf16[2,72,2688]{2,1,0:T(8,128)(2,1)S(1)}, u32[]{:S(2)}, u32[]{:S(2)}) collective-permute-start(bf16[2,72,2688]{2,1,0:T(8,128)(2,1)S(1)} %pad_maximum_fusion.refs_9_), channel_id=1, source_target_pairs={{0,18},{16,0},{2,16},{18,2},{1,19},{17,1},{3,17},{19,3},{4,22},{20... | collective-permute-start | bytes 2322440 | tf_op jit(solution)/shard_map/ppermute | solution.py:24
  12.9 34.4 %collective-permute-start.23 = (bf16[576,384]{1,0:T(8,128)(2,1)S(1)}, bf16[576,384]{1,0:T(8,128)(2,1)}, u32[]{:S(2)}, u32[]{:S(2)}) collective-permute-start(bf16[576,384]{1,0:T(8,128)(2,1)S(1)} %down.1), channel_id=1, source_target_pairs={{0,2},{16,18},{2,0},{18,16},{1,3},{17,19},{3,1},{19,17},{4,6},{20,... | collective-permute-start | bytes 1327112 | tf_op jit(solution)/shard_map/ppermute | solution.py:24
  17.6 1.9 %copy-start.4 = (bf16[576,384]{1,0:T(8,128)(2,1)}, bf16[576,384]{1,0:T(8,128)(2,1)S(1)}, u32[]{:S(2)}) copy-start(bf16[576,384]{1,0:T(8,128)(2,1)S(1)} %collective-permute-done.21) | copy-start | bytes 1327108
  17.6 9.9 %collective-permute-start.1 = (bf16[64,2688]{1,0:T(8,128)(2,1)}, bf16[64,2688]{1,0:T(8,128)(2,1)}, u32[]{:S(2)}, u32[]{:S(2)}) collective-permute-start(bf16[64,2688]{1,0:T(8,128)(2,1)} %collective-permute-done.refs_1_), channel_id=1, source_target_pairs={{0,32},{32,64},{64,96},{96,128},{128,160},{160,192},{192,224},{224... | collective-permute-start | bytes 1032200 | tf_op jit(solution)/shard_map/ppermute | solution.py:32
  19.5 0.8 copy-start.5
  20.3 9.1 %collective-permute-start.4 = (bf16[64,2688]{1,0:T(8,128)(2,1)}, bf16[64,2688]{1,0:T(8,128)(2,1)}, u32[]{:S(2)}, u32[]{:S(2)}) collective-permute-start(bf16[64,2688]{1,0:T(8,128)(2,1)} %collective-permute-done.3.refs_4_), channel_id=1, source_target_pairs={{0,224},{32,0},{64,32},{96,64},{128,96},{160,128},{192,160},{224,1... | collective-permute-start | bytes 1032200 | tf_op jit(solution)/shard_map/ppermute | solution.py:32
  24.9 34.0 %copy-start.2 = (bf16[64,2688]{1,0:T(8,128)(2,1)S(1)}, bf16[64,2688]{1,0:T(8,128)(2,1)}, u32[]{:S(2)}) copy-start(bf16[64,2688]{1,0:T(8,128)(2,1)} %copy-done.1) | copy-start | bytes 1032196
  27.4 21.2 %collective-permute-start.2 = (bf16[64,2688]{1,0:T(8,128)(2,1)}, bf16[64,2688]{1,0:T(8,128)(2,1)S(1)}, u32[]{:S(2)}, u32[]{:S(2)}) collective-permute-start(bf16[64,2688]{1,0:T(8,128)(2,1)} %collective-permute-done.1.refs_2_), channel_id=1, source_target_pairs={{0,32},{32,64},{64,96},{96,128},{128,160},{160,192},{192,224},{224... | collective-permute-start | bytes 1032200 | tf_op jit(solution)/shard_map/ppermute | solution.py:32
  29.4 21.3 %collective-permute-start.5 = (bf16[64,2688]{1,0:T(8,128)(2,1)}, bf16[64,2688]{1,0:T(8,128)(2,1)S(1)}, u32[]{:S(2)}, u32[]{:S(2)}) collective-permute-start(bf16[64,2688]{1,0:T(8,128)(2,1)} %collective-permute-done.4.refs_5_), channel_id=1, source_target_pairs={{0,224},{32,0},{64,32},{96,64},{128,96},{160,128},{192,160},{224,1... | collective-permute-start | bytes 1032200 | tf_op jit(solution)/shard_map/ppermute | solution.py:32
  35.4 17.8 %collective-permute-start.10 = (bf16[1,72,2688]{2,1,0:T(8,128)(2,1)S(1)}, bf16[1,72,2688]{2,1,0:T(8,128)(2,1)S(1)}, u32[]{:S(2)}, u32[]{:S(2)}) collective-permute-start(bf16[1,72,2688]{2,1,0:T(8,128)(2,1)S(1)} %slice.34), channel_id=1, source_target_pairs={{0,16},{16,2},{2,18},{18,0},{1,17},{17,3},{3,19},{19,1},{4,20},{20... | collective-permute-start | bytes 1161224 | tf_op jit(solution)/shard_map/ppermute | solution.py:24
  35.6 17.7 %collective-permute-start.11 = (bf16[1,72,2688]{2,1,0:T(8,128)(2,1)S(1)}, bf16[1,72,2688]{2,1,0:T(8,128)(2,1)S(1)}, u32[]{:S(2)}, u32[]{:S(2)}) collective-permute-start(bf16[1,72,2688]{2,1,0:T(8,128)(2,1)S(1)} %slice.35), channel_id=1, source_target_pairs={{0,18},{16,0},{2,16},{18,2},{1,19},{17,1},{3,17},{19,3},{4,22},{20... | collective-permute-start | bytes 1161224 | tf_op jit(solution)/shard_map/ppermute | solution.py:24
  48.5 39.9 %collective-permute-start.24 = (bf16[1152,768]{1,0:T(8,128)(2,1)S(1)}, bf16[1152,768]{1,0:T(8,128)(2,1)S(1)}, u32[]{:S(2)}, u32[]{:S(2)}) collective-permute-start(bf16[1152,768]{1,0:T(8,128)(2,1)S(1)} %maximum_maximum_fusion.refs_9_), channel_id=1, source_target_pairs={{0,1},{1,0},{2,3},{3,2},{4,5},{5,4},{6,7},{7,6},{8,9},{9,8},{10,11... | collective-permute-start | bytes 5308424 | tf_op jit(solution)/shard_map/ppermute | solution.py:36
  48.7 9.3 %collective-permute-start.6 = (bf16[32,2688]{1,0:T(8,128)(2,1)S(1)}, bf16[32,2688]{1,0:T(8,128)(2,1)S(1)}, u32[]{:S(2)}, u32[]{:S(2)}) collective-permute-start(bf16[32,2688]{1,0:T(8,128)(2,1)S(1)} %slice.32), channel_id=1, source_target_pairs={{0,32},{32,64},{64,96},{96,128},{128,160},{160,192},{192,224},{224... | collective-permute-start | bytes 516104 | tf_op jit(solution)/shard_map/ppermute | solution.py:32
  50.7 8.2 %collective-permute-start.7 = (bf16[32,2688]{1,0:T(8,128)(2,1)S(1)}, bf16[32,2688]{1,0:T(8,128)(2,1)S(1)}, u32[]{:S(2)}, u32[]{:S(2)}) collective-permute-start(bf16[32,2688]{1,0:T(8,128)(2,1)S(1)} %slice.33), channel_id=1, source_target_pairs={{0,224},{32,0},{64,32},{96,64},{128,96},{160,128},{192,160},{224,1... | collective-permute-start | bytes 516104 | tf_op jit(solution)/shard_map/ppermute | solution.py:32
  61.7 2.1 %collective-permute-start.12 = (f32[576,256]{1,0:T(8,128)S(1)}, f32[576,256]{1,0:T(8,128)S(1)}, u32[]{:S(2)}, u32[]{:S(2)}) collective-permute-start(f32[576,256]{1,0:T(8,128)S(1)} %get-tuple-element.14), channel_id=1, source_target_pairs={{0,1},{1,0},{2,3},{3,2},{4,5},{5,4},{6,7},{7,6},{8,9},{9,8},{10,11... | collective-permute-start | bytes 1769480 | tf_op jit(solution)/shard_map/ppermute | solution.py:36
  64.0 12.5 %collective-permute-start.14 = (bf16[288,256]{1,0:T(8,128)(2,1)S(1)}, bf16[288,256]{1,0:T(8,128)(2,1)S(1)}, u32[]{:S(2)}, u32[]{:S(2)}) collective-permute-start(bf16[288,256]{1,0:T(8,128)(2,1)S(1)} %fusion.refs_0_), channel_id=1, source_target_pairs={{0,64},{32,96},{64,128},{96,160},{128,192},{160,224},{192,0},{224,... | collective-permute-start | bytes 442376 | tf_op jit(solution)/shard_map/ppermute | solution.py:32
  69.2 9.4 %collective-permute-start.17 = (bf16[288,256]{1,0:T(8,128)(2,1)S(1)}, bf16[288,256]{1,0:T(8,128)(2,1)S(1)}, u32[]{:S(2)}, u32[]{:S(2)}) collective-permute-start(bf16[288,256]{1,0:T(8,128)(2,1)S(1)} %fusion.refs_0_), channel_id=1, source_target_pairs={{0,192},{32,224},{64,0},{96,32},{128,64},{160,96},{192,128},{224,1... | collective-permute-start | bytes 442376 | tf_op jit(solution)/shard_map/ppermute | solution.py:32
  69.2 9.7 %collective-permute-start.13 = (bf16[288,256]{1,0:T(8,128)(2,1)S(1)}, bf16[288,256]{1,0:T(8,128)(2,1)S(1)}, u32[]{:S(2)}, u32[]{:S(2)}) collective-permute-start(bf16[288,256]{1,0:T(8,128)(2,1)S(1)} %fusion.refs_0_), channel_id=1, source_target_pairs={{0,32},{32,64},{64,96},{96,128},{128,160},{160,192},{192,224},{224... | collective-permute-start | bytes 442376 | tf_op jit(solution)/shard_map/ppermute | solution.py:32
  69.7 12.9 %collective-permute-start.16 = (bf16[288,256]{1,0:T(8,128)(2,1)S(1)}, bf16[288,256]{1,0:T(8,128)(2,1)S(1)}, u32[]{:S(2)}, u32[]{:S(2)}) collective-permute-start(bf16[288,256]{1,0:T(8,128)(2,1)S(1)} %fusion.refs_0_), channel_id=1, source_target_pairs={{0,224},{32,0},{64,32},{96,64},{128,96},{160,128},{192,160},{224,1... | collective-permute-start | bytes 442376 | tf_op jit(solution)/shard_map/ppermute | solution.py:32
  76.5 12.0 %collective-permute-start.15 = (bf16[288,256]{1,0:T(8,128)(2,1)S(1)}, bf16[288,256]{1,0:T(8,128)(2,1)S(1)}, u32[]{:S(2)}, u32[]{:S(2)}) collective-permute-start(bf16[288,256]{1,0:T(8,128)(2,1)S(1)} %collective-permute-done.14.refs_2_), channel_id=1, source_target_pairs={{0,32},{32,64},{64,96},{96,128},{128,160},{160,192},{192,224},{224... | collective-permute-start | bytes 442376 | tf_op jit(solution)/shard_map/ppermute | solution.py:32
  78.6 9.9 %collective-permute-start.18 = (bf16[288,256]{1,0:T(8,128)(2,1)S(1)}, bf16[288,256]{1,0:T(8,128)(2,1)S(1)}, u32[]{:S(2)}, u32[]{:S(2)}) collective-permute-start(bf16[288,256]{1,0:T(8,128)(2,1)S(1)} %collective-permute-done.17.refs_5_), channel_id=1, source_target_pairs={{0,224},{32,0},{64,32},{96,64},{128,96},{160,128},{192,160},{224,1... | collective-permute-start | bytes 442376 | tf_op jit(solution)/shard_map/ppermute | solution.py:32
  78.9 7.3 %collective-permute-start.19 = (bf16[144,256]{1,0:T(8,128)(2,1)S(1)}, bf16[144,256]{1,0:T(8,128)(2,1)S(1)}, u32[]{:S(2)}, u32[]{:S(2)}) collective-permute-start(bf16[144,256]{1,0:T(8,128)(2,1)S(1)} %slice.38), channel_id=1, source_target_pairs={{0,64},{32,96},{64,128},{96,160},{128,192},{160,224},{192,0},{224,... | collective-permute-start | bytes 221192 | tf_op jit(solution)/shard_map/ppermute | solution.py:32
  82.6 5.8 %collective-permute-start.20 = (bf16[144,256]{1,0:T(8,128)(2,1)S(1)}, bf16[144,256]{1,0:T(8,128)(2,1)S(1)}, u32[]{:S(2)}, u32[]{:S(2)}) collective-permute-start(bf16[144,256]{1,0:T(8,128)(2,1)S(1)} %slice.39), channel_id=1, source_target_pairs={{0,192},{32,224},{64,0},{96,32},{128,64},{160,96},{192,128},{224,1... | collective-permute-start | bytes 221192 | tf_op jit(solution)/shard_map/ppermute | solution.py:32
  89.9 4.7 %collective-permute-start.25 = (bf16[64,768]{1,0:T(8,128)(2,1)S(1)}, bf16[64,768]{1,0:T(8,128)(2,1)S(1)}, u32[]{:S(2)}, u32[]{:S(2)}) collective-permute-start(bf16[64,768]{1,0:T(8,128)(2,1)S(1)} %get-tuple-element.16), channel_id=1, source_target_pairs={{0,4},{4,8},{8,12},{12,0},{1,5},{5,9},{9,13},{13,1},{2,6},{6,10},{... | collective-permute-start | bytes 294920 | tf_op jit(solution)/shard_map/ppermute | solution.py:28
  90.2 6.1 %collective-permute-start.26 = (bf16[64,768]{1,0:T(8,128)(2,1)S(1)}, bf16[64,768]{1,0:T(8,128)(2,1)S(1)}, u32[]{:S(2)}, u32[]{:S(2)}) collective-permute-start(bf16[64,768]{1,0:T(8,128)(2,1)S(1)} %get-tuple-element.17), channel_id=1, source_target_pairs={{0,8},{4,12},{8,0},{12,4},{1,9},{5,13},{9,1},{13,5},{2,10},{6,14},... | collective-permute-start | bytes 294920 | tf_op jit(solution)/shard_map/ppermute | solution.py:28
  92.7 5.8 %collective-permute-start.27 = (bf16[64,768]{1,0:T(8,128)(2,1)S(1)}, bf16[64,768]{1,0:T(8,128)(2,1)S(1)}, u32[]{:S(2)}, u32[]{:S(2)}) collective-permute-start(bf16[64,768]{1,0:T(8,128)(2,1)S(1)} %get-tuple-element.18), channel_id=1, source_target_pairs={{0,12},{4,0},{8,4},{12,8},{1,13},{5,1},{9,5},{13,9},{2,14},{6,2},{... | collective-permute-start | bytes 294920 | tf_op jit(solution)/shard_map/ppermute | solution.py:28
  98.7 9.3 %collective-permute-start.28 = (bf16[64,384]{1,0:T(8,128)(2,1)S(1)}, bf16[64,384]{1,0:T(8,128)(2,1)S(1)}, u32[]{:S(2)}, u32[]{:S(2)}) collective-permute-start(bf16[64,384]{1,0:T(8,128)(2,1)S(1)} %get-tuple-element.24), channel_id=1, source_target_pairs={{0,96},{1,128},{2,97},{3,129},{4,64},{5,160},{6,65},{7,161},{8,0},... | collective-permute-start | bytes 147464 | tf_op jit(solution)/shard_map/ppermute | solution.py:236
  103.3 11.6 %collective-permute-start.29 = (bf16[64,384]{1,0:T(8,128)(2,1)S(1)}, bf16[64,384]{1,0:T(8,128)(2,1)S(1)}, u32[]{:S(2)}, u32[]{:S(2)}) collective-permute-start(bf16[64,384]{1,0:T(8,128)(2,1)S(1)} %get-tuple-element.23), channel_id=1, source_target_pairs={{0,97},{1,129},{2,96},{3,128},{4,65},{5,161},{6,64},{7,160},{8,1},... | collective-permute-start | bytes 147464 | tf_op jit(solution)/shard_map/ppermute | solution.py:236

commit v5 on v4

--- a/solution.py
+++ b/solution.py
@@ -82,36 +82,39 @@
     return src // 4 ^ c, lax.rem(src, 4)
 
 
-def first_kernel(*refs):
-    blocks, (u4, d4), weights = refs[:7], refs[7:9], refs[9:14]
-    send, tok, wts, far_tok = refs[14:]
-    z, xl, c, xh = (lax.axis_index(a) for a in ("z", "xl", "c", "xh"))
-    n, units = blocks[0].shape[0], weights[3].shape[1]
-
-    def put(off, lo, rows):
-        half, at = place(z, c, off)
-        at = pl.multiple_of(at * n + lo, n // 2)
-
-        @pl.when(half == 0)
+def write_rows(near, far, off, lo, rows):
+    n = near.shape[0] // 4
+    half, at = place(lax.axis_index("z"), lax.axis_index("c"), off)
+    at = pl.multiple_of(at * n + lo, n // 2)
+    for which, dst in enumerate((near, far)):
+        @pl.when(half == which)
         def _():
-            tok[pl.ds(at, rows.shape[0]), :] = rows[...]
-
-        @pl.when(half != 0)
-        def _():
-            far_tok[pl.ds(at, rows.shape[0]), :] = rows[...]
-
+            dst[pl.ds(at, rows.shape[0]), :] = rows[...]
+
+
+def unit_slot(off):
+    xl, xh = lax.axis_index("xl"), lax.axis_index("xh")
+    src = lax.rem(xh * 2 + xl + off + 4, 4)
+    return (src // 2 ^ xh) * 2 + lax.rem(src, 2)
+
+
+def gather_kernel(*refs):
+    blocks, weights, (near, far, wts) = refs[:7], refs[7:10], refs[10:]
+    units = weights[0].shape[1]
     for block, off in zip(blocks, OFFSETS):
-        put(off, 0, block)
-    for i, part in enumerate((u4, d4)):
-        put(4, i * n // 2, part)
-    w, w_m1, w_p1, g2, u2 = weights
-    for (gate, up), off in zip(((w.at[0], w.at[1]), (w_m1.at[0], w_m1.at[1]), (w_p1.at[0], w_p1.at[1]), (g2.at[0], u2.at[0])),
-                               (0, -1, 1, 2)):
-        src = lax.rem(xh * 2 + xl + off + 4, 4)
-        dst = (src // 2 ^ xh) * 2 + lax.rem(src, 2)
-        wts[dst, :units, :] = gate[...]
-        wts[dst, units:, :] = up[...]
-    half_product(far_tok, wts, send)
+        write_rows(near, far, off, 0, block)
+    for w, off in zip(weights, (0, -1, 1)):
+        for i in range(2):
+            wts[unit_slot(off), i * units:(i + 1) * units, :] = w[i]
+
+
+def first_kernel(u4, d4, gate, up, near_in, far_in, wts_in, send, near, far, wts):
+    units = gate.shape[1]
+    for i, rows in enumerate((u4, d4)):
+        write_rows(near, far, 4, i * rows.shape[0], rows)
+    for i, w in enumerate((gate, up)):
+        wts[unit_slot(2), i * units:(i + 1) * units, :] = w[0]
+    half_product(far, wts, send)
 
 
 def out_kernel(a, b, out):
@@ -194,16 +197,26 @@
 
         m, t = 8 * units, Z * n
         half = jax.ShapeDtypeStruct((m, t // 2), jnp.float32)
-        send, tok, wts = pl.pallas_call(
+        token_half, blocks = jax.ShapeDtypeStruct((t // 2, k), bf16), jax.ShapeDtypeStruct((4, 2 * units, k), bf16)
+        placed = pl.pallas_call(
+            gather_kernel,
+            out_shape=(token_half, token_half, blocks),
+            in_specs=[VMEM] * 10,
+            out_specs=(VMEM,) * 3,
+            compiler_params=pltpu.CompilerParams(vmem_limit_bytes=4 << 20),
+            cost_estimate=pl.CostEstimate(flops=10**8, bytes_accessed=6 << 20, transcendentals=0),
+            name="gather",
+        )(*toks[:7], *weights[:3])
+        send, tok, _, wts = pl.pallas_call(
             first_kernel,
-            out_shape=(half, jax.ShapeDtypeStruct((t // 2, k), bf16), jax.ShapeDtypeStruct((4, 2 * units, k), bf16)),
-            in_specs=[VMEM] * 14,
-            out_specs=(VMEM,) * 3,
-            scratch_shapes=[pltpu.VMEM((t // 2, k), bf16)],
-            compiler_params=pltpu.CompilerParams(vmem_limit_bytes=12 << 20),
+            out_shape=(half, token_half, token_half, blocks),
+            in_specs=[VMEM] * 7,
+            out_specs=(VMEM,) * 4,
+            input_output_aliases={4: 1, 5: 2, 6: 3},
+            compiler_params=pltpu.CompilerParams(vmem_limit_bytes=8 << 20),
             cost_estimate=pl.CostEstimate(flops=m * t * k, bytes_accessed=2 * k * (m + t), transcendentals=0),
             name="first",
-        )(*toks, *weights)
+        )(*toks[7:], *weights[3:], *placed)
         keep = pl.pallas_call(
             half_product,
             out_shape=half,

time: 116 us -> 114 us (0.983)
  waiting for transfers between devices: 49.3 us -> 44.8 us
  starting transfers between devices: 53.1 us -> 56 us
    ppermute x16, waiting for transfers between devices: 24.8 us -> 20.6 us  [pz(): return lax.ppermute(v, 'z', ring(Z, k))]
    ppermute x1, starting transfers between devices: 4.61 us -> 7.5 us  [body(): lax.ppermute(mine, final_axes, final_perms[0])]
    ppermute x1, waiting for transfers between devices: 4.69 us -> 1.85 us  [body(): lax.ppermute(mine, final_axes, final_perms[0])]
    ppermute x1, waiting for transfers between devices: 6.92 us -> 9.76 us  [body(): lax.ppermute(other, final_axes, final_perms[1])]
    pallas_call x1 -> x2, Pallas kernels: 2.8 us -> 2.82 us  [the longest x1 1.75 us: body(): pl.pallas_call(gather_kernel, out_shape=(token_half, token_half, blocks),...]
    unnamed x12 -> x14, local copies, waits for them, and re-layouts: 2.88 us -> 2.88 us
  transfers between devices with their start and end apart: 30 -> 30, of which waited for: 19 -> 20; matrix products, arithmetic and copies ran while one was open for 3% -> 3% of each run, Pallas kernels for 3% -> 4%
where the time goes in v5:
time: 114 us
  starting transfers between devices  56 us (49%)
  waiting for transfers between devices  44.8 us (39%)
  Pallas kernels  6.16 us (5%)
  other arithmetic  3.73 us (3%)
  local copies, waits for them, and re-layouts  3.07 us (3%)
    ppermute x16, starting transfers between devices, pz(): return lax.ppermute(v, 'z', ring(Z, k))  27.4 us
    ppermute x16, waiting for transfers between devices, pz(): return lax.ppermute(v, 'z', ring(Z, k))  20.6 us
    ppermute x7, starting transfers between devices, px(): return lax.ppermute(v, ('xl', 'xh'), x_ring(k))  18 us
    ppermute x1, waiting for transfers between devices, body(): lax.ppermute(other, final_axes, final_perms[1])  9.76 us
    ppermute x1, starting transfers between devices, body(): lax.ppermute(mine, final_axes, final_perms[0])  7.5 us
    ppermute x7, waiting for transfers between devices, px(): return lax.ppermute(v, ('xl', 'xh'), x_ring(k))  5.86 us
    ppermute x3, waiting for transfers between devices, py(): return lax.ppermute(v, 'y', ring(Y, k))  5.82 us
    ppermute x3, starting transfers between devices, py(): return lax.ppermute(v, 'y', ring(Y, k))  2.89 us
  transfers between devices with their start and end apart: 30, of which 20 were waited for; matrix products, arithmetic and copies ran while one was open for 3% of the time, Pallas kernels for 4%

profile of v5, /device:TPU:58, one launch (start us, length us, event | category | flops | bytes accessed | tf_op | source)
XLA Modules:
  0.0 114.0 jit_solution(8022905061892634861)
XLA Ops:
  0.0 1.1 copy-done
  1.1 2.0 %collective-permute-start = (bf16[64,2688]{1,0:T(8,128)(2,1)S(1)}, bf16[64,2688]{1,0:T(8,128)(2,1)}, u32[]{:S(2)}, u32[]{:S(2)}) collective-permute-start(bf16[64,2688]{1,0:T(8,128)(2,1)S(1)} %constant_dynamic-slice_fusion.2.refs_0_), channel_id=1, source_target_pairs={{0,32},{32,64},{64,96},{96,128},{128,160},{160,192},{192,224},{224... | collective-permute-start | bytes 1032200 | tf_op jit(solution)/shard_map/ppermute | solution.py:32
  3.2 1.0 copy-done.3
  4.4 0.6 collective-permute-start.21
  5.0 1.5 %collective-permute-start.22 = (bf16[576,384]{1,0:T(8,128)(2,1)S(1)}, bf16[576,384]{1,0:T(8,128)(2,1)S(1)}, u32[]{:S(2)}, u32[]{:S(2)}) collective-permute-start(bf16[576,384]{1,0:T(8,128)(2,1)S(1)} %down.1), channel_id=1, source_target_pairs={{0,16},{16,2},{2,18},{18,0},{1,17},{17,3},{3,19},{19,1},{4,20},{20... | collective-permute-start | bytes 1327112 | tf_op jit(solution)/shard_map/ppermute | solution.py:24
  6.5 1.1 pad_maximum_fusion.refs_7_
  7.6 1.3 %collective-permute-start.10 = (bf16[2,72,2688]{2,1,0:T(8,128)(2,1)S(1)}, bf16[2,72,2688]{2,1,0:T(8,128)(2,1)S(1)}, u32[]{:S(2)}, u32[]{:S(2)}) collective-permute-start(bf16[2,72,2688]{2,1,0:T(8,128)(2,1)S(1)} %pad_maximum_fusion.refs_7_), channel_id=1, source_target_pairs={{0,18},{16,0},{2,16},{18,2},{1,19},{17,1},{3,17},{19,3},{4,22},{20... | collective-permute-start | bytes 2322440 | tf_op jit(solution)/shard_map/ppermute | solution.py:24
  9.0 2.2 %collective-permute-done.refs_1_ = bf16[64,2688]{1,0:T(8,128)(2,1)} collective-permute-done((bf16[64,2688]{1,0:T(8,128)(2,1)S(1)}, bf16[64,2688]{1,0:T(8,128)(2,1)}, u32[]{:S(2)}, u32[]{:S(2)}) %collective-permute-start) | collective-permute-done | bytes 344096 | tf_op jit(solution)/shard_map/ppermute | solution.py:32
  11.1 1.5 %collective-permute-start.8 = (bf16[2,72,2688]{2,1,0:T(8,128)(2,1)S(1)}, bf16[2,72,2688]{2,1,0:T(8,128)(2,1)S(1)}, u32[]{:S(2)}, u32[]{:S(2)}) collective-permute-start(bf16[2,72,2688]{2,1,0:T(8,128)(2,1)S(1)} %pad_maximum_fusion.refs_7_), channel_id=1, source_target_pairs={{0,16},{16,2},{2,18},{18,0},{1,17},{17,3},{3,19},{19,1},{4,20},{20... | collective-permute-start | bytes 2322440 | tf_op jit(solution)/shard_map/ppermute | solution.py:24
  12.9 2.1 %collective-permute-start.23 = (bf16[576,384]{1,0:T(8,128)(2,1)S(1)}, bf16[576,384]{1,0:T(8,128)(2,1)}, u32[]{:S(2)}, u32[]{:S(2)}) collective-permute-start(bf16[576,384]{1,0:T(8,128)(2,1)S(1)} %down.1), channel_id=1, source_target_pairs={{0,2},{16,18},{2,0},{18,16},{1,3},{17,19},{3,1},{19,17},{4,6},{20,... | collective-permute-start | bytes 1327112 | tf_op jit(solution)/shard_map/ppermute | solution.py:24
  15.1 2.5 %collective-permute-done.21 = bf16[576,384]{1,0:T(8,128)(2,1)S(1)} collective-permute-done((bf16[576,384]{1,0:T(8,128)(2,1)S(1)}, bf16[576,384]{1,0:T(8,128)(2,1)S(1)}, u32[]{:S(2)}, u32[]{:S(2)}) %collective-permute-start.21) | collective-permute-done | bytes 442400 | tf_op jit(solution)/shard_map/ppermute | solution.py:24
  17.6 1.9 %collective-permute-start.1 = (bf16[64,2688]{1,0:T(8,128)(2,1)}, bf16[64,2688]{1,0:T(8,128)(2,1)}, u32[]{:S(2)}, u32[]{:S(2)}) collective-permute-start(bf16[64,2688]{1,0:T(8,128)(2,1)} %collective-permute-done.refs_1_), channel_id=1, source_target_pairs={{0,32},{32,64},{64,96},{96,128},{128,160},{160,192},{192,224},{224... | collective-permute-start | bytes 1032200 | tf_op jit(solution)/shard_map/ppermute | solution.py:32
  19.5 0.8 copy-done.5
  20.3 3.4 %collective-permute-start.5 = (bf16[64,2688]{1,0:T(8,128)(2,1)}, bf16[64,2688]{1,0:T(8,128)(2,1)}, u32[]{:S(2)}, u32[]{:S(2)}) collective-permute-start(bf16[64,2688]{1,0:T(8,128)(2,1)} %collective-permute-done.4.refs_4_), channel_id=1, source_target_pairs={{0,224},{32,0},{64,32},{96,64},{128,96},{160,128},{192,160},{224,1... | collective-permute-start | bytes 1032200 | tf_op jit(solution)/shard_map/ppermute | solution.py:32
  23.6 1.2 %broadcast_select_fusion.1 = (bf16[576,384]{1,0:T(8,128)(2,1)S(1)}, bf16[576,384]{1,0:T(8,128)(2,1)S(1)}) fusion(bf16[576,384]{1,0:T(8,128)(2,1)} %copy-done.4, bf16[576,384]{1,0:T(8,128)(2,1)} %copy-done.5, pred[]{:T(512)S(6)} %eq.4), kind=kLoop, calls=%fused_computation.3 | loop fusion | flops 442368 | bytes 1769473 | tf_op jit(solution)/shard_map/jit(_where)/select_n | solution.py:194
  24.9 2.5 %collective-permute-done.1.refs_2_ = bf16[64,2688]{1,0:T(8,128)(2,1)} collective-permute-done((bf16[64,2688]{1,0:T(8,128)(2,1)}, bf16[64,2688]{1,0:T(8,128)(2,1)}, u32[]{:S(2)}, u32[]{:S(2)}) %collective-permute-start.1) | collective-permute-done | bytes 344096 | tf_op jit(solution)/shard_map/ppermute | solution.py:32
  27.4 0.6 collective-permute-start.2
  28.1 1.3 %collective-permute-done.5.refs_5_ = bf16[64,2688]{1,0:T(8,128)(2,1)} collective-permute-done((bf16[64,2688]{1,0:T(8,128)(2,1)}, bf16[64,2688]{1,0:T(8,128)(2,1)}, u32[]{:S(2)}, u32[]{:S(2)}) %collective-permute-start.5) | collective-permute-done | bytes 344096 | tf_op jit(solution)/shard_map/ppermute | solution.py:32
  29.4 2.5 %collective-permute-start.6 = (bf16[64,2688]{1,0:T(8,128)(2,1)}, bf16[64,2688]{1,0:T(8,128)(2,1)S(1)}, u32[]{:S(2)}, u32[]{:S(2)}) collective-permute-start(bf16[64,2688]{1,0:T(8,128)(2,1)} %collective-permute-done.5.refs_5_), channel_id=1, source_target_pairs={{0,224},{32,0},{64,32},{96,64},{128,96},{160,128},{192,160},{224,1... | collective-permute-start | bytes 1032200 | tf_op jit(solution)/shard_map/ppermute | solution.py:32
  31.9 1.4 %collective-permute-done.10.refs_9_ = bf16[2,72,2688]{2,1,0:T(8,128)(2,1)S(1)} collective-permute-done((bf16[2,72,2688]{2,1,0:T(8,128)(2,1)S(1)}, bf16[2,72,2688]{2,1,0:T(8,128)(2,1)S(1)}, u32[]{:S(2)}, u32[]{:S(2)}) %collective-permute-start.10) | collective-permute-done | bytes 774176 | tf_op jit(solution)/shard_map/ppermute | solution.py:24
  33.2 10.8 %collective-permute-start.11 = (bf16[1,72,2688]{2,1,0:T(8,128)(2,1)S(1)}, bf16[1,72,2688]{2,1,0:T(8,128)(2,1)S(1)}, u32[]{:S(2)}, u32[]{:S(2)}) collective-permute-start(bf16[1,72,2688]{2,1,0:T(8,128)(2,1)S(1)} %slice.35), channel_id=1, source_target_pairs={{0,18},{16,0},{2,16},{18,2},{1,19},{17,1},{3,17},{19,3},{4,22},{20... | collective-permute-start | bytes 1161224 | tf_op jit(solution)/shard_map/ppermute | solution.py:24
  44.7 1.2 %maximum_maximum_fusion.refs_9_ = bf16[1152,768]{1,0:T(8,128)(2,1)S(1)} fusion(bf16[576,384]{1,0:T(8,128)(2,1)S(1)} %get-tuple-element.26, bf16[576,384]{1,0:T(8,128)(2,1)} %collective-permute-done.23, bf16[576,384]{1,0:T(8,128)(2,1)S(1)} %get-tuple-element.25, bf16[576,384]{1,0:T(8,128)(2,1)S(1)} %down.1), kind=kLoop, calls=%fused_computation | loop fusion | flops 7077888 | bytes 3538944 | tf_op jit(solution)/shard_map/concatenate | solution.py:195
  46.0 2.0 %collective-permute-start.3 = (bf16[32,2688]{1,0:T(8,128)(2,1)S(1)}, bf16[32,2688]{1,0:T(8,128)(2,1)S(1)}, u32[]{:S(2)}, u32[]{:S(2)}) collective-permute-start(bf16[32,2688]{1,0:T(8,128)(2,1)S(1)} %slice.32), channel_id=1, source_target_pairs={{0,32},{32,64},{64,96},{96,128},{128,160},{160,192},{192,224},{224... | collective-permute-start | bytes 516104 | tf_op jit(solution)/shard_map/ppermute | solution.py:32
  48.1 2.4 %collective-permute-start.7 = (bf16[32,2688]{1,0:T(8,128)(2,1)S(1)}, bf16[32,2688]{1,0:T(8,128)(2,1)S(1)}, u32[]{:S(2)}, u32[]{:S(2)}) collective-permute-start(bf16[32,2688]{1,0:T(8,128)(2,1)S(1)} %slice.33), channel_id=1, source_target_pairs={{0,224},{32,0},{64,32},{96,64},{128,96},{160,128},{192,160},{224,1... | collective-permute-start | bytes 516104 | tf_op jit(solution)/shard_map/ppermute | solution.py:32
  50.5 1.7 %gather.1 = (bf16[256,2688]{1,0:T(8,128)(2,1)S(1)}, bf16[256,2688]{1,0:T(8,128)(2,1)S(1)}, bf16[4,144,2688]{2,1,0:T(8,128)(2,1)S(1)}) custom-call(bf16[64,2688]{1,0:T(8,128)(2,1)S(1)} %copy-done.2, bf16[64,2688]{1,0:T(8,128)(2,1)} %collective-permute-done.refs_1_, bf16[64,2688]{1,0:T(8,128)(2,1)} %collective-permute-done.1.refs_2_, ...), custom_call_target="tpu_custom_call" | custom-call | flops 100000000 | bytes 6291456 | tf_op jit(solution)/shard_map/gather/pallas_call | solution.py:201
  52.2 1.5 %collective-permute-done.9.gate = bf16[1,72,2688]{2,1,0:T(8,128)(2,1)S(1)} collective-permute-done((bf16[1,72,2688]{2,1,0:T(8,128)(2,1)S(1)}, bf16[1,72,2688]{2,1,0:T(8,128)(2,1)S(1)}, u32[]{:S(2)}, u32[]{:S(2)}) %collective-permute-start.9) | collective-permute-done | bytes 387104 | tf_op jit(solution)/shard_map/ppermute | solution.py:24
  53.7 1.5 %collective-permute-done.3.u4 = bf16[32,2688]{1,0:T(8,128)(2,1)S(1)} collective-permute-done((bf16[32,2688]{1,0:T(8,128)(2,1)S(1)}, bf16[32,2688]{1,0:T(8,128)(2,1)S(1)}, u32[]{:S(2)}, u32[]{:S(2)}) %collective-permute-start.3) | collective-permute-done | bytes 172064 | tf_op jit(solution)/shard_map/ppermute | solution.py:32
  55.2 0.9 collective-permute-done.7.d4
  56.1 1.1 first.1
  57.3 1.0 keep.1
  58.3 0.9 collective-permute-done.12
  59.5 5.7 %collective-permute-start.14 = (bf16[288,256]{1,0:T(8,128)(2,1)S(1)}, bf16[288,256]{1,0:T(8,128)(2,1)S(1)}, u32[]{:S(2)}, u32[]{:S(2)}) collective-permute-start(bf16[288,256]{1,0:T(8,128)(2,1)S(1)} %fusion.refs_0_), channel_id=1, source_target_pairs={{0,64},{32,96},{64,128},{96,160},{128,192},{160,224},{192,0},{224,... | collective-permute-start | bytes 442376 | tf_op jit(solution)/shard_map/ppermute | solution.py:32
  65.7 1.5 %collective-permute-start.16 = (bf16[288,256]{1,0:T(8,128)(2,1)S(1)}, bf16[288,256]{1,0:T(8,128)(2,1)S(1)}, u32[]{:S(2)}, u32[]{:S(2)}) collective-permute-start(bf16[288,256]{1,0:T(8,128)(2,1)S(1)} %fusion.refs_0_), channel_id=1, source_target_pairs={{0,224},{32,0},{64,32},{96,64},{128,96},{160,128},{192,160},{224,1... | collective-permute-start | bytes 442376 | tf_op jit(solution)/shard_map/ppermute | solution.py:32
  67.2 4.9 %collective-permute-done.14.refs_2_ = bf16[288,256]{1,0:T(8,128)(2,1)S(1)} collective-permute-done((bf16[288,256]{1,0:T(8,128)(2,1)S(1)}, bf16[288,256]{1,0:T(8,128)(2,1)S(1)}, u32[]{:S(2)}, u32[]{:S(2)}) %collective-permute-start.14) | collective-permute-done | bytes 147488 | tf_op jit(solution)/shard_map/ppermute | solution.py:32
  72.7 2.4 %collective-permute-done.17.refs_5_ = bf16[288,256]{1,0:T(8,128)(2,1)S(1)} collective-permute-done((bf16[288,256]{1,0:T(8,128)(2,1)S(1)}, bf16[288,256]{1,0:T(8,128)(2,1)S(1)}, u32[]{:S(2)}, u32[]{:S(2)}) %collective-permute-start.17) | collective-permute-done | bytes 147488 | tf_op jit(solution)/shard_map/ppermute | solution.py:32
  75.1 3.0 %collective-permute-start.19 = (bf16[144,256]{1,0:T(8,128)(2,1)S(1)}, bf16[144,256]{1,0:T(8,128)(2,1)S(1)}, u32[]{:S(2)}, u32[]{:S(2)}) collective-permute-start(bf16[144,256]{1,0:T(8,128)(2,1)S(1)} %slice.38), channel_id=1, source_target_pairs={{0,64},{32,96},{64,128},{96,160},{128,192},{160,224},{192,0},{224,... | collective-permute-start | bytes 221192 | tf_op jit(solution)/shard_map/ppermute | solution.py:32
  78.1 1.2 %collective-permute-start.20 = (bf16[144,256]{1,0:T(8,128)(2,1)S(1)}, bf16[144,256]{1,0:T(8,128)(2,1)S(1)}, u32[]{:S(2)}, u32[]{:S(2)}) collective-permute-start(bf16[144,256]{1,0:T(8,128)(2,1)S(1)} %slice.39), channel_id=1, source_target_pairs={{0,192},{32,224},{64,0},{96,32},{128,64},{160,96},{192,128},{224,1... | collective-permute-start | bytes 221192 | tf_op jit(solution)/shard_map/ppermute | solution.py:32
  79.3 2.7 %collective-permute-done.19.refs_7_ = bf16[144,256]{1,0:T(8,128)(2,1)S(1)} collective-permute-done((bf16[144,256]{1,0:T(8,128)(2,1)S(1)}, bf16[144,256]{1,0:T(8,128)(2,1)S(1)}, u32[]{:S(2)}, u32[]{:S(2)}) %collective-permute-start.19) | collective-permute-done | bytes 73760 | tf_op jit(solution)/shard_map/ppermute | solution.py:32
  82.0 1.9 %collective-permute-done.20.refs_8_ = bf16[144,256]{1,0:T(8,128)(2,1)S(1)} collective-permute-done((bf16[144,256]{1,0:T(8,128)(2,1)S(1)}, bf16[144,256]{1,0:T(8,128)(2,1)S(1)}, u32[]{:S(2)}, u32[]{:S(2)}) %collective-permute-start.20) | collective-permute-done | bytes 73760 | tf_op jit(solution)/shard_map/ppermute | solution.py:32
  83.9 1.4 %second.1 = (bf16[64,768]{1,0:T(8,128)(2,1)S(1)}, bf16[64,768]{1,0:T(8,128)(2,1)S(1)}, bf16[64,768]{1,0:T(8,128)(2,1)S(1)}, bf16[64,768]{1,0:T(8,128)(2,1)S(1)}) custom-call(bf16[288,256]{1,0:T(8,128)(2,1)S(1)} %fusion.refs_0_, bf16[288,256]{1,0:T(8,128)(2,1)S(1)} %collective-permute-done.13.refs_1_, bf16[288,256]{1,0:T(8,128)(2,1)S(1)} %collective-permute-done.14.refs_2_, ...), custom_call_target="tpu_custom_call" | custom-call | flops 905969664 | bytes 6291456 | tf_op jit(solution)/shard_map/second/pallas_call | solution.py:235
  85.6 2.6 %collective-permute-start.26 = (bf16[64,768]{1,0:T(8,128)(2,1)S(1)}, bf16[64,768]{1,0:T(8,128)(2,1)S(1)}, u32[]{:S(2)}, u32[]{:S(2)}) collective-permute-start(bf16[64,768]{1,0:T(8,128)(2,1)S(1)} %get-tuple-element.23), channel_id=1, source_target_pairs={{0,8},{4,12},{8,0},{12,4},{1,9},{5,13},{9,1},{13,5},{2,10},{6,14},... | collective-permute-start | bytes 294920 | tf_op jit(solution)/shard_map/ppermute | solution.py:28
  88.2 1.8 %collective-permute-done.25 = bf16[64,768]{1,0:T(8,128)(2,1)S(1)} collective-permute-done((bf16[64,768]{1,0:T(8,128)(2,1)S(1)}, bf16[64,768]{1,0:T(8,128)(2,1)S(1)}, u32[]{:S(2)}, u32[]{:S(2)}) %collective-permute-start.25) | collective-permute-done | bytes 98336 | tf_op jit(solution)/shard_map/ppermute | solution.py:28
  90.0 1.7 %collective-permute-done.26 = bf16[64,768]{1,0:T(8,128)(2,1)S(1)} collective-permute-done((bf16[64,768]{1,0:T(8,128)(2,1)S(1)}, bf16[64,768]{1,0:T(8,128)(2,1)S(1)}, u32[]{:S(2)}, u32[]{:S(2)}) %collective-permute-start.26) | collective-permute-done | bytes 98336 | tf_op jit(solution)/shard_map/ppermute | solution.py:28
  91.8 2.3 %collective-permute-done.27 = bf16[64,768]{1,0:T(8,128)(2,1)S(1)} collective-permute-done((bf16[64,768]{1,0:T(8,128)(2,1)S(1)}, bf16[64,768]{1,0:T(8,128)(2,1)S(1)}, u32[]{:S(2)}, u32[]{:S(2)}) %collective-permute-start.27) | collective-permute-done | bytes 98336 | tf_op jit(solution)/shard_map/ppermute | solution.py:28
  94.1 7.5 %collective-permute-start.28 = (bf16[64,384]{1,0:T(8,128)(2,1)S(1)}, bf16[64,384]{1,0:T(8,128)(2,1)S(1)}, u32[]{:S(2)}, u32[]{:S(2)}) collective-permute-start(bf16[64,384]{1,0:T(8,128)(2,1)S(1)} %get-tuple-element.30), channel_id=1, source_target_pairs={{0,96},{1,128},{2,97},{3,129},{4,64},{5,160},{6,65},{7,161},{8,0},... | collective-permute-start | bytes 147464 | tf_op jit(solution)/shard_map/ppermute | solution.py:249
  101.6 1.8 %collective-permute-done.28.a = bf16[64,384]{1,0:T(8,128)(2,1)S(1)} collective-permute-done((bf16[64,384]{1,0:T(8,128)(2,1)S(1)}, bf16[64,384]{1,0:T(8,128)(2,1)S(1)}, u32[]{:S(2)}, u32[]{:S(2)}) %collective-permute-start.28) | collective-permute-done | bytes 49184 | tf_op jit(solution)/shard_map/ppermute | solution.py:249
  103.5 9.8 %collective-permute-done.29.b = bf16[64,384]{1,0:T(8,128)(2,1)S(1)} collective-permute-done((bf16[64,384]{1,0:T(8,128)(2,1)S(1)}, bf16[64,384]{1,0:T(8,128)(2,1)S(1)}, u32[]{:S(2)}, u32[]{:S(2)}) %collective-permute-start.29) | collective-permute-done | bytes 49184 | tf_op jit(solution)/shard_map/ppermute | solution.py:249
  113.2 0.7 out.1
  (47 shorter events, 3.2 us)
Async XLA Ops:
  0.0 1.1 copy-start
  0.0 6.5 %copy-start.6 = (bf16[72,2688]{1,0:T(8,128)(2,1)S(1)}, bf16[72,2688]{1,0:T(8,128)(2,1)}, u32[]{:S(2)}) copy-start(bf16[72,2688]{1,0:T(8,128)(2,1)} %param.6) | copy-start | bytes 1161220
  1.1 18.4 %copy-start.1 = (bf16[64,2688]{1,0:T(8,128)(2,1)}, bf16[64,2688]{1,0:T(8,128)(2,1)S(1)}, u32[]{:S(2)}) copy-start(bf16[64,2688]{1,0:T(8,128)(2,1)S(1)} %constant_dynamic-slice_fusion.2.refs_0_) | copy-start | bytes 1032196
  1.1 10.0 %collective-permute-start = (bf16[64,2688]{1,0:T(8,128)(2,1)S(1)}, bf16[64,2688]{1,0:T(8,128)(2,1)}, u32[]{:S(2)}, u32[]{:S(2)}) collective-permute-start(bf16[64,2688]{1,0:T(8,128)(2,1)S(1)} %constant_dynamic-slice_fusion.2.refs_0_), channel_id=1, source_target_pairs={{0,32},{32,64},{64,96},{96,128},{128,160},{160,192},{192,224},{224... | collective-permute-start | bytes 1032200 | tf_op jit(solution)/shard_map/ppermute | solution.py:32
  3.1 9.8 %collective-permute-start.4 = (bf16[64,2688]{1,0:T(8,128)(2,1)S(1)}, bf16[64,2688]{1,0:T(8,128)(2,1)}, u32[]{:S(2)}, u32[]{:S(2)}) collective-permute-start(bf16[64,2688]{1,0:T(8,128)(2,1)S(1)} %constant_dynamic-slice_fusion.2.refs_0_), channel_id=1, source_target_pairs={{0,224},{32,0},{64,32},{96,64},{128,96},{160,128},{192,160},{224,1... | collective-permute-start | bytes 1032200 | tf_op jit(solution)/shard_map/ppermute | solution.py:32
  3.2 1.0 copy-start.3
  4.4 13.1 %collective-permute-start.21 = (bf16[576,384]{1,0:T(8,128)(2,1)S(1)}, bf16[576,384]{1,0:T(8,128)(2,1)S(1)}, u32[]{:S(2)}, u32[]{:S(2)}) collective-permute-start(bf16[576,384]{1,0:T(8,128)(2,1)S(1)} %down.1), channel_id=1, source_target_pairs={{0,18},{16,0},{2,16},{18,2},{1,19},{17,1},{3,17},{19,3},{4,22},{20... | collective-permute-start | bytes 1327112 | tf_op jit(solution)/shard_map/ppermute | solution.py:24
  5.0 14.4 %collective-permute-start.22 = (bf16[576,384]{1,0:T(8,128)(2,1)S(1)}, bf16[576,384]{1,0:T(8,128)(2,1)S(1)}, u32[]{:S(2)}, u32[]{:S(2)}) collective-permute-start(bf16[576,384]{1,0:T(8,128)(2,1)S(1)} %down.1), channel_id=1, source_target_pairs={{0,16},{16,2},{2,18},{18,0},{1,17},{17,3},{3,19},{19,1},{4,20},{20... | collective-permute-start | bytes 1327112 | tf_op jit(solution)/shard_map/ppermute | solution.py:24
  7.6 25.6 %collective-permute-start.10 = (bf16[2,72,2688]{2,1,0:T(8,128)(2,1)S(1)}, bf16[2,72,2688]{2,1,0:T(8,128)(2,1)S(1)}, u32[]{:S(2)}, u32[]{:S(2)}) collective-permute-start(bf16[2,72,2688]{2,1,0:T(8,128)(2,1)S(1)} %pad_maximum_fusion.refs_7_), channel_id=1, source_target_pairs={{0,18},{16,0},{2,16},{18,2},{1,19},{17,1},{3,17},{19,3},{4,22},{20... | collective-permute-start | bytes 2322440 | tf_op jit(solution)/shard_map/ppermute | solution.py:24
  11.1 33.0 %collective-permute-start.8 = (bf16[2,72,2688]{2,1,0:T(8,128)(2,1)S(1)}, bf16[2,72,2688]{2,1,0:T(8,128)(2,1)S(1)}, u32[]{:S(2)}, u32[]{:S(2)}) collective-permute-start(bf16[2,72,2688]{2,1,0:T(8,128)(2,1)S(1)} %pad_maximum_fusion.refs_7_), channel_id=1, source_target_pairs={{0,16},{16,2},{2,18},{18,0},{1,17},{17,3},{3,19},{19,1},{4,20},{20... | collective-permute-start | bytes 2322440 | tf_op jit(solution)/shard_map/ppermute | solution.py:24
  12.9 31.8 %collective-permute-start.23 = (bf16[576,384]{1,0:T(8,128)(2,1)S(1)}, bf16[576,384]{1,0:T(8,128)(2,1)}, u32[]{:S(2)}, u32[]{:S(2)}) collective-permute-start(bf16[576,384]{1,0:T(8,128)(2,1)S(1)} %down.1), channel_id=1, source_target_pairs={{0,2},{16,18},{2,0},{18,16},{1,3},{17,19},{3,1},{19,17},{4,6},{20,... | collective-permute-start | bytes 1327112 | tf_op jit(solution)/shard_map/ppermute | solution.py:24
  17.6 1.9 %copy-start.4 = (bf16[576,384]{1,0:T(8,128)(2,1)}, bf16[576,384]{1,0:T(8,128)(2,1)S(1)}, u32[]{:S(2)}) copy-start(bf16[576,384]{1,0:T(8,128)(2,1)S(1)} %collective-permute-done.21) | copy-start | bytes 1327108
  17.6 9.9 %collective-permute-start.1 = (bf16[64,2688]{1,0:T(8,128)(2,1)}, bf16[64,2688]{1,0:T(8,128)(2,1)}, u32[]{:S(2)}, u32[]{:S(2)}) collective-permute-start(bf16[64,2688]{1,0:T(8,128)(2,1)} %collective-permute-done.refs_1_), channel_id=1, source_target_pairs={{0,32},{32,64},{64,96},{96,128},{128,160},{160,192},{192,224},{224... | collective-permute-start | bytes 1032200 | tf_op jit(solution)/shard_map/ppermute | solution.py:32
  19.5 0.8 copy-start.5
  20.3 9.1 %collective-permute-start.5 = (bf16[64,2688]{1,0:T(8,128)(2,1)}, bf16[64,2688]{1,0:T(8,128)(2,1)}, u32[]{:S(2)}, u32[]{:S(2)}) collective-permute-start(bf16[64,2688]{1,0:T(8,128)(2,1)} %collective-permute-done.4.refs_4_), channel_id=1, source_target_pairs={{0,224},{32,0},{64,32},{96,64},{128,96},{160,128},{192,160},{224,1... | collective-permute-start | bytes 1032200 | tf_op jit(solution)/shard_map/ppermute | solution.py:32
  27.4 18.6 %collective-permute-start.2 = (bf16[64,2688]{1,0:T(8,128)(2,1)}, bf16[64,2688]{1,0:T(8,128)(2,1)S(1)}, u32[]{:S(2)}, u32[]{:S(2)}) collective-permute-start(bf16[64,2688]{1,0:T(8,128)(2,1)} %collective-permute-done.1.refs_2_), channel_id=1, source_target_pairs={{0,32},{32,64},{64,96},{96,128},{128,160},{160,192},{192,224},{224... | collective-permute-start | bytes 1032200 | tf_op jit(solution)/shard_map/ppermute | solution.py:32
  29.4 18.7 %collective-permute-start.6 = (bf16[64,2688]{1,0:T(8,128)(2,1)}, bf16[64,2688]{1,0:T(8,128)(2,1)S(1)}, u32[]{:S(2)}, u32[]{:S(2)}) collective-permute-start(bf16[64,2688]{1,0:T(8,128)(2,1)} %collective-permute-done.5.refs_5_), channel_id=1, source_target_pairs={{0,224},{32,0},{64,32},{96,64},{128,96},{160,128},{192,160},{224,1... | collective-permute-start | bytes 1032200 | tf_op jit(solution)/shard_map/ppermute | solution.py:32
  33.2 19.0 %collective-permute-start.11 = (bf16[1,72,2688]{2,1,0:T(8,128)(2,1)S(1)}, bf16[1,72,2688]{2,1,0:T(8,128)(2,1)S(1)}, u32[]{:S(2)}, u32[]{:S(2)}) collective-permute-start(bf16[1,72,2688]{2,1,0:T(8,128)(2,1)S(1)} %slice.35), channel_id=1, source_target_pairs={{0,18},{16,0},{2,16},{18,2},{1,19},{17,1},{3,17},{19,3},{4,22},{20... | collective-permute-start | bytes 1161224 | tf_op jit(solution)/shard_map/ppermute | solution.py:24
  44.1 9.6 %collective-permute-start.9 = (bf16[1,72,2688]{2,1,0:T(8,128)(2,1)S(1)}, bf16[1,72,2688]{2,1,0:T(8,128)(2,1)S(1)}, u32[]{:S(2)}, u32[]{:S(2)}) collective-permute-start(bf16[1,72,2688]{2,1,0:T(8,128)(2,1)S(1)} %slice.34), channel_id=1, source_target_pairs={{0,16},{16,2},{2,18},{18,0},{1,17},{17,3},{3,19},{19,1},{4,20},{20... | collective-permute-start | bytes 1161224 | tf_op jit(solution)/shard_map/ppermute | solution.py:24
  44.7 5.7 %copy-start.2 = (bf16[64,2688]{1,0:T(8,128)(2,1)S(1)}, bf16[64,2688]{1,0:T(8,128)(2,1)}, u32[]{:S(2)}) copy-start(bf16[64,2688]{1,0:T(8,128)(2,1)} %copy-done.1) | copy-start | bytes 1032196
  45.9 38.0 %collective-permute-start.24 = (bf16[1152,768]{1,0:T(8,128)(2,1)S(1)}, bf16[1152,768]{1,0:T(8,128)(2,1)S(1)}, u32[]{:S(2)}, u32[]{:S(2)}) collective-permute-start(bf16[1152,768]{1,0:T(8,128)(2,1)S(1)} %maximum_maximum_fusion.refs_9_), channel_id=1, source_target_pairs={{0,1},{1,0},{2,3},{3,2},{4,5},{5,4},{6,7},{7,6},{8,9},{9,8},{10,11... | collective-permute-start | bytes 5308424 | tf_op jit(solution)/shard_map/ppermute | solution.py:36
  46.0 9.1 %collective-permute-start.3 = (bf16[32,2688]{1,0:T(8,128)(2,1)S(1)}, bf16[32,2688]{1,0:T(8,128)(2,1)S(1)}, u32[]{:S(2)}, u32[]{:S(2)}) collective-permute-start(bf16[32,2688]{1,0:T(8,128)(2,1)S(1)} %slice.32), channel_id=1, source_target_pairs={{0,32},{32,64},{64,96},{96,128},{128,160},{160,192},{192,224},{224... | collective-permute-start | bytes 516104 | tf_op jit(solution)/shard_map/ppermute | solution.py:32
  48.1 8.0 %collective-permute-start.7 = (bf16[32,2688]{1,0:T(8,128)(2,1)S(1)}, bf16[32,2688]{1,0:T(8,128)(2,1)S(1)}, u32[]{:S(2)}, u32[]{:S(2)}) collective-permute-start(bf16[32,2688]{1,0:T(8,128)(2,1)S(1)} %slice.33), channel_id=1, source_target_pairs={{0,224},{32,0},{64,32},{96,64},{128,96},{160,128},{192,160},{224,1... | collective-permute-start | bytes 516104 | tf_op jit(solution)/shard_map/ppermute | solution.py:32
  57.2 2.1 %collective-permute-start.12 = (f32[576,256]{1,0:T(8,128)S(1)}, f32[576,256]{1,0:T(8,128)S(1)}, u32[]{:S(2)}, u32[]{:S(2)}) collective-permute-start(f32[576,256]{1,0:T(8,128)S(1)} %get-tuple-element.20), channel_id=1, source_target_pairs={{0,1},{1,0},{2,3},{3,2},{4,5},{5,4},{6,7},{7,6},{8,9},{9,8},{10,11... | collective-permute-start | bytes 1769480 | tf_op jit(solution)/shard_map/ppermute | solution.py:36
  59.5 12.7 %collective-permute-start.14 = (bf16[288,256]{1,0:T(8,128)(2,1)S(1)}, bf16[288,256]{1,0:T(8,128)(2,1)S(1)}, u32[]{:S(2)}, u32[]{:S(2)}) collective-permute-start(bf16[288,256]{1,0:T(8,128)(2,1)S(1)} %fusion.refs_0_), channel_id=1, source_target_pairs={{0,64},{32,96},{64,128},{96,160},{128,192},{160,224},{192,0},{224,... | collective-permute-start | bytes 442376 | tf_op jit(solution)/shard_map/ppermute | solution.py:32
  65.2 9.9 %collective-permute-start.17 = (bf16[288,256]{1,0:T(8,128)(2,1)S(1)}, bf16[288,256]{1,0:T(8,128)(2,1)S(1)}, u32[]{:S(2)}, u32[]{:S(2)}) collective-permute-start(bf16[288,256]{1,0:T(8,128)(2,1)S(1)} %fusion.refs_0_), channel_id=1, source_target_pairs={{0,192},{32,224},{64,0},{96,32},{128,64},{160,96},{192,128},{224,1... | collective-permute-start | bytes 442376 | tf_op jit(solution)/shard_map/ppermute | solution.py:32
  65.2 9.9 %collective-permute-start.13 = (bf16[288,256]{1,0:T(8,128)(2,1)S(1)}, bf16[288,256]{1,0:T(8,128)(2,1)S(1)}, u32[]{:S(2)}, u32[]{:S(2)}) collective-permute-start(bf16[288,256]{1,0:T(8,128)(2,1)S(1)} %fusion.refs_0_), channel_id=1, source_target_pairs={{0,32},{32,64},{64,96},{96,128},{128,160},{160,192},{192,224},{224... | collective-permute-start | bytes 442376 | tf_op jit(solution)/shard_map/ppermute | solution.py:32
  65.7 12.4 %collective-permute-start.16 = (bf16[288,256]{1,0:T(8,128)(2,1)S(1)}, bf16[288,256]{1,0:T(8,128)(2,1)S(1)}, u32[]{:S(2)}, u32[]{:S(2)}) collective-permute-start(bf16[288,256]{1,0:T(8,128)(2,1)S(1)} %fusion.refs_0_), channel_id=1, source_target_pairs={{0,224},{32,0},{64,32},{96,64},{128,96},{160,128},{192,160},{224,1... | collective-permute-start | bytes 442376 | tf_op jit(solution)/shard_map/ppermute | solution.py:32
  72.1 11.8 %collective-permute-start.15 = (bf16[288,256]{1,0:T(8,128)(2,1)S(1)}, bf16[288,256]{1,0:T(8,128)(2,1)S(1)}, u32[]{:S(2)}, u32[]{:S(2)}) collective-permute-start(bf16[288,256]{1,0:T(8,128)(2,1)S(1)} %collective-permute-done.14.refs_2_), channel_id=1, source_target_pairs={{0,32},{32,64},{64,96},{96,128},{128,160},{160,192},{192,224},{224... | collective-permute-start | bytes 442376 | tf_op jit(solution)/shard_map/ppermute | solution.py:32
  75.1 8.8 %collective-permute-start.18 = (bf16[288,256]{1,0:T(8,128)(2,1)S(1)}, bf16[288,256]{1,0:T(8,128)(2,1)S(1)}, u32[]{:S(2)}, u32[]{:S(2)}) collective-permute-start(bf16[288,256]{1,0:T(8,128)(2,1)S(1)} %collective-permute-done.17.refs_5_), channel_id=1, source_target_pairs={{0,224},{32,0},{64,32},{96,64},{128,96},{160,128},{192,160},{224,1... | collective-permute-start | bytes 442376 | tf_op jit(solution)/shard_map/ppermute | solution.py:32
  75.1 6.9 %collective-permute-start.19 = (bf16[144,256]{1,0:T(8,128)(2,1)S(1)}, bf16[144,256]{1,0:T(8,128)(2,1)S(1)}, u32[]{:S(2)}, u32[]{:S(2)}) collective-permute-start(bf16[144,256]{1,0:T(8,128)(2,1)S(1)} %slice.38), channel_id=1, source_target_pairs={{0,64},{32,96},{64,128},{96,160},{128,192},{160,224},{192,0},{224,... | collective-permute-start | bytes 221192 | tf_op jit(solution)/shard_map/ppermute | solution.py:32
  78.1 5.8 %collective-permute-start.20 = (bf16[144,256]{1,0:T(8,128)(2,1)S(1)}, bf16[144,256]{1,0:T(8,128)(2,1)S(1)}, u32[]{:S(2)}, u32[]{:S(2)}) collective-permute-start(bf16[144,256]{1,0:T(8,128)(2,1)S(1)} %slice.39), channel_id=1, source_target_pairs={{0,192},{32,224},{64,0},{96,32},{128,64},{160,96},{192,128},{224,1... | collective-permute-start | bytes 221192 | tf_op jit(solution)/shard_map/ppermute | solution.py:32
  85.3 4.7 %collective-permute-start.25 = (bf16[64,768]{1,0:T(8,128)(2,1)S(1)}, bf16[64,768]{1,0:T(8,128)(2,1)S(1)}, u32[]{:S(2)}, u32[]{:S(2)}) collective-permute-start(bf16[64,768]{1,0:T(8,128)(2,1)S(1)} %get-tuple-element.22), channel_id=1, source_target_pairs={{0,4},{4,8},{8,12},{12,0},{1,5},{5,9},{9,13},{13,1},{2,6},{6,10},{... | collective-permute-start | bytes 294920 | tf_op jit(solution)/shard_map/ppermute | solution.py:28
  85.6 6.1 %collective-permute-start.26 = (bf16[64,768]{1,0:T(8,128)(2,1)S(1)}, bf16[64,768]{1,0:T(8,128)(2,1)S(1)}, u32[]{:S(2)}, u32[]{:S(2)}) collective-permute-start(bf16[64,768]{1,0:T(8,128)(2,1)S(1)} %get-tuple-element.23), channel_id=1, source_target_pairs={{0,8},{4,12},{8,0},{12,4},{1,9},{5,13},{9,1},{13,5},{2,10},{6,14},... | collective-permute-start | bytes 294920 | tf_op jit(solution)/shard_map/ppermute | solution.py:28
  88.2 5.8 %collective-permute-start.27 = (bf16[64,768]{1,0:T(8,128)(2,1)S(1)}, bf16[64,768]{1,0:T(8,128)(2,1)S(1)}, u32[]{:S(2)}, u32[]{:S(2)}) collective-permute-start(bf16[64,768]{1,0:T(8,128)(2,1)S(1)} %get-tuple-element.24), channel_id=1, source_target_pairs={{0,12},{4,0},{8,4},{12,8},{1,13},{5,1},{9,5},{13,9},{2,14},{6,2},{... | collective-permute-start | bytes 294920 | tf_op jit(solution)/shard_map/ppermute | solution.py:28
  94.1 9.3 %collective-permute-start.28 = (bf16[64,384]{1,0:T(8,128)(2,1)S(1)}, bf16[64,384]{1,0:T(8,128)(2,1)S(1)}, u32[]{:S(2)}, u32[]{:S(2)}) collective-permute-start(bf16[64,384]{1,0:T(8,128)(2,1)S(1)} %get-tuple-element.30), channel_id=1, source_target_pairs={{0,96},{1,128},{2,97},{3,129},{4,64},{5,160},{6,65},{7,161},{8,0},... | collective-permute-start | bytes 147464 | tf_op jit(solution)/shard_map/ppermute | solution.py:249
  101.6 11.6 %collective-permute-start.29 = (bf16[64,384]{1,0:T(8,128)(2,1)S(1)}, bf16[64,384]{1,0:T(8,128)(2,1)S(1)}, u32[]{:S(2)}, u32[]{:S(2)}) collective-permute-start(bf16[64,384]{1,0:T(8,128)(2,1)S(1)} %get-tuple-element.29), channel_id=1, source_target_pairs={{0,97},{1,129},{2,96},{3,128},{4,65},{5,161},{6,64},{7,160},{8,1},... | collective-permute-start | bytes 147464 | tf_op jit(solution)/shard_map/ppermute | solution.py:249
